TPU v7x, 32 devices: a whole 2x2x4 slice. The times are simulated.
32 devices in a mesh: shard: 4 (over y, core), ctx: 2 (over x), tp: 4 (over z).
Axes of the slice: x: 2, y: 2, z: 4, core: 2. Of those that a mesh axis runs over, the one named last changes fastest.
Arguments:
- block_input: bfloat16 [1024, 2048], P(('shard', 'ctx')), may hold values from -6 to 6
- norm1_gain: bfloat16 [2048], P('shard'), may hold values from 0.5 to 1.5
- q_weight: bfloat16 [2048, 3072], P('shard', 'tp'), may hold values from -0.15467961 to 0.15467961
- kva_weight: bfloat16 [2048, 576], P('shard'), may hold values from -0.15467961 to 0.15467961
- kv_norm_gain: bfloat16 [512], P('shard'), may hold values from 0.5 to 1.5
- kvb_weight: bfloat16 [512, 4096], P('shard', 'tp'), may hold values from -0.30935922 to 0.30935922
- out_weight: bfloat16 [2048, 2048], P('tp', 'shard'), may hold values from -0.75 to 0.75
- norm2_gain: bfloat16 [2048], P('shard'), may hold values from 0.5 to 1.5
- router_weight: bfloat16 [2048, 16], P('shard'), may hold values from -0.92807765 to 0.92807765
- shared_gate: bfloat16 [2048, 2816], P('shard', 'tp'), may hold values from -0.125 to 0.125
- shared_up: bfloat16 [2048, 2816], P('shard', 'tp'), may hold values from -0.125 to 0.125
- shared_down: bfloat16 [2816, 2048], P('tp', 'shard'), may hold values from -0.109375 to 0.109375
- expert_gate: bfloat16 [16, 2048, 1408], P(('shard', 'ctx'), None, 'tp'), may hold values from -0.125 to 0.125
- expert_up: bfloat16 [16, 2048, 1408], P(('shard', 'ctx'), None, 'tp'), may hold values from -0.125 to 0.125
- expert_down: bfloat16 [16, 1408, 2048], P(('shard', 'ctx'), 'tp'), may hold values from -0.15625 to 0.15625
- routes: int32 [1024, 6], P(('shard', 'ctx')), may hold values from 0 to 15, all different within a row; in each aligned block of 128 rows (0 to 127, 128 to 255, ...) at most 96 rows name the same one
- cotangent: float32 [1024, 2048], P(('shard', 'ctx')), may hold values from -6 to 6
Outputs:
- block_output: float32 [1024, 2048], P(('shard', 'ctx'))
- input_grad: float32 [1024, 2048], P(('shard', 'ctx'))
- grad_norm1: float32 [2048], P('shard')
- grad_query_w: float32 [2048, 3072], P('shard', 'tp')
- grad_latent_w: float32 [2048, 576], P('shard')
- grad_kv_norm: float32 [512], P('shard')
- grad_expand_w: float32 [512, 4096], P('shard', 'tp')
- grad_out_w: float32 [2048, 2048], P('tp', 'shard')
- grad_norm2: float32 [2048], P('shard')
- grad_router: float32 [2048, 16], P('shard')
- grad_shared_gate: float32 [2048, 2816], P('shard', 'tp')
- grad_shared_up: float32 [2048, 2816], P('shard', 'tp')
- grad_shared_down: float32 [2816, 2048], P('tp', 'shard')
- grad_expert_gate: float32 [16, 2048, 1408], P(('shard', 'ctx'), None, 'tp')
- grad_expert_up: float32 [16, 2048, 1408], P(('shard', 'ctx'), None, 'tp')
- grad_expert_down: float32 [16, 1408, 2048], P(('shard', 'ctx'), 'tp')
Inputs may be any that keep to these rules, and one draw needn't show every extreme that they name: `routes`: in the rows of one device (aligned blocks of 128 rows) each row names 6 different experts, and no expert is named by more than 96 rows of a block; some expert is named by exactly 96 rows.
All inputs are finite; a program needn't handle non-finite values.
Results may differ from a plain program's by a relative error of at most 0.04.
Values may be sent and summed in bfloat16 or wider, within the bound.
A program may use at most 256 MiB of HBM per device.

v0:
```python
import jax
import jax.numpy as jnp
from jax import lax
from jax.sharding import PartitionSpec as P

DN = 128
DR = 64
DV = 128
KVR = 512


EPS = 1e-06
NEG = -1e30


def norm_rows(value, gain):
    factor = lax.rsqrt(jnp.mean(value * value, axis=-1, keepdims=True) + EPS)
    return value * factor * gain.astype(jnp.float32)


def rope_tables(count, offset):
    half_size = DR // 2
    position = jnp.arange(count, dtype=jnp.float32) + offset
    freqs = 10000.0 ** (-(jnp.arange(half_size, dtype=jnp.float32) * 2.0 / DR))
    angle = position[:, None] * freqs[None, :]
    return (jnp.cos(angle), jnp.sin(angle))


def rotate(value, cosine, sine_table):
    half_size = DR // 2
    first = value[..., :half_size]
    second = value[..., half_size:]
    return jnp.concatenate(
        [first * cosine - second * sine_table, first * sine_table + second * cosine], axis=-1
    )


def rotate_back(grad, cosine, sine_table):
    half_size = DR // 2
    first = grad[..., :half_size]
    second = grad[..., half_size:]
    return jnp.concatenate(
        [first * cosine + second * sine_table, second * cosine - first * sine_table], axis=-1
    )


def silu_slope(value):
    sigmoid = jax.nn.sigmoid(value)
    return sigmoid * (1.0 + value * (1.0 - sigmoid))


def mdot(left, right):
    return jnp.dot(left, right, preferred_element_type=jnp.float32)


def send_rows(buffer):
    return lax.all_to_all(buffer, ("shard", "ctx"), split_axis=0, concat_axis=0, tiled=True)


def return_rows(partial_value, slots):
    back_rows = lax.all_to_all(
        partial_value, ("shard", "ctx"), split_axis=0, concat_axis=0, tiled=True
    )
    flat_back = back_rows.reshape(-1, back_rows.shape[-1])
    return flat_back[slots]


def per_device(
    block_input,
    norm1_gain,
    q_weight,
    kva_weight,
    kv_norm_gain,
    kvb_weight,
    out_weight,
    norm2_gain,
    router_weight,
    shared_gate,
    shared_up,
    shared_down,
    expert_gate,
    expert_up,
    expert_down,
    routes,
    cotangent,
):
    tok_rows = block_input.shape[0]
    head_count = q_weight.shape[1] // (DN + DR)
    score_scale = (DN + DR) ** (-0.5)
    (
        gain_one,
        w_query,
        w_latent,
        gain_kv,
        w_expand,
        w_output,
        gain_two,
        w_router,
        w_sgate,
        w_sup,
        w_sdown,
    ) = (
        lax.all_gather(norm1_gain, "shard", axis=0, tiled=True),
        lax.all_gather(q_weight, "shard", axis=0, tiled=True),
        lax.all_gather(kva_weight, "shard", axis=0, tiled=True),
        lax.all_gather(kv_norm_gain, "shard", axis=0, tiled=True),
        lax.all_gather(kvb_weight, "shard", axis=0, tiled=True),
        lax.all_gather(out_weight, "shard", axis=1, tiled=True),
        lax.all_gather(norm2_gain, "shard", axis=0, tiled=True),
        lax.all_gather(router_weight, "shard", axis=0, tiled=True),
        lax.all_gather(shared_gate, "shard", axis=0, tiled=True),
        lax.all_gather(shared_up, "shard", axis=0, tiled=True),
        lax.all_gather(shared_down, "shard", axis=1, tiled=True),
    )
    block_index = lax.axis_index("ctx")
    cosine, sine_table = rope_tables(tok_rows, (block_index * tok_rows).astype(jnp.float32))
    x_float = block_input.astype(jnp.float32)
    normed_one = norm_rows(x_float, gain_one).astype(jnp.bfloat16)
    query = mdot(normed_one, w_query).reshape(tok_rows, head_count, DN + DR)
    query_rot = rotate(query[..., DN:], cosine[:, None, :], sine_table[:, None, :])
    query = jnp.concatenate([query[..., :DN], query_rot], axis=-1).astype(jnp.bfloat16)
    query_nope = query[..., :DN]
    query_rope = query[..., DN:]
    latent = mdot(normed_one, w_latent)
    compressed = latent[:, :KVR]
    latent_n = norm_rows(compressed, gain_kv).astype(jnp.bfloat16)
    rope_key = rotate(latent[:, KVR:], cosine, sine_table).astype(jnp.bfloat16)
    first_piece = mdot(latent_n, w_expand).astype(jnp.bfloat16)
    gathered, rope_all = (
        lax.all_gather(first_piece, "ctx", axis=0, tiled=True),
        lax.all_gather(rope_key, "ctx", axis=0, tiled=True),
    )
    query_pos = block_index * tok_rows + jnp.arange(tok_rows, dtype=jnp.int32)

    def scores_at(block_id):
        blk_start = block_id * tok_rows
        kv_block = lax.dynamic_slice_in_dim(gathered, blk_start, tok_rows, 0).reshape(
            tok_rows, head_count, DN + DV
        )
        rope_block = lax.dynamic_slice_in_dim(rope_all, blk_start, tok_rows, 0)
        score = jnp.einsum(
            "qhd,khd->hqk", query_nope, kv_block[..., :DN], preferred_element_type=jnp.float32
        )
        score = score + jnp.einsum(
            "qhd,kd->hqk", query_rope, rope_block, preferred_element_type=jnp.float32
        )
        score = score * score_scale
        key_pos = blk_start + jnp.arange(tok_rows, dtype=jnp.int32)
        score = jnp.where(key_pos[None, None, :] <= query_pos[None, :, None], score, NEG)
        return (score, kv_block, rope_block)

    def forward_block(block_id, carry):
        run_max, run_sum, weighted = carry
        score, kv_block, rope_block = scores_at(block_id)
        new_max = jnp.maximum(run_max, jnp.max(score, axis=-1))
        factor = jnp.exp(run_max - new_max)
        expo = jnp.exp(score - new_max[..., None])
        run_sum = factor * run_sum + jnp.sum(expo, axis=-1)
        weighted = factor[..., None] * weighted + jnp.einsum(
            "hqk,khd->hqd",
            expo.astype(jnp.bfloat16),
            kv_block[..., DN:],
            preferred_element_type=jnp.float32,
        )
        return (new_max, run_sum, weighted)

    start_state = (
        jnp.full((head_count, tok_rows), NEG, jnp.float32),
        jnp.zeros((head_count, tok_rows), jnp.float32),
        jnp.zeros((head_count, tok_rows, DV), jnp.float32),
    )
    run_max, run_sum, weighted = lax.fori_loop(0, block_index + 1, forward_block, start_state)
    lse = run_max + jnp.log(run_sum)
    attn_rows = (weighted / run_sum[..., None]).astype(jnp.bfloat16).transpose(1, 0, 2)
    attn_flat = attn_rows.reshape(tok_rows, head_count * DV)
    attn_full = lax.psum(mdot(attn_flat, w_output), "tp")
    mid = x_float + attn_full
    normed_two = norm_rows(mid, gain_two).astype(jnp.bfloat16)
    probs = jax.nn.softmax(mdot(normed_two, w_router), axis=-1)
    experts = probs.shape[1]
    topk = routes.shape[1]
    picks = (routes[:, :, None] == jnp.arange(experts, dtype=jnp.int32)[None, None, :]).astype(
        jnp.float32
    )
    route_w = jnp.sum(picks * probs[:, None, :], axis=-1)
    shared_a = mdot(normed_two, w_sgate)
    shared_b = mdot(normed_two, w_sup)
    shared_h = (jax.nn.silu(shared_a) * shared_b).astype(jnp.bfloat16)
    shared_y = mdot(shared_h, w_sdown)
    capacity = 2 * tok_rows * topk // experts
    owners = lax.axis_size(("shard", "ctx"))
    local_experts = expert_gate.shape[0]
    width = normed_two.shape[1]
    flat_routes = routes.reshape(-1)
    onehot = (flat_routes[:, None] == jnp.arange(experts, dtype=jnp.int32)[None, :]).astype(
        jnp.int32
    )
    rank = jnp.sum((jnp.cumsum(onehot, axis=0) - 1) * onehot, axis=1)
    slots = flat_routes * capacity + rank
    source_row = jnp.arange(tok_rows * topk, dtype=jnp.int32) // topk
    send_buffer = (
        jnp.zeros((experts * capacity, width), jnp.bfloat16).at[slots].set(normed_two[source_row])
    )
    received = send_rows(send_buffer.reshape(owners, local_experts * capacity, width)).reshape(
        owners, local_experts, capacity, width
    )
    gate_act = jnp.einsum(
        "gecd,edf->gecf", received, expert_gate, preferred_element_type=jnp.float32
    )
    up_act = jnp.einsum("gecd,edf->gecf", received, expert_up, preferred_element_type=jnp.float32)
    hidden = (jax.nn.silu(gate_act) * up_act).astype(jnp.bfloat16)
    expert_y = jnp.einsum("gecf,efd->gecd", hidden, expert_down, preferred_element_type=jnp.float32)
    routed_out = return_rows(
        expert_y.reshape(owners, local_experts * capacity, width), slots
    ).reshape(tok_rows, topk, width)
    routed_part = jnp.sum(route_w[:, :, None] * routed_out, axis=1) + shared_y
    weight_part = jnp.sum(routed_out * cotangent[:, None, :], axis=-1)
    moe_out, route_grad = lax.psum((routed_part, weight_part), "tp")
    block_output = mid + moe_out
    cot_b = cotangent.astype(jnp.bfloat16)
    routed_grad = (
        (route_w[:, :, None] * cotangent[:, None, :])
        .astype(jnp.bfloat16)
        .reshape(tok_rows * topk, width)
    )
    grad_buffer = jnp.zeros((experts * capacity, width), jnp.bfloat16).at[slots].set(routed_grad)
    grad_recv = send_rows(grad_buffer.reshape(owners, local_experts * capacity, width)).reshape(
        owners, local_experts, capacity, width
    )
    hidden_grad = jnp.einsum(
        "gecd,efd->gecf", grad_recv, expert_down, preferred_element_type=jnp.float32
    )
    gate_grad = (hidden_grad * up_act * silu_slope(gate_act)).astype(jnp.bfloat16)
    up_grad = (hidden_grad * jax.nn.silu(gate_act)).astype(jnp.bfloat16)
    grad_expert_down = jnp.einsum(
        "gecf,gecd->efd", hidden, grad_recv, preferred_element_type=jnp.float32
    )
    grad_expert_gate = jnp.einsum(
        "gecd,gecf->edf", received, gate_grad, preferred_element_type=jnp.float32
    )
    grad_expert_up = jnp.einsum(
        "gecd,gecf->edf", received, up_grad, preferred_element_type=jnp.float32
    )
    row_grad = jnp.einsum(
        "gecf,edf->gecd", gate_grad, expert_gate, preferred_element_type=jnp.float32
    )
    row_grad = row_grad + jnp.einsum(
        "gecf,edf->gecd", up_grad, expert_up, preferred_element_type=jnp.float32
    )
    routed_back = return_rows(
        row_grad.reshape(owners, local_experts * capacity, width), slots
    ).reshape(tok_rows, topk, width)
    shared_grad = jnp.einsum("td,fd->tf", cot_b, w_sdown, preferred_element_type=jnp.float32)
    sgate_grad = (shared_grad * shared_b * silu_slope(shared_a)).astype(jnp.bfloat16)
    sup_grad = (shared_grad * jax.nn.silu(shared_a)).astype(jnp.bfloat16)
    grad_sdown = jnp.einsum("tf,td->fd", shared_h, cot_b, preferred_element_type=jnp.float32)
    grad_sgate = jnp.einsum("td,tf->df", normed_two, sgate_grad, preferred_element_type=jnp.float32)
    grad_sup = jnp.einsum("td,tf->df", normed_two, sup_grad, preferred_element_type=jnp.float32)
    two_part = jnp.sum(routed_back, axis=1)
    two_part = two_part + jnp.einsum(
        "tf,df->td", sgate_grad, w_sgate, preferred_element_type=jnp.float32
    )
    two_part = two_part + jnp.einsum(
        "tf,df->td", sup_grad, w_sup, preferred_element_type=jnp.float32
    )
    two_grad = lax.psum(two_part, "tp")
    prob_grad = jnp.sum(picks * route_grad[:, :, None], axis=1)
    logit_grad = (probs * (prob_grad - jnp.sum(probs * prob_grad, axis=-1, keepdims=True))).astype(
        jnp.bfloat16
    )
    grad_router = jnp.einsum(
        "td,te->de", normed_two, logit_grad, preferred_element_type=jnp.float32
    )
    two_grad = two_grad + jnp.einsum(
        "te,de->td", logit_grad, w_router, preferred_element_type=jnp.float32
    )
    _, norm_two_back = jax.vjp(norm_rows, mid, gain_two.astype(jnp.float32))
    mid_norm_grad, grad_gain_two = norm_two_back(two_grad)
    mid_grad = cotangent + mid_norm_grad
    mid_b = mid_grad.astype(jnp.bfloat16)
    grad_out_w = jnp.einsum("tj,td->jd", attn_flat, mid_b, preferred_element_type=jnp.float32)
    out_grad = jnp.einsum("td,jd->tj", mid_b, w_output, preferred_element_type=jnp.float32).reshape(
        tok_rows, head_count, DV
    )
    out_grad_b = out_grad.astype(jnp.bfloat16)
    delta = jnp.sum(out_grad * attn_rows.astype(jnp.float32), axis=-1).T
    key_count = gathered.shape[0]
    term_width = head_count * (DN + DV + DR)

    def back_block(block_id, carry):
        nope_grad, rope_qgrad, terms = carry
        score, kv_block, rope_block = scores_at(block_id)
        probs_blk = jnp.exp(score - lse[..., None])
        prob_b = probs_blk.astype(jnp.bfloat16)
        dprob = jnp.einsum(
            "qhd,khd->hqk", out_grad_b, kv_block[..., DN:], preferred_element_type=jnp.float32
        )
        dscore = (probs_blk * (dprob - delta[..., None])).astype(jnp.bfloat16)
        nope_grad = (
            nope_grad
            + jnp.einsum(
                "hqk,khd->qhd", dscore, kv_block[..., :DN], preferred_element_type=jnp.float32
            )
            * score_scale
        )
        rope_qgrad = (
            rope_qgrad
            + jnp.einsum("hqk,kd->qhd", dscore, rope_block, preferred_element_type=jnp.float32)
            * score_scale
        )
        key_nope_grad = (
            jnp.einsum("hqk,qhd->khd", dscore, query_nope, preferred_element_type=jnp.float32)
            * score_scale
        )
        key_rope_grad = (
            jnp.einsum("hqk,qhd->khd", dscore, query_rope, preferred_element_type=jnp.float32)
            * score_scale
        )
        value_grad = jnp.einsum(
            "hqk,qhd->khd", prob_b, out_grad_b, preferred_element_type=jnp.float32
        )
        block_terms = jnp.concatenate([key_nope_grad, value_grad, key_rope_grad], axis=-1).reshape(
            tok_rows, term_width
        )
        terms = lax.dynamic_update_slice_in_dim(terms, block_terms, block_id * tok_rows, 0)
        return (nope_grad, rope_qgrad, terms)

    back_init = (
        jnp.zeros((tok_rows, head_count, DN), jnp.float32),
        jnp.zeros((tok_rows, head_count, DR), jnp.float32),
        jnp.zeros((key_count, term_width), jnp.float32),
    )
    nope_grad, rope_qgrad, terms = lax.fori_loop(0, block_index + 1, back_block, back_init)
    key_terms = lax.psum_scatter(terms, "ctx", scatter_dimension=0, tiled=True).reshape(
        tok_rows, head_count, DN + DV + DR
    )
    kv_grad = (
        key_terms[..., : DN + DV].reshape(tok_rows, head_count * (DN + DV)).astype(jnp.bfloat16)
    )
    rope_grad = rotate_back(jnp.sum(key_terms[..., DN + DV :], axis=1), cosine, sine_table)
    grad_expand = jnp.einsum("ti,tj->ij", latent_n, kv_grad, preferred_element_type=jnp.float32)
    latent_part = jnp.einsum("tj,ij->ti", kv_grad, w_expand, preferred_element_type=jnp.float32)
    rope_qback = rotate_back(rope_qgrad, cosine[:, None, :], sine_table[:, None, :])
    query_grad = (
        jnp.concatenate([nope_grad, rope_qback], axis=-1)
        .astype(jnp.bfloat16)
        .reshape(tok_rows, head_count * (DN + DR))
    )
    grad_query = jnp.einsum("td,tj->dj", normed_one, query_grad, preferred_element_type=jnp.float32)
    normed_part = jnp.einsum("tj,dj->td", query_grad, w_query, preferred_element_type=jnp.float32)
    latent_sum, normed_sum = lax.psum(
        (jnp.concatenate([latent_part, rope_grad], axis=-1), normed_part), "tp"
    )
    _, kv_back = jax.vjp(norm_rows, compressed, gain_kv.astype(jnp.float32))
    compressed_grad, grad_gain_kv = kv_back(latent_sum[:, :KVR])
    latent_grad = jnp.concatenate([compressed_grad, latent_sum[:, KVR:]], axis=-1).astype(
        jnp.bfloat16
    )
    grad_latent = jnp.einsum(
        "td,tl->dl", normed_one, latent_grad, preferred_element_type=jnp.float32
    )
    one_grad = normed_sum + jnp.einsum(
        "tl,dl->td", latent_grad, w_latent, preferred_element_type=jnp.float32
    )
    _, one_back = jax.vjp(norm_rows, x_float, gain_one.astype(jnp.float32))
    input_norm_grad, grad_gain_one = one_back(one_grad)
    input_grad = mid_grad + input_norm_grad
    (
        red_one,
        red_query,
        red_latent,
        red_kv,
        red_expand,
        red_output,
        red_two,
        red_router,
        red_sgate,
        red_sup,
        red_sdown,
    ) = (
        lax.psum_scatter(grad_gain_one, "shard", scatter_dimension=0, tiled=True),
        lax.psum_scatter(grad_query, "shard", scatter_dimension=0, tiled=True),
        lax.psum_scatter(grad_latent, "shard", scatter_dimension=0, tiled=True),
        lax.psum_scatter(grad_gain_kv, "shard", scatter_dimension=0, tiled=True),
        lax.psum_scatter(grad_expand, "shard", scatter_dimension=0, tiled=True),
        lax.psum_scatter(grad_out_w, "shard", scatter_dimension=1, tiled=True),
        lax.psum_scatter(grad_gain_two, "shard", scatter_dimension=0, tiled=True),
        lax.psum_scatter(grad_router, "shard", scatter_dimension=0, tiled=True),
        lax.psum_scatter(grad_sgate, "shard", scatter_dimension=0, tiled=True),
        lax.psum_scatter(grad_sup, "shard", scatter_dimension=0, tiled=True),
        lax.psum_scatter(grad_sdown, "shard", scatter_dimension=1, tiled=True),
    )
    (
        sum_one,
        sum_query,
        sum_latent,
        sum_kv,
        sum_expand,
        sum_output,
        sum_two,
        sum_router,
        sum_sgate,
        sum_sup,
        sum_sdown,
    ) = lax.psum(
        (
            red_one,
            red_query,
            red_latent,
            red_kv,
            red_expand,
            red_output,
            red_two,
            red_router,
            red_sgate,
            red_sup,
            red_sdown,
        ),
        "ctx",
    )
    return (
        block_output,
        input_grad,
        sum_one,
        sum_query,
        sum_latent,
        sum_kv,
        sum_expand,
        sum_output,
        sum_two,
        sum_router,
        sum_sgate,
        sum_sup,
        sum_sdown,
        grad_expert_gate,
        grad_expert_up,
        grad_expert_down,
    )


def solution(mesh):
    in_specs = (
        P(("shard", "ctx"), None),
        P("shard"),
        P("shard", "tp"),
        P("shard", None),
        P("shard"),
        P("shard", "tp"),
        P("tp", "shard"),
        P("shard"),
        P("shard", None),
        P("shard", "tp"),
        P("shard", "tp"),
        P("tp", "shard"),
        P(("shard", "ctx"), None, "tp"),
        P(("shard", "ctx"), None, "tp"),
        P(("shard", "ctx"), "tp", None),
        P(("shard", "ctx"), None),
        P(("shard", "ctx"), None),
    )
    out_specs = (
        P(("shard", "ctx"), None),
        P(("shard", "ctx"), None),
        P("shard"),
        P("shard", "tp"),
        P("shard", None),
        P("shard"),
        P("shard", "tp"),
        P("tp", "shard"),
        P("shard"),
        P("shard", None),
        P("shard", "tp"),
        P("shard", "tp"),
        P("tp", "shard"),
        P(("shard", "ctx"), None, "tp"),
        P(("shard", "ctx"), None, "tp"),
        P(("shard", "ctx"), "tp", None),
    )
    return jax.shard_map(
        per_device, mesh=mesh, in_specs=in_specs, out_specs=out_specs, check_vma=False
    )
```

profile of v0, /device:TPU:0, one launch (start us, length us, event | category | flops | bytes accessed | tf_op | source)
XLA Modules:
  0.0 1551.4 jit_solution(7781636419899242746)
XLA Ops:
  12.5 6.2 all-gather
  18.7 5.5 all-gather.1
  24.2 12.2 all-gather.11.cloned.1.call-done
  45.0 9.7 all-gather.13.cloned.1.call-done
  56.5 9.2 all_gather.43
  67.7 17.1 %all-gather.15.cloned.1.call-done = bf16[2048,768]{1,0:T(8,128)(2,1)} async-done(((bf16[512,768]{1,0:T(8,128)(2,1)}), bf16[2048,768]{1,0:T(8,128)(2,1)}) %all-gather.15.cloned.1.call-update) | async-done | bytes 3145744 | tf_op jit(solution)/shard_map/all_gather | solution.py:104
  100.1 8.8 all-gather.17.cloned.1.call-done
  136.9 27.1 %all-reduce.12.cloned.1.call-done = f32[128,2048]{1,0:T(8,128)} async-done(((f32[128,2048]{1,0:T(8,128)}), f32[128,2048]{1,0:T(8,128)}) %all-reduce.12.cloned.1.call-update) | async-done | bytes 1048592 | tf_op jit(solution)/shard_map/psum | solution.py:176
  166.5 24.3 %scatter_custom_fusion = bf16[1536,2048]{1,0:T(8,128)(2,1)} fusion(s32[768]{0:T(1024)} %fusion.113, bf16[128,2048]{1,0:T(8,128)(2,1)S(1)} %multiply_convert_fusion.2, s32[1024]{0:T(1024)} %pad_clamp_fusion.1, bf16[]{:T(256)} %constant.102.clone.1), kind=kCustom, calls=%fused_computation.83 | custom fusion | bytes 6291968 | tf_op jit(solution)/shard_map/scatter | solution.py:202
  195.6 5.7 mul.497
  201.3 8.3 mul.498
  209.6 57.7 %all_gather.48 = bf16[2048,16]{0,1:T(8,128)(2,1)S(1)} all-gather(bf16[512,16]{0,1:T(8,128)(2,1)S(1)} %copy-done.64), channel_id=1, replica_groups=mesh['shard'=4,'ctx'=2,'tp'=4] {'shard'}, dimensions={0}, use_global_device_ids=true | all-gather | bytes 81920 | tf_op jit(solution)/shard_map/all_gather | solution.py:110
  270.2 12.4 scatter_custom_fusion.1
  287.6 8.6 fusion.44
  296.2 7.6 fusion.46
  303.8 54.8 %all-to-all-done.2 = bf16[8,192,2048]{2,1,0:T(8,128)(2,1)} async-done(((bf16[8,192,2048]{2,1,0:T(8,128)(2,1)}), bf16[8,192,2048]{2,1,0:T(8,128)(2,1)}, u32[]{:S(2)}, u32[]{:S(2)}) %all-to-all-start.2) | async-done | bytes 6291488 | tf_op jit(solution)/shard_map/all_to_all | solution.py:57
  358.6 9.5 fusion.66
  371.5 6.8 add_bitcast_fusion
  378.3 11.3 copy.193
  395.5 7.9 convolution_bitcast_fusion.5
  403.4 11.9 copy.190
  415.3 133.1 %all-to-all-done.3 = f32[8,192,2048]{2,1,0:T(8,128)} async-done(((f32[8,192,2048]{2,1,0:T(8,128)}), f32[8,192,2048]{2,1,0:T(8,128)}, u32[]{:S(2)}, u32[]{:S(2)}) %all-to-all-start.3) | async-done | bytes 12582944 | tf_op jit(solution)/shard_map/all_to_all | solution.py:61
  548.4 5.5 all-to-all-start.1
  558.3 78.7 %all-gather.21.cloned.1.call-done = bf16[2048,704]{0,1:T(8,128)(2,1)} async-done(((bf16[512,704]{0,1:T(8,128)(2,1)}), bf16[2048,704]{0,1:T(8,128)(2,1)}) %all-gather.21.cloned.1.call-update) | async-done | bytes 2883600 | tf_op jit(solution)/shard_map/all_gather | solution.py:112
  639.8 75.0 %all-gather.23.cloned.1.call-done = bf16[704,2048]{1,0:T(8,128)(2,1)} async-done(((bf16[704,512]{1,0:T(8,128)(2,1)}), bf16[704,2048]{1,0:T(8,128)(2,1)}) %all-gather.23.cloned.1.call-update) | async-done | bytes 2883600 | tf_op jit(solution)/shard_map/all_gather | solution.py:113
  718.2 12.1 gather_fusion.1
  730.2 7.8 reshape.404
  738.1 7.0 reduce_sum.192
  749.8 11.9 gather_fusion
  761.7 7.9 reshape.399
  769.6 7.4 multiply_reduce_fusion
  777.0 21.3 %psum.122 = f32[128,6]{1,0:T(8,128)S(1)} all-reduce(f32[128,6]{1,0:T(8,128)S(1)} %get-tuple-element.303), channel_id=1, replica_groups=mesh['shard'=4,'ctx'=2,'tp'=4] {'tp'}, use_global_device_ids=true, to_apply=%region_21.22 | all-reduce | flops 768 | bytes 6144 | tf_op jit(solution)/shard_map/psum | solution.py:218
  809.3 5.6 while.31
  824.6 17.1 %reduce-scatter.10.cloned.1.call-done = f32[128,1280]{0,1:T(8,128)} async-done(((f32[256,1280]{0,1:T(8,128)}), f32[128,1280]{0,1:T(8,128)}) %reduce-scatter.10.cloned.1.call-update) | async-done | bytes 655376 | tf_op jit(solution)/shard_map/reduce_scatter | solution.py:334
  868.2 72.9 %all-reduce.16.cloned.1.call-done = (f32[128,2048]{1,0:T(8,128)}, f32[128,2048]{1,0:T(8,128)}, f32[128,576]{0,1:T(8,128)}) async-done(((f32[128,2048]{1,0:T(8,128)}, f32[128,2048]{1,0:T(8,128)}, f32[128,576]{0,1:T(8,128)}), (f32[128,2048]{1,0:T(8,128)}, f32[128,2048]{1,0:T(8,128)}, f32[128,576]{0,1:T(8,128)})) %all-reduce.16.cloned.1.call-update) | async-done | bytes 2392080 | tf_op jit(solution)/shard_map/psum | solution.py:218
  948.4 49.1 %reduce-scatter.22.cloned.1.call-done = f32[512,704]{0,1:T(8,128)} async-done(((f32[2048,704]{0,1:T(8,128)}), f32[512,704]{0,1:T(8,128)}) %reduce-scatter.22.cloned.1.call-update) | async-done | bytes 1441808 | tf_op jit(solution)/shard_map/reduce_scatter | solution.py:389
  997.6 57.7 %reduce-scatter.24.cloned.1.call-done = f32[512,704]{0,1:T(8,128)} async-done(((f32[2048,704]{0,1:T(8,128)}), f32[512,704]{0,1:T(8,128)}) %reduce-scatter.24.cloned.1.call-update) | async-done | bytes 1441808 | tf_op jit(solution)/shard_map/reduce_scatter | solution.py:390
  1055.3 57.6 %reduce-scatter.26.cloned.1.call-done = f32[704,512]{1,0:T(8,128)} async-done(((f32[704,2048]{1,0:T(8,128)}), f32[704,512]{1,0:T(8,128)}) %reduce-scatter.26.cloned.1.call-update) | async-done | bytes 1441808 | tf_op jit(solution)/shard_map/reduce_scatter | solution.py:391
  1112.8 33.6 %reduce-scatter.16.cloned.1.call-done = f32[128,1024]{1,0:T(8,128)} async-done(((f32[512,1024]{1,0:T(8,128)}), f32[128,1024]{1,0:T(8,128)}) %reduce-scatter.16.cloned.1.call-update) | async-done | bytes 524304 | tf_op jit(solution)/shard_map/reduce_scatter | solution.py:385
  1146.4 46.8 %reduce-scatter.18.cloned.1.call-done = f32[512,512]{1,0:T(8,128)} async-done(((f32[512,2048]{1,0:T(8,128)}), f32[512,512]{1,0:T(8,128)}) %reduce-scatter.18.cloned.1.call-update) | async-done | bytes 1048592 | tf_op jit(solution)/shard_map/reduce_scatter | solution.py:386
  1193.3 61.3 %reduce-scatter.12.cloned.1.call-done = f32[512,768]{1,0:T(8,128)} async-done(((f32[2048,768]{1,0:T(8,128)}), f32[512,768]{1,0:T(8,128)}) %reduce-scatter.12.cloned.1.call-update) | async-done | bytes 1572880 | tf_op jit(solution)/shard_map/reduce_scatter | solution.py:382
  1254.5 50.2 %reduce-scatter.14.cloned.1.call-done = f32[512,576]{0,1:T(8,128)} async-done(((f32[2048,576]{0,1:T(8,128)}), f32[512,576]{0,1:T(8,128)}) %reduce-scatter.14.cloned.1.call-update) | async-done | bytes 1179664 | tf_op jit(solution)/shard_map/reduce_scatter | solution.py:383
  1307.3 8.2 convolution_bitcast_fusion.6
  1315.5 7.9 convolution_bitcast_fusion.7
  1323.4 8.0 fusion.48
  1333.1 10.8 all-reduce.4
  1346.4 10.9 all-reduce.5
  1360.1 174.8 %all-reduce.18.cloned.1.call-done = (f32[512,768]{1,0:T(8,128)}, f32[512,576]{0,1:T(8,128)}, f32[128,1024]{1,0:T(8,128)}, f32[512,512]{1,0:T(8,128)}, f32[512,70...) async-done(((f32[512,768]{1,0:T(8,128)}, f32[512,576]{0,1:T(8,128)}, f32[128,1024]{1,0:T(8,128)}, f32[512,512]{1,0:T(8,128)}, f32[512,704]{0,1:T(8,128)}, ...) | async-done | bytes 8650768 | tf_op jit(solution)/shard_map/psum | solution.py:405
  (352 shorter events, 182.9 us)
Async XLA Ops:
  7.2 351.4 %copy-start = (bf16[2,352,2048]{2,1,0:T(8,128)(2,1)S(1)}, bf16[2,352,2048]{2,1,0:T(8,128)(2,1)}, u32[]{:S(2)}) copy-start(bf16[2,352,2048]{2,1,0:T(8,128)(2,1)} %param.35) | copy-start | bytes 8650756
  7.2 29.2 %copy-start.2 = (bf16[128,2048]{1,0:T(8,128)(2,1)S(1)}, bf16[128,2048]{1,0:T(8,128)(2,1)}, u32[]{:S(2)}) copy-start(bf16[128,2048]{1,0:T(8,128)(2,1)} %param.21) | copy-start | bytes 1572868
  7.2 29.2 %all-gather.11.cloned.1.call-start = ((), (), s32[]{:S(2)}) async-start(), calls=%async_computation.13 | async-start | bytes 2949120 | tf_op jit(solution)/shard_map/all_gather | solution.py:105
  7.9 46.7 %all-gather.13.cloned.1.call-start = ((), (), s32[]{:S(2)}) async-start(), calls=%async_computation.14 | async-start | bytes 1310720 | tf_op jit(solution)/shard_map/all_gather | solution.py:107
  8.7 76.1 %all-gather.15.cloned.1.call-start = ((), (), s32[]{:S(2)}) async-start(), calls=%async_computation.15 | async-start | bytes 3932160 | tf_op jit(solution)/shard_map/all_gather | solution.py:104
  9.4 99.4 %all-gather.17.cloned.1.call-start = ((), (), s32[]{:S(2)}) async-start(), calls=%async_computation.16 | async-start | bytes 2621440 | tf_op jit(solution)/shard_map/all_gather | solution.py:108
  10.0 153.9 %all-reduce.12.cloned.1.call-start = ((), (), s32[]{:S(2)}) async-start(), calls=%async_computation.17 | async-start | bytes 2097152 | tf_op jit(solution)/shard_map/psum | solution.py:176
  10.1 30.3 %copy-start.74 = (f32[32]{0:T(128)}, f32[32]{0:T(128)S(1)}, u32[]{:S(2)}) copy-start(f32[32]{0:T(128)S(1)} %negate_power_fusion) | copy-start | bytes 388
  11.8 73.0 %copy-start.62 = (f32[128]{0:T(128)}, f32[128]{0:T(128)S(1)}, u32[]{:S(2)}) copy-start(f32[128]{0:T(128)S(1)} %fusion.115) | copy-start | bytes 1540
  18.7 66.1 %copy-start.49 = (f32[4,1,512]{2,1,0:T(1,128)}, f32[4,1,512]{2,1,0:T(1,128)S(1)}, u32[]{:S(2)}) copy-start(f32[4,1,512]{2,1,0:T(1,128)S(1)} %convert_element_type.122) | copy-start | bytes 24580
  24.2 41.4 %copy-start.60 = (f32[4,1,128]{2,1,0:T(1,128)}, f32[4,1,128]{2,1,0:T(1,128)S(1)}, u32[]{:S(2)}) copy-start(f32[4,1,128]{2,1,0:T(1,128)S(1)} %convert_element_type.123) | copy-start | bytes 6148
  39.6 48.4 %copy-start.81 = (f32[128]{0:T(128)}, f32[128]{0:T(128)S(1)}, u32[]{:S(2)}) copy-start(f32[128]{0:T(128)S(1)} %multiply_reduce_fusion.8) | copy-start | bytes 1540
  40.4 49.2 %copy-start.52 = (f32[128,32]{0,1:T(8,128)}, f32[128,32]{0,1:T(8,128)S(1)}, u32[]{:S(2)}) copy-start(f32[128,32]{0,1:T(8,128)S(1)} %get-tuple-element.398) | copy-start | bytes 49156
  45.0 43.1 %copy-start.70 = (f32[128]{0:T(128)}, f32[128]{0:T(128)S(1)}, u32[]{:S(2)}) copy-start(f32[128]{0:T(128)S(1)} %fusion.116) | copy-start | bytes 1540
  100.0 65.3 %copy-start.36 = (bf16[4,128,128]{1,2,0:T(8,128)(2,1)}, bf16[4,128,128]{1,2,0:T(8,128)(2,1)S(1)}, u32[]{:S(2)}) copy-start(bf16[4,128,128]{1,2,0:T(8,128)(2,1)S(1)} %divide_convert_fusion) | copy-start | bytes 393220
  120.9 69.9 %copy-start.55 = (f32[4,1,512]{2,1,0:T(1,128)}, f32[4,1,512]{2,1,0:T(1,128)S(1)}, u32[]{:S(2)}) copy-start(f32[4,1,512]{2,1,0:T(1,128)S(1)} %convert_element_type.124) | copy-start | bytes 24580
  165.4 25.5 %copy-start.72 = (f32[128]{0:T(128)}, f32[128]{0:T(128)S(1)}, u32[]{:S(2)}) copy-start(f32[128]{0:T(128)S(1)} %fusion.117) | copy-start | bytes 1540
  190.9 91.8 %all-to-all-start = ((bf16[8,192,2048]{2,1,0:T(8,128)(2,1)}), bf16[8,192,2048]{2,1,0:T(8,128)(2,1)}, u32[]{:S(2)}, u32[]{:S(2)}) async-start(bf16[8,192,2048]{2,1,0:T(8,128)(2,1)} %bitcast.283), calls=%async_computation | async-start | bytes 12582912 | tf_op jit(solution)/shard_map/all_to_all | solution.py:57
  201.3 66.8 %copy-start.58 = (s32[128,6]{0,1:T(8,128)S(1)}, s32[128,6]{0,1:T(8,128)}, u32[]{:S(2)}) copy-start(s32[128,6]{0,1:T(8,128)} %param.36) | copy-start | bytes 9220
  282.6 75.9 %all-to-all-start.2 = ((bf16[8,192,2048]{2,1,0:T(8,128)(2,1)}), bf16[8,192,2048]{2,1,0:T(8,128)(2,1)}, u32[]{:S(2)}, u32[]{:S(2)}) async-start(bf16[8,192,2048]{2,1,0:T(8,128)(2,1)} %bitcast.284), calls=%async_computation.2 | async-start | bytes 12582912 | tf_op jit(solution)/shard_map/all_to_all | solution.py:57
  389.6 158.8 %all-to-all-start.3 = ((f32[8,192,2048]{2,1,0:T(8,128)}), f32[8,192,2048]{2,1,0:T(8,128)}, u32[]{:S(2)}, u32[]{:S(2)}) async-start(f32[8,192,2048]{2,1,0:T(8,128)} %bitcast.277), calls=%async_computation.3 | async-start | bytes 25165824 | tf_op jit(solution)/shard_map/all_to_all | solution.py:61
  394.9 160.6 %all-gather.19.cloned.1.call-start = ((), (), s32[]{:S(2)}) async-start(), calls=%async_computation.18 | async-start | bytes 3604480 | tf_op jit(solution)/shard_map/all_gather | solution.py:111
  548.4 201.3 %all-to-all-start.1 = ((f32[8,192,2048]{2,1,0:T(8,128)}), f32[8,192,2048]{2,1,0:T(8,128)}, u32[]{:S(2)}, u32[]{:S(2)}) async-start(f32[8,192,2048]{2,1,0:T(8,128)} %bitcast.276), calls=%async_computation.1 | async-start | bytes 25165824 | tf_op jit(solution)/shard_map/all_to_all | solution.py:61
  553.9 83.2 %all-gather.21.cloned.1.call-start = ((), (), s32[]{:S(2)}) async-start(), calls=%async_computation.19 | async-start | bytes 3604480 | tf_op jit(solution)/shard_map/all_gather | solution.py:112
  554.7 160.1 %all-gather.23.cloned.1.call-start = ((), (), s32[]{:S(2)}) async-start(), calls=%async_computation.20 | async-start | bytes 3604480 | tf_op jit(solution)/shard_map/all_gather | solution.py:113
  555.4 246.9 %all-reduce.14.cloned.1.call-start = ((), (), s32[]{:S(2)}) async-start(), calls=%async_computation.21 | async-start | bytes 2097152 | tf_op jit(solution)/shard_map/psum | solution.py:266
  555.5 159.3 %copy-start.6 = (f32[128,2048]{1,0:T(8,128)S(1)}, f32[128,2048]{1,0:T(8,128)}, u32[]{:S(2)}) copy-start(f32[128,2048]{1,0:T(8,128)} %param.37) | copy-start | bytes 3145732
  718.2 26.9 %copy-start.33 = (bf16[128,704]{0,1:T(8,128)(2,1)}, bf16[128,704]{0,1:T(8,128)(2,1)S(1)}, u32[]{:S(2)}) copy-start(bf16[128,704]{0,1:T(8,128)(2,1)S(1)} %get-tuple-element.388) | copy-start | bytes 540676
  718.2 29.8 %copy-start.31 = (bf16[128,704]{0,1:T(8,128)(2,1)}, bf16[128,704]{0,1:T(8,128)(2,1)S(1)}, u32[]{:S(2)}) copy-start(bf16[128,704]{0,1:T(8,128)(2,1)S(1)} %get-tuple-element.387) | copy-start | bytes 540676
  749.7 92.0 %reduce-scatter.10.cloned.1.call-start = ((), (), s32[]{:S(2)}) async-start(), calls=%async_computation.22 | async-start | bytes 1966080 | tf_op jit(solution)/shard_map/reduce_scatter | solution.py:334
  769.6 28.8 %copy-start.59 = (s32[128,6]{0,1:T(8,128)S(1)}, s32[128,6]{0,1:T(8,128)}, u32[]{:S(2)}) copy-start(s32[128,6]{0,1:T(8,128)} %param.36) | copy-start | bytes 9220
  769.6 28.9 %copy-start.67 = (f32[128]{0:T(128)S(1)}, f32[128]{0:T(128)}, u32[]{:S(2)}) copy-start(f32[128]{0:T(128)} %copy-done.66) | copy-start | bytes 1540
  769.6 28.9 %copy-start.69 = (f32[128]{0:T(128)S(1)}, f32[128]{0:T(128)}, u32[]{:S(2)}) copy-start(f32[128]{0:T(128)} %copy-done.68) | copy-start | bytes 1540
  769.6 32.7 %copy-start.5 = (f32[128,2048]{1,0:T(8,128)S(1)}, f32[128,2048]{1,0:T(8,128)}, u32[]{:S(2)}) copy-start(f32[128,2048]{1,0:T(8,128)} %copy-done.4) | copy-start | bytes 3145732
  769.6 32.7 %copy-start.56 = (f32[4,1,512]{2,1,0:T(1,128)S(1)}, f32[4,1,512]{2,1,0:T(1,128)}, u32[]{:S(2)}) copy-start(f32[4,1,512]{2,1,0:T(1,128)} %copy-done.55) | copy-start | bytes 24580
  769.6 32.7 %copy-start.73 = (f32[128]{0:T(128)S(1)}, f32[128]{0:T(128)}, u32[]{:S(2)}) copy-start(f32[128]{0:T(128)} %copy-done.72) | copy-start | bytes 1540
  777.0 27.1 %copy-start.84 = (f32[128]{0:T(128)S(1)}, f32[128]{0:T(128)}, u32[]{:S(2)}) copy-start(f32[128]{0:T(128)} %copy-done.83) | copy-start | bytes 1540
  814.9 126.1 %all-reduce.16.cloned.1.call-start = ((), (), s32[]{:S(2)}) async-start(), calls=%async_computation.31 | async-start | bytes 4784128 | tf_op jit(solution)/shard_map/psum | solution.py:218
  845.1 152.5 %reduce-scatter.22.cloned.1.call-start = ((), (), s32[]{:S(2)}) async-start(), calls=%async_computation.28 | async-start | bytes 7208960 | tf_op jit(solution)/shard_map/reduce_scatter | solution.py:389
  848.6 206.7 %reduce-scatter.24.cloned.1.call-start = ((), (), s32[]{:S(2)}) async-start(), calls=%async_computation.29 | async-start | bytes 7208960 | tf_op jit(solution)/shard_map/reduce_scatter | solution.py:390
  852.9 259.9 %reduce-scatter.26.cloned.1.call-start = ((), (), s32[]{:S(2)}) async-start(), calls=%async_computation.30 | async-start | bytes 7208960 | tf_op jit(solution)/shard_map/reduce_scatter | solution.py:391
  857.6 288.8 %reduce-scatter.16.cloned.1.call-start = ((), (), s32[]{:S(2)}) async-start(), calls=%async_computation.25 | async-start | bytes 2621440 | tf_op jit(solution)/shard_map/reduce_scatter | solution.py:385
  860.4 332.8 %reduce-scatter.18.cloned.1.call-start = ((), (), s32[]{:S(2)}) async-start(), calls=%async_computation.26 | async-start | bytes 5242880 | tf_op jit(solution)/shard_map/reduce_scatter | solution.py:386
  863.3 391.3 %reduce-scatter.12.cloned.1.call-start = ((), (), s32[]{:S(2)}) async-start(), calls=%async_computation.23 | async-start | bytes 7864320 | tf_op jit(solution)/shard_map/reduce_scatter | solution.py:382
  868.1 74.9 %copy-start.82 = (f32[128]{0:T(128)S(1)}, f32[128]{0:T(128)}, u32[]{:S(2)}) copy-start(f32[128]{0:T(128)} %copy-done.81) | copy-start | bytes 1540
  868.1 436.6 %reduce-scatter.14.cloned.1.call-start = ((), (), s32[]{:S(2)}) async-start(), calls=%async_computation.24 | async-start | bytes 5898240 | tf_op jit(solution)/shard_map/reduce_scatter | solution.py:383
  947.2 399.2 %reduce-scatter.20.cloned.1.call-start = ((), (), s32[]{:S(2)}) async-start(), calls=%async_computation.27 | async-start | bytes 163840 | tf_op jit(solution)/shard_map/reduce_scatter | solution.py:388
  948.1 586.8 %all-reduce.18.cloned.1.call-start = ((), (), s32[]{:S(2)}) async-start(), calls=%async_computation.32 | async-start | bytes 17301504 | tf_op jit(solution)/shard_map/psum | solution.py:405
  (62 other events, 333.4 us)
Sparse Core Ops, SparseCore 0:
  9.6 26.7 all-gather.10
  38.0 16.6 all-gather.12
  56.2 28.4 all-gather.14
  86.2 22.5 all-gather.16
  112.0 51.8 all-reduce.11
  397.0 80.4 all-gather.18
  556.3 80.7 all-gather.20
  638.6 76.1 all-gather.22
  749.8 52.4 all-reduce.13
  815.0 26.6 reduce-scatter.9
  845.2 95.7 all-reduce.15
  944.0 53.5 reduce-scatter.21
  1000.7 54.5 reduce-scatter.23
  1058.2 54.5 reduce-scatter.25
  1115.2 31.1 reduce-scatter.15
  1148.8 44.4 reduce-scatter.17
  1195.6 58.8 reduce-scatter.11
  1256.9 47.7 reduce-scatter.13
  1307.7 19.6 reduce-scatter.19
  1330.3 204.6 all-reduce.17
where the time goes:
time: 1560 us; the launch traced here: 1550 us
  waiting for transfers between devices  1050 us (67%)
  local copies, waits for them, and re-layouts  145 us (9%)
  matrix products  134 us (9%)
  blocking collectives  131 us (8%)
  other arithmetic  55.8 us (4%)
  starting transfers between devices  21.6 us (1%)
  between operations  16.9 us (1%)
    psum x1, waiting for transfers between devices, per_device(): lax.psum((red_one, red_query, red_latent, red_kv, red_expand, red_output,...  175 us
    all_to_all x2, waiting for transfers between devices, return_rows(): lax.all_to_all(partial_value, ('shard', 'ctx'), split_axis=0, concat_axis...  133 us
    all_gather x1, waiting for transfers between devices, per_device(): lax.all_gather(shared_up, 'shard', axis=0, tiled=True)  78.7 us
    all_gather x1, waiting for transfers between devices, per_device(): lax.all_gather(shared_down, 'shard', axis=1, tiled=True)  75 us
    psum x1, waiting for transfers between devices, per_device(): moe_out, route_grad = lax.psum((routed_part, weight_part), 'tp')  72.9 us
    reduce_scatter x1, waiting for transfers between devices, per_device(): lax.psum_scatter(grad_query, 'shard', scatter_dimension=0, tiled=True)  61.3 us
    reduce_scatter x1, waiting for transfers between devices, per_device(): lax.psum_scatter(grad_sup, 'shard', scatter_dimension=0, tiled=True)  57.7 us
    all_gather x1, blocking collectives, per_device(): lax.all_gather(router_weight, 'shard', axis=0, tiled=True)  57.7 us
  transfers between devices with their start and end apart: 24, of which 20 were waited for; matrix products, arithmetic and copies ran while one was open for 16% of the time, Pallas kernels for 0%

commit v1 on v0

--- a/solution.py
+++ b/solution.py
@@ -1,27 +1,45 @@
+import functools
+
 import jax
 import jax.numpy as jnp
 from jax import lax
+from jax.experimental import pallas as pl
+from jax.experimental.pallas import tpu as pltpu
 from jax.sharding import PartitionSpec as P
 
 DN = 128
 DR = 64
 DV = 128
 KVR = 512
-
+LANES = 128
+SHARD, CTX, TP = "shard", "ctx", "tp"
 
 EPS = 1e-06
 NEG = -1e30
 
+BF = jnp.bfloat16
+F32 = jnp.float32
+MESH = pl.DeviceIdType.MESH
+ANY = pl.ANY
+VMEM = pltpu.VMEM
+
 
 def norm_rows(value, gain):
     factor = lax.rsqrt(jnp.mean(value * value, axis=-1, keepdims=True) + EPS)
-    return value * factor * gain.astype(jnp.float32)
+    return value * factor * gain.astype(F32)
+
+
+def norm_back(value, gain, grad):
+    factor = lax.rsqrt(jnp.mean(value * value, axis=-1, keepdims=True) + EPS)
+    scaled = grad * gain.astype(F32)
+    inner = jnp.mean(scaled * value, axis=-1, keepdims=True)
+    return factor * (scaled - value * (factor * factor * inner)), grad * value * factor
 
 
 def rope_tables(count, offset):
     half_size = DR // 2
-    position = jnp.arange(count, dtype=jnp.float32) + offset
-    freqs = 10000.0 ** (-(jnp.arange(half_size, dtype=jnp.float32) * 2.0 / DR))
+    position = jnp.arange(count, dtype=F32) + offset
+    freqs = 10000.0 ** (-(jnp.arange(half_size, dtype=F32) * 2.0 / DR))
     angle = position[:, None] * freqs[None, :]
     return (jnp.cos(angle), jnp.sin(angle))
 
@@ -50,22 +68,878 @@
 
 
 def mdot(left, right):
-    return jnp.dot(left, right, preferred_element_type=jnp.float32)
+    return jnp.dot(left, right, preferred_element_type=F32)
+
+
+def dot_nt(left, right):
+    return lax.dot_general(left, right, (((1,), (1,)), ((), ())), preferred_element_type=F32)
+
+
+def dot_tn(left, right):
+    return lax.dot_general(left, right, (((0,), (0,)), ((), ())), preferred_element_type=F32)
+
+
+class Place:
+    def __init__(self, n_tp):
+        self.s = lax.axis_index(SHARD)
+        self.c = lax.axis_index(CTX)
+        self.t = lax.axis_index(TP)
+        self.core = lax.rem(self.s, 2)
+        self.y = self.s // 2
+        self.n_tp = n_tp
+
+    def at(self, s, c, t):
+        return {SHARD: s, CTX: c, TP: t}
+
+    @property
+    def over_x(self):
+        return self.at(self.s, 1 - self.c, self.t)
+
+    @property
+    def over_y(self):
+        return self.at(lax.rem(self.s + 2, 4), self.c, self.t)
+
+    @property
+    def over_core(self):
+        return self.at(self.s + 1 - 2 * self.core, self.c, self.t)
+
+    def along(self, step):
+        return self.at(self.s, self.c, lax.rem(self.t + step + self.n_tp, self.n_tp))
+
+    def flip(self, dy, dcore, dx):
+        y = self.y + dy * (1 - 2 * self.y)
+        core = self.core + dcore * (1 - 2 * self.core)
+        x = self.c + dx * (1 - 2 * self.c)
+        return self.at(2 * y + core, x, self.t)
+
+
+def slot(s, c):
+    return 2 * s + c
+
+
+class Net:
+    def __init__(self, send, recv, local):
+        self.send, self.recv, self.local = send, recv, local
+        self.puts, self.locals = [], []
+        self.n_local = 0
+
+    def put(self, src, dst, to):
+        i = len(self.puts)
+        copy = pltpu.make_async_remote_copy(
+            src_ref=src,
+            dst_ref=dst,
+            send_sem=self.send.at[i],
+            recv_sem=self.recv.at[i],
+            device_id=to,
+            device_id_type=MESH,
+        )
+        copy.start()
+        self.puts.append(copy)
+        return copy
+
+    def move(self, src, dst):
+        copy = pltpu.make_async_copy(src, dst, self.local.at[self.n_local])
+        self.n_local += 1
+        copy.start()
+        return copy
+
+    def finish(self):
+        for copy in self.puts:
+            copy.wait_send()
+
+
+def greet(peers):
+    barrier = pltpu.get_barrier_semaphore()
+    for peer in peers:
+        pl.semaphore_signal(barrier, inc=1, device_id=peer, device_id_type=MESH)
+    pl.semaphore_wait(barrier, len(peers))
+
+
+def comm_call(body, ins, outs, scratch, n_put, n_local, collective_id, name, in_space, out_space):
+    return pl.pallas_call(
+        body,
+        out_shape=tuple(jax.ShapeDtypeStruct(shape, dtype) for shape, dtype in outs),
+        in_specs=[pl.BlockSpec(memory_space=space) for space in in_space],
+        out_specs=tuple(pl.BlockSpec(memory_space=space) for space in out_space),
+        scratch_shapes=[
+            *scratch,
+            pltpu.SemaphoreType.DMA((n_put,)),
+            pltpu.SemaphoreType.DMA((n_put,)),
+            pltpu.SemaphoreType.DMA((max(n_local, 1),)),
+        ],
+        compiler_params=pltpu.CompilerParams(
+            collective_id=collective_id, has_side_effects=True, vmem_limit_bytes=60 * 2**20
+        ),
+        name=name,
+    )(*ins)
+
+
+def start_gather(weights, small, block, n_tp):
+    shapes = [w.shape for w in weights]
+
+    def body(*refs):
+        n = len(shapes)
+        w_in, (small_in, x_in) = refs[:n], refs[n : n + 2]
+        w_out, (small_out, x_out) = refs[n + 2 : 2 * n + 2], refs[2 * n + 2 : 2 * n + 4]
+        bounce = refs[2 * n + 4 : 3 * n + 6]
+        send, recv, local = refs[3 * n + 6 :]
+        me = Place(n_tp)
+        net = Net(send, recv, local)
+        greet([me.over_x, me.over_y, me.over_core])
+
+        def half(ref, index, which, rows):
+            return ref.at[index, pl.ds(which * (rows // 2), rows // 2)]
+
+        other = lax.rem(me.s + 2, 4)
+        loads = [net.move(src, b) for src, b in zip((*w_in, small_in, x_in), bounce)]
+        from_y, own = [], []
+        for ref, out, shape in zip(w_in, w_out, shapes):
+            rows = shape[0]
+            from_y.append(
+                net.put(ref.at[pl.ds(me.c * (rows // 2), rows // 2)], half(out, me.s, me.c, rows), me.over_y)
+            )
+            if ref is w_in[0]:
+                wait_x = net.put(x_in, x_out.at[me.c], me.over_x)
+        for ref, out in zip(w_in, w_out):
+            own.append(net.put(ref, out.at[me.s], me.over_core))
+        small_y = net.put(small_in, small_out.at[me.s], me.over_y)
+        small_c = net.put(small_in, small_out.at[me.s], me.over_core)
+        stores = []
+        outs = [o.at[me.s] for o in (*w_out, small_out)] + [x_out.at[me.c]]
+        for load, b, out in zip(loads, bounce, outs):
+            load.wait()
+            stores.append(net.move(b, out))
+        from_x, relays = [], []
+        for got, out, shape in zip(from_y, w_out, shapes):
+            rows = shape[0]
+            got.wait_recv()
+            piece = half(out, other, me.c, rows)
+            from_x.append(net.put(piece, piece, me.over_x))
+            relays.append(net.put(piece, piece, me.over_core))
+        small_y.wait_recv()
+        relays.append(net.put(small_out.at[other], small_out.at[other], me.over_core))
+        for got, out, shape in zip(from_x, w_out, shapes):
+            rows = shape[0]
+            got.wait_recv()
+            piece = half(out, other, 1 - me.c, rows)
+            relays.append(net.put(piece, piece, me.over_core))
+        wait_x.wait_recv()
+        small_c.wait_recv()
+        for got in own + relays:
+            got.wait_recv()
+        for store in stores:
+            store.wait()
+        net.finish()
+
+    n = len(weights)
+    outs = [((4, *w.shape), BF) for w in weights] + [((4, *small.shape), small.dtype), ((2, *block.shape), BF)]
+    return comm_call(
+        body,
+        (*weights, small, block),
+        outs,
+        [VMEM(w.shape, w.dtype) for w in (*weights, small, block)],
+        5 * n + 4,
+        2 * n + 4,
+        0,
+        "start_gather",
+        [ANY] * (n + 2),
+        [ANY] * (n + 2),
+    )
+
+
+def tp_reduce_scatter(part, n_tp, collective_id, name):
+    rows, width = part.shape
+    piece = rows // n_tp
+
+    def body(in_ref, out_ref, got, send, recv, local):
+        me = Place(n_tp)
+        net = Net(send, recv, local)
+        greet([me.along(k) for k in range(1, n_tp)])
+        waits = []
+        for k in range(1, n_tp):
+            to = lax.rem(me.t + k, n_tp)
+            waits.append(
+                net.put(in_ref.at[pl.ds(to * piece, piece)], got.at[k - 1], me.along(k))
+            )
+        for wait in waits:
+            wait.wait_recv()
+        total = in_ref[pl.ds(pl.multiple_of(me.t * piece, piece), piece), :].astype(F32)
+        for k in range(1, n_tp):
+            total = total + got[k - 1].astype(F32)
+        out_ref[...] = total
+        net.finish()
+
+    return comm_call(
+        body,
+        (part,),
+        [((piece, width), F32)],
+        [VMEM((n_tp - 1, piece, width), BF)],
+        n_tp - 1,
+        0,
+        collective_id,
+        name,
+        [VMEM],
+        [VMEM],
+    )[0]
+
+
+def tp_ring(net, me, own, out, base):
+    piece = own.shape[0]
+    half = piece // 2
+
+    def rows(p, which=None):
+        start = base + p * piece
+        if which is None:
+            return out.at[pl.ds(start, piece)]
+        return out.at[pl.ds(start + which * half, half)]
+
+    right, left = me.along(1), me.along(-1)
+    p_left, p_right = lax.rem(me.t + 3, 4), lax.rem(me.t + 1, 4)
+    far = lax.rem(me.t + 2, 4)
+    to_right = net.put(own, rows(me.t), right)
+    to_left = net.put(own, rows(me.t), left)
+    to_right.wait_recv()
+    hop_right = net.put(rows(p_left, 0), rows(p_left, 0), right)
+    yield p_left
+    to_left.wait_recv()
+    hop_left = net.put(rows(p_right, 1), rows(p_right, 1), left)
+    yield p_right
+    hop_right.wait_recv()
+    hop_left.wait_recv()
+    yield far
+
+
+def tp_all_gather(pieces, n_tp, collective_id, name):
+    def body(*refs):
+        n = len(pieces)
+        ins, outs, (send, recv, local) = refs[:n], refs[n : 2 * n], refs[2 * n :]
+        me = Place(n_tp)
+        net = Net(send, recv, local)
+        greet([me.along(1), me.along(-1)])
+        rings = []
+        for src, dst in zip(ins, outs):
+            size = src.shape[0]
+            rings.append(tp_ring(net, me, src, dst, 0))
+        for _ in range(3):
+            for ring in rings:
+                next(ring)
+        for src, dst in zip(ins, outs):
+            size = src.shape[0]
+            dst[pl.ds(pl.multiple_of(me.t * size, size), size), :] = src[...]
+        net.finish()
+
+    return comm_call(
+        body,
+        pieces,
+        [((n_tp * p.shape[0], p.shape[1]), p.dtype) for p in pieces],
+        [],
+        4 * len(pieces),
+        0,
+        collective_id,
+        name,
+        [VMEM] * len(pieces),
+        [VMEM] * len(pieces),
+    )
+
+
+def relay_chunks(net, me, out, chunks):
+    g_x, g_y = slot(me.s, 1 - me.c), slot(lax.rem(me.s + 2, 4), me.c)
+    g_d = slot(lax.rem(me.s + 2, 4), 1 - me.c)
+    first = 1 - me.core
+    relay_slot = first * g_x + me.core * g_y
+    relay_to = me.flip(first, 0, me.core)
+    diags, waits = [], []
+    for from_x, from_y, (start, size) in chunks:
+        from_x.wait_recv()
+        from_y.wait_recv()
+        src = out.at[relay_slot, pl.ds(start, size)]
+        diags.append(net.put(src, src, relay_to))
+        for g in (g_x, g_y):
+            piece = out.at[g, pl.ds(start, size)]
+            waits.append(net.put(piece, piece, me.over_core))
+    for diag, (_, _, (start, size)) in zip(diags, chunks):
+        diag.wait_recv()
+        piece = out.at[g_d, pl.ds(start, size)]
+        waits.append(net.put(piece, piece, me.over_core))
+    return waits
+
+
+def gather_everywhere(own, n_tp, collective_id, name):
+    piece, width = own.shape
+
+    def body(in_ref, out_ref, bounce, send, recv, local):
+        me = Place(n_tp)
+        net = Net(send, recv, local)
+        greet([me.over_x, me.over_y, me.over_core, me.along(1), me.along(-1)])
+        load = net.move(in_ref, bounce)
+        g_me = slot(me.s, me.c)
+        chunks, cores = [], []
+
+        def spread(src, p):
+            dst = out_ref.at[g_me, pl.ds(p * piece, piece)]
+            from_x = net.put(src, dst, me.over_x)
+            from_y = net.put(src, dst, me.over_y)
+            cores.append(net.put(src, dst, me.over_core))
+            chunks.append((from_x, from_y, (p * piece, piece)))
+
+        spread(in_ref, me.t)
+        ring = tp_ring(net, me, in_ref, out_ref.at[g_me], 0)
+        load.wait()
+        store = net.move(bounce, out_ref.at[g_me, pl.ds(me.t * piece, piece)])
+        for p in ring:
+            spread(out_ref.at[g_me, pl.ds(p * piece, piece)], p)
+        waits = cores + relay_chunks(net, me, out_ref, chunks)
+        for wait in waits:
+            wait.wait_recv()
+        store.wait()
+        net.finish()
+
+    return comm_call(
+        body,
+        (own,),
+        [((8, n_tp * piece, width), own.dtype)],
+        [VMEM(own.shape, own.dtype)],
+        4 * 7 + 4,
+        2,
+        collective_id,
+        name,
+        [ANY],
+        [ANY],
+    )[0]
+
+
+def plane_exchange(gathers, columns, rows88, n_tp, collective_id, name, n_chunk=4):
+    ng, nc, nr = len(gathers), len(columns), len(rows88)
+    ins = (*gathers, *columns, *rows88)
+
+    def body(*refs):
+        n = ng + nc + nr
+        src, dst, bounce = refs[:n], refs[n : 2 * n], refs[2 * n : 3 * n]
+        send, recv, local = refs[3 * n :]
+        me = Place(n_tp)
+        net = Net(send, recv, local)
+        flips = [(dy, dk, dx) for dy in (0, 1) for dk in (0, 1) for dx in (0, 1)][1:]
+        if nc or nr:
+            greet([me.flip(*f) for f in flips])
+        else:
+            greet([me.over_x, me.over_y, me.over_core])
+        g_me = slot(me.s, me.c)
+        loads, waits, work = [], [], []
+        for i in range(n):
+            s, d, b = src[i], dst[i], bounce[i]
+            if i < ng:
+                rows = s.shape[0]
+                size = rows // n_chunk
+                chunks = []
+                for j in range(n_chunk):
+                    part = s.at[pl.ds(j * size, size)]
+                    to = d.at[g_me, pl.ds(j * size, size)]
+                    chunks.append((net.put(part, to, me.over_x), net.put(part, to, me.over_y), (j * size, size)))
+                    waits.append(net.put(part, to, me.over_core))
+                work.append((d, chunks))
+                loads.append((net.move(s, b), b, d.at[g_me]))
+            elif i < ng + nc:
+                w = s.shape[1] // 4
+                for f in flips:
+                    peer = me.flip(*f)
+                    part = s.at[:, pl.ds(pl.multiple_of(peer[SHARD] * w, LANES), w)]
+                    waits.append(net.put(part, d.at[g_me], peer))
+                part = s.at[:, pl.ds(pl.multiple_of(me.s * w, LANES), w)]
+                loads.append((net.move(part, b), b, d.at[g_me]))
+            else:
+                h, w = s.shape[0] // 8, s.shape[1]
+                to = d.at[:, pl.ds(pl.multiple_of(me.s * w, LANES), w)]
+                for f in ((0, 1, 0), (1, 0, 0), (1, 1, 0)):
+                    peer = me.flip(*f)
+                    row = pl.multiple_of(slot(peer[SHARD], peer[CTX]) * h, 8)
+                    waits.append(net.put(s.at[pl.ds(row, h)], to, peer))
+                row = pl.multiple_of(g_me * h, 8)
+                loads.append((net.move(s.at[pl.ds(row, h)], b), b, to))
+        stores = []
+        for load, b, to in loads:
+            load.wait()
+            stores.append(net.move(b, to))
+        for d, chunks in work:
+            waits += relay_chunks(net, me, d, chunks)
+        for wait in waits:
+            wait.wait_recv()
+        for store in stores:
+            store.wait()
+        net.finish()
+
+    outs, scratch = [], []
+    for a in gathers:
+        outs.append(((8, *a.shape), a.dtype))
+        scratch.append(VMEM(a.shape, a.dtype))
+    for a in columns:
+        outs.append(((8, a.shape[0], a.shape[1] // 4), a.dtype))
+        scratch.append(VMEM((a.shape[0], a.shape[1] // 4), a.dtype))
+    for a in rows88:
+        outs.append(((a.shape[0] // 8, a.shape[1] * 4), a.dtype))
+        scratch.append(VMEM((a.shape[0] // 8, a.shape[1]), a.dtype))
+    return comm_call(
+        body,
+        ins,
+        outs,
+        scratch,
+        ng * 7 * n_chunk + nc * 7 + nr * 3,
+        2 * len(ins),
+        collective_id,
+        name,
+        [ANY] * len(ins),
+        [ANY] * len(ins),
+    )
+
+
+def ctx_swap(block, collective_id, name):
+    def body(in_ref, out_ref, send, recv, local):
+        me = Place(1)
+        net = Net(send, recv, local)
+        greet([me.over_x])
+        net.put(in_ref, out_ref, me.over_x).wait_recv()
+        net.finish()
+
+    return comm_call(
+        body, (block,), [(block.shape, block.dtype)], [], 1, 0, collective_id, name, [ANY], [ANY]
+    )[0]
+
+
+def reduce_everywhere(part, n_tp, collective_id, name):
+    _, rows, width = part.shape
+    half = width // 2
+    piece = rows // n_tp
+    step = 16
+
+    def body(in_ref, out_ref, mine, rc, rx, ry, q0, q1, r0, r1, last, got, send, recv, local):
+        me = Place(n_tp)
+        net = Net(send, recv, local)
+        greet([me.over_x, me.over_y, me.over_core] + [me.along(k) for k in range(1, n_tp)])
+        a, b = pl.ds(0, half), pl.ds(half, half)
+        order = [(1, 1), (0, 1), (1, 0), (0, 0)]
+        pairs = []
+        for dy, dx in order:
+            y, x = me.y + dy * (1 - 2 * me.y), me.c + dx * (1 - 2 * me.c)
+            pairs.append((2 * y + x, slot(2 * y + me.core, x), slot(2 * y + 1 - me.core, x)))
+        loads, cores = [], []
+        for i, g_mine, g_other in pairs:
+            cores.append(net.put(in_ref.at[g_other], rc.at[i], me.over_core))
+            loads.append(net.move(in_ref.at[g_mine], mine.at[i]))
+
+        def add(target, cols, left, right):
+            def one(r, carry):
+                at = pl.ds(pl.multiple_of(r * step, step), step)
+                total = left(at).astype(F32) + right(at).astype(F32)
+                target[at, cols] = total.astype(target.dtype)
+                return carry
+
+            lax.fori_loop(0, rows // step, one, 0)
+
+        def sum_cores(k):
+            i = pairs[k][0]
+            loads[k].wait()
+            cores[k].wait_recv()
+            add(mine.at[i], pl.ds(0, width), lambda at: mine[i, at, :], lambda at: rc[i, at, :])
+            return i
+
+        i_yx = sum_cores(0)
+        ax0 = net.put(mine.at[i_yx, :, a], rx.at[1 - me.y], me.over_x)
+        by0 = net.put(mine.at[i_yx, :, b], ry.at[1 - me.c], me.over_y)
+        i_x = sum_cores(1)
+        ax1 = net.put(mine.at[i_x, :, a], rx.at[me.y], me.over_x)
+        i_y = sum_cores(2)
+        by1 = net.put(mine.at[i_y, :, b], ry.at[me.c], me.over_y)
+        i_me = sum_cores(3)
+        every = pl.ds(0, half)
+        ax0.wait_recv()
+        add(q0, every, lambda at: mine[i_y, at, a], lambda at: rx[1 - me.y, at, :])
+        y0 = net.put(q0, r0, me.over_y)
+        by0.wait_recv()
+        add(q1, every, lambda at: mine[i_x, at, b], lambda at: ry[1 - me.c, at, :])
+        x1 = net.put(q1, r1, me.over_x)
+        ax1.wait_recv()
+        by1.wait_recv()
+        y0.wait_recv()
+        x1.wait_recv()
+
+        def final(r, carry):
+            at = pl.ds(pl.multiple_of(r * step, step), step)
+            left = mine[i_me, at, a].astype(F32) + rx[me.y, at, :].astype(F32) + r0[at, :].astype(F32)
+            right = mine[i_me, at, b].astype(F32) + ry[me.c, at, :].astype(F32) + r1[at, :].astype(F32)
+            last[at, a] = left.astype(BF)
+            last[at, b] = right.astype(BF)
+            return carry
+
+        lax.fori_loop(0, rows // step, final, 0)
+        waits = []
+        for k in range(1, n_tp):
+            to = lax.rem(me.t + k, n_tp)
+            waits.append(net.put(last.at[pl.ds(to * piece, piece)], got.at[k - 1], me.along(k)))
+        for wait in waits:
+            wait.wait_recv()
+        for r in range(piece // step):
+            at = pl.ds(pl.multiple_of(me.t * piece + r * step, step), step)
+            total = last[at, :].astype(F32)
+            for k in range(n_tp - 1):
+                total = total + got[k, r * step : (r + 1) * step, :].astype(F32)
+            out_ref[r * step : (r + 1) * step, :] = total
+        net.finish()
+
+    block = (rows, width)
+    return comm_call(
+        body,
+        (part,),
+        [((piece, width), F32)],
+        [
+            VMEM((4, *block), BF),
+            VMEM((4, *block), BF),
+            VMEM((2, rows, half), BF),
+            VMEM((2, rows, half), BF),
+            VMEM((rows, half), BF),
+            VMEM((rows, half), BF),
+            VMEM((rows, half), BF),
+            VMEM((rows, half), BF),
+            VMEM(block, BF),
+            VMEM((n_tp - 1, piece, width), BF),
+        ],
+        10 + n_tp - 1,
+        4,
+        collective_id,
+        name,
+        [ANY],
+        [VMEM],
+    )[0]
+
+
+def sum_everywhere(part, n_tp, collective_id, name):
+    def body(in_ref, out_ref, from_tp, mid, from_plane, send, recv, local):
+        me = Place(n_tp)
+        net = Net(send, recv, local)
+        flips = [(dy, dk, dx) for dy in (0, 1) for dk in (0, 1) for dx in (0, 1)][1:]
+        greet([me.along(k) for k in range(1, n_tp)] + [me.flip(*f) for f in flips])
+        waits = [net.put(in_ref, from_tp.at[k - 1], me.along(k)) for k in range(1, n_tp)]
+        for wait in waits:
+            wait.wait_recv()
+        total = in_ref[...]
+        for k in range(n_tp - 1):
+            total = total + from_tp[k]
+        mid[...] = total
+        waits = [net.put(mid, from_plane.at[i], me.flip(*f)) for i, f in enumerate(flips)]
+        for wait in waits:
+            wait.wait_recv()
+        for i in range(7):
+            total = total + from_plane[i]
+        out_ref[...] = total
+        net.finish()
+
+    return comm_call(
+        body,
+        (part,),
+        [(part.shape, F32)],
+        [VMEM((n_tp - 1, *part.shape), F32), VMEM(part.shape, F32), VMEM((7, *part.shape), F32)],
+        n_tp - 1 + 7,
+        0,
+        collective_id,
+        name,
+        [VMEM],
+        [VMEM],
+    )[0]
+
+
+def per_device(
+    block_input,
+    norm1_gain,
+    q_weight,
+    kva_weight,
+    kv_norm_gain,
+    kvb_weight,
+    out_weight,
+    norm2_gain,
+    router_weight,
+    shared_gate,
+    shared_up,
+    shared_down,
+    expert_gate,
+    expert_up,
+    expert_down,
+    routes,
+    cotangent,
+):
+    n_tp = lax.axis_size(TP)
+    rows, width = block_input.shape
+    topk = routes.shape[1]
+    experts = router_weight.shape[1]
+    local_experts = expert_gate.shape[0]
+    heads = q_weight.shape[1] // (DN + DR)
+    scale = (DN + DR) ** (-0.5)
+    piece = rows // n_tp
+    s_id, c_id, t_id = lax.axis_index(SHARD), lax.axis_index(CTX), lax.axis_index(TP)
+    shard_w = width // 4
+    kv_w = KVR // 4
+
+    small = jnp.concatenate(
+        [
+            norm1_gain.reshape(-1, LANES),
+            norm2_gain.reshape(-1, LANES),
+            kv_norm_gain.reshape(-1, LANES),
+            jnp.zeros((7, LANES), BF),
+            jnp.pad(router_weight, ((0, 0), (0, LANES - experts))),
+        ]
+    )
+    w_query, w_latent, w_expand, w_output, small_all, x_pair = start_gather(
+        (q_weight, kva_weight, kvb_weight, out_weight), small, block_input, n_tp
+    )
+    w_query = w_query.reshape(width, -1)
+    w_latent = w_latent.reshape(width, -1)
+    w_expand = w_expand.reshape(KVR, -1)
+    w_output = w_output.transpose(1, 0, 2).reshape(-1, width)
+    gain_one = small_all[:, 0:4].reshape(-1)
+    gain_two = small_all[:, 4:8].reshape(-1)
+    gain_kv = small_all[:, 8:9].reshape(-1)
+    w_router = small_all[:, 16:, :experts].reshape(width, experts)
+
+    cot_b = cotangent.astype(BF)
+    cot_pack = jnp.concatenate(
+        [cot_b, jnp.pad(routes.astype(BF), ((0, 0), (0, LANES - topk)))], axis=1
+    )
+    cot_all, sg_t, su_t, sd = plane_exchange(
+        (cot_pack,), (), (shared_gate.T, shared_up.T, shared_down), n_tp, 1, "early_exchange"
+    )
+    cot_all = cot_all.reshape(-1, width + LANES)
+    routes_all = cot_all[:, width : width + topk].astype(jnp.int32)
+    cot_all = cot_all[:, :width]
+
+    x_float = block_input.astype(F32)
+    cosine, sine = rope_tables(rows, (c_id * rows).astype(F32))
+    cos_all, sin_all = rope_tables(2 * rows, jnp.float32(0))
+    normed_pair = norm_rows(x_pair.reshape(2 * rows, width).astype(F32), gain_one).astype(BF)
+    normed_one = norm_rows(x_float, gain_one).astype(BF)
+    query = mdot(normed_one, w_query).reshape(rows, heads, DN + DR)
+    query_nope = query[..., :DN].astype(BF)
+    query_rope = rotate(query[..., DN:], cosine[:, None, :], sine[:, None, :]).astype(BF)
+    latent = mdot(normed_pair, w_latent)
+    latent_pair = norm_rows(latent[:, :KVR], gain_kv).astype(BF)
+    rope_pair = rotate(latent[:, KVR:], cos_all, sin_all).astype(BF)
+    kv_pair = mdot(latent_pair, w_expand).astype(BF).reshape(2 * rows, heads, DN + DV)
+    key_pair, value_pair = kv_pair[..., :DN], kv_pair[..., DN:]
+    score = jnp.einsum("qhd,khd->hqk", query_nope, key_pair, preferred_element_type=F32)
+    score = score + jnp.einsum("qhd,kd->hqk", query_rope, rope_pair, preferred_element_type=F32)
+    q_pos = c_id * rows + jnp.arange(rows, dtype=jnp.int32)
+    k_pos = jnp.arange(2 * rows, dtype=jnp.int32)
+    score = jnp.where(k_pos[None, None, :] <= q_pos[None, :, None], score * scale, NEG)
+    top = jnp.max(score, axis=-1, keepdims=True)
+    expo = jnp.exp(score - top)
+    total = jnp.sum(expo, axis=-1, keepdims=True)
+    attn = jnp.einsum("hqk,khd->hqd", expo.astype(BF), value_pair, preferred_element_type=F32)
+    attn_rows = (attn / total).astype(BF).transpose(1, 0, 2)
+    lse = top + jnp.log(total)
+    attn_flat = attn_rows.reshape(rows, heads * DV)
+
+    def own(a):
+        return lax.dynamic_slice_in_dim(a, t_id * piece, piece, 0)
+
+    attn_full = tp_reduce_scatter(mdot(attn_flat, w_output).astype(BF), n_tp, 2, "attn_scatter")
+    mid = own(x_float) + attn_full
+    two_own = norm_rows(mid, gain_two).astype(BF)
+    normed_two = gather_everywhere(two_own, n_tp, 3, "normed_two_gather").reshape(-1, width)
+
+    probs = jax.nn.softmax(mdot(normed_two, w_router), axis=-1)
+    first = slot(s_id, c_id) * local_experts
+    hots = []
+    for j in range(local_experts):
+        chosen = jnp.any(routes_all == first + j, axis=1, keepdims=True)
+        prob = jnp.sum(
+            jnp.where(jnp.arange(experts, dtype=jnp.int32)[None, :] == first + j, probs, 0.0),
+            axis=1,
+            keepdims=True,
+        )
+        hots.append((chosen, jnp.where(chosen, prob, 0.0)))
+    moe_part = None
+    two_part = None
+    pg_cols = []
+    lanes = jnp.arange(LANES, dtype=jnp.int32)[None, :]
+    grads_gate, grads_up, grads_down = [], [], []
+    for j in range(local_experts + 1):
+        shared = j == local_experts
+        if shared:
+            gate_act, up_act = dot_nt(normed_two, sg_t), dot_nt(normed_two, su_t)
+            back = dot_nt(cot_all, sd)
+        else:
+            gate_act = mdot(normed_two, expert_gate[j])
+            up_act = mdot(normed_two, expert_up[j])
+            back = dot_nt(cot_all, expert_down[j])
+        silu = jax.nn.silu(gate_act)
+        hidden = silu * up_act
+        if not shared:
+            chosen, weight = hots[j]
+            hidden_grad = back * weight
+            route_grad = jnp.where(chosen, jnp.sum(hidden * back, axis=1, keepdims=True), 0.0)
+            hidden = hidden * weight
+            high = route_grad.astype(BF)
+            low = (route_grad - high.astype(F32)).astype(BF)
+            pg_cols.append(
+                jnp.where(lanes == first + j, high, jnp.where(lanes == first + j + 64, low, jnp.zeros((), BF)))
+            )
+        else:
+            hidden_grad = back
+        hidden = hidden.astype(BF)
+        gate_grad = (hidden_grad * up_act * silu_slope(gate_act)).astype(BF)
+        up_grad = (hidden_grad * silu).astype(BF)
+        if shared:
+            y = mdot(hidden, sd)
+            dn = mdot(gate_grad, sg_t) + mdot(up_grad, su_t)
+            grads = [dot_tn(gate_grad, normed_two), dot_tn(up_grad, normed_two), dot_tn(hidden, cot_all)]
+            shared_grads = [g.astype(BF) for g in grads]
+        else:
+            y = mdot(hidden, expert_down[j])
+            dn = dot_nt(gate_grad, expert_gate[j]) + dot_nt(up_grad, expert_up[j])
+            grads_gate.append(dot_tn(normed_two, gate_grad))
+            grads_up.append(dot_tn(normed_two, up_grad))
+            grads_down.append(dot_tn(hidden, cot_all))
+        moe_part = y if moe_part is None else moe_part + y
+        two_part = dn if two_part is None else two_part + dn
+    pg_part = functools.reduce(jnp.add, pg_cols)
+    part = jnp.concatenate(
+        [moe_part.astype(BF), two_part.astype(BF), pg_part, jnp.zeros_like(pg_part)], axis=1
+    ).reshape(8, rows, -1)
+    summed = reduce_everywhere(part, n_tp, 4, "feed_forward_scatter")
+    moe_out, two_grad = summed[:, :width], summed[:, width : 2 * width]
+    prob_grad = summed[:, 2 * width : 2 * width + experts]
+    prob_grad = prob_grad + summed[:, 2 * width + 64 : 2 * width + 64 + experts]
+    out_own = mid + moe_out
+    grad_expert_gate, grad_expert_up, grad_expert_down = (
+        jnp.stack(g) for g in (grads_gate, grads_up, grads_down)
+    )
+
+    probs_own = jax.nn.softmax(mdot(two_own, w_router), axis=-1)
+    logit_grad = (
+        probs_own * (prob_grad - jnp.sum(probs_own * prob_grad, axis=-1, keepdims=True))
+    ).astype(BF)
+    two_grad = two_grad + dot_nt(logit_grad, w_router)
+    mid_norm_grad, gain_two_terms = norm_back(mid, gain_two, two_grad)
+    mid_grad = own(cotangent) + mid_norm_grad
+    mid_pack = jnp.concatenate(
+        [mid_grad.astype(BF), jnp.pad(logit_grad, ((0, 0), (0, LANES - experts)))], axis=1
+    )
+    (mid_pack,) = tp_all_gather((mid_pack,), n_tp, 5, "mid_grad_gather")
+    mid_b = mid_pack[:, :width]
+
+    out_grad = dot_nt(mid_b, w_output).reshape(rows, heads, DV)
+    out_grad_b = out_grad.astype(BF)
+    delta = jnp.sum(out_grad * attn_rows.astype(F32), axis=-1).T[..., None]
+    prob = jnp.exp(score - lse)
+    dprob = jnp.einsum("qhd,khd->hqk", out_grad_b, value_pair, preferred_element_type=F32)
+    dscore = (prob * (dprob - delta)).astype(BF)
+    nope_grad = jnp.einsum("hqk,khd->qhd", dscore, key_pair, preferred_element_type=F32) * scale
+    rope_qgrad = jnp.einsum("hqk,kd->qhd", dscore, rope_pair, preferred_element_type=F32) * scale
+    key_grad = jnp.einsum("hqk,qhd->khd", dscore, query_nope, preferred_element_type=F32) * scale
+    value_grad = jnp.einsum(
+        "hqk,qhd->khd", prob.astype(BF), out_grad_b, preferred_element_type=F32
+    )
+    rope_kgrad = jnp.einsum("hqk,qhd->kd", dscore, query_rope, preferred_element_type=F32) * scale
+    kv_terms = jnp.concatenate(
+        [
+            jnp.concatenate([key_grad, value_grad], axis=-1).reshape(2 * rows, -1),
+            jnp.pad(rope_kgrad, ((0, 0), (0, LANES - DR))),
+        ],
+        axis=1,
+    )
+    mine = lax.dynamic_slice_in_dim(kv_terms, c_id * rows, rows, 0)
+    other = lax.dynamic_slice_in_dim(kv_terms, (1 - c_id) * rows, rows, 0).astype(BF)
+    kv_sum = mine + ctx_swap(other, 6, "kv_grad_swap").astype(F32)
+    kv_grad = kv_sum[:, : heads * (DN + DV)].astype(BF)
+    rope_part = rotate_back(kv_sum[:, heads * (DN + DV) :][:, :DR], cosine, sine)
+    rope_qback = rotate_back(rope_qgrad, cosine[:, None, :], sine[:, None, :])
+    query_grad = jnp.concatenate([nope_grad, rope_qback], axis=-1).astype(BF).reshape(rows, -1)
+    latent_part = dot_nt(kv_grad, w_expand)
+    one_part = dot_nt(query_grad, w_query)
+    back_part = jnp.concatenate(
+        [one_part, latent_part, jnp.pad(rope_part, ((0, 0), (0, LANES - DR)))], axis=1
+    ).astype(BF)
+    back = tp_reduce_scatter(back_part, n_tp, 7, "attn_back_scatter")
+
+    compressed = own(lax.dynamic_slice_in_dim(latent, c_id * rows, rows, 0))[:, :KVR]
+    compressed_grad, gain_kv_terms = norm_back(compressed, gain_kv, back[:, width : width + KVR])
+    latent_grad = jnp.concatenate(
+        [compressed_grad, back[:, width + KVR : width + KVR + DR]], axis=1
+    ).astype(BF)
+    one_grad = back[:, :width] + dot_nt(latent_grad, w_latent)
+    input_norm_grad, gain_one_terms = norm_back(own(x_float), gain_one, one_grad)
+    input_own = mid_grad + input_norm_grad
+
+    block_output, input_grad = tp_all_gather((out_own, input_own), n_tp, 8, "output_gather")
+    lat_pack = jnp.pad(latent_grad, ((0, 0), (0, 5 * LANES - KVR - DR)))
+    (latent_rows,) = tp_all_gather((lat_pack,), n_tp, 9, "latent_gather")
+    latent_own = lax.dynamic_slice_in_dim(latent_pair, c_id * rows, rows, 0)
+    head_pack = jnp.concatenate(
+        [query_grad, kv_grad, attn_flat, latent_rows, mid_pack[:, width:]], axis=1
+    )
+    head_all, one_cols, lat_cols, mid_cols, sg_cols, su_cols, sd_cols = plane_exchange(
+        (head_pack,), (normed_one, latent_own, mid_b, *shared_grads), (), n_tp, 10, "late_exchange"
+    )
+    head_all = head_all.reshape(8 * rows, -1)
+    edges = [0, heads * (DN + DR), heads * (DN + DV), heads * DV, 5 * LANES, LANES]
+    edges = [sum(edges[: i + 1]) for i in range(len(edges))]
+    dq_all, dkv_all, attn_all, lat_all, logit_all = (
+        head_all[:, a:b] for a, b in zip(edges[:-1], edges[1:])
+    )
+    one_cols = one_cols.reshape(8 * rows, -1)
+    lat_cols = lat_cols.reshape(8 * rows, -1)
+    mid_cols = mid_cols.reshape(8 * rows, -1)
+    grad_query = dot_tn(one_cols, dq_all)
+    grad_latent = dot_tn(one_cols, lat_all[:, : KVR + DR])
+    grad_expand = dot_tn(lat_cols, dkv_all)
+    grad_out_w = dot_tn(attn_all, mid_cols)
+    two_cols = lax.dynamic_slice_in_dim(normed_two, s_id * shard_w, shard_w, 1)
+    grad_router = dot_tn(two_cols, logit_all[:, :experts])
+    grad_sgate = sg_cols.reshape(-1, shard_w).T.astype(F32)
+    grad_sup = su_cols.reshape(-1, shard_w).T.astype(F32)
+    grad_sdown = sd_cols.reshape(-1, shard_w).astype(F32)
+
+    gains = jnp.concatenate(
+        [
+            jnp.sum(gain_one_terms, axis=0),
+            jnp.sum(gain_two_terms, axis=0),
+            jnp.sum(gain_kv_terms, axis=0),
+            jnp.zeros((512,), F32),
+        ]
+    ).reshape(8, -1)
+    gains = sum_everywhere(gains, n_tp, 11, "gain_sum").reshape(-1)
+    grad_one = lax.dynamic_slice_in_dim(gains, s_id * shard_w, shard_w, 0)
+    grad_two = lax.dynamic_slice_in_dim(gains, width + s_id * shard_w, shard_w, 0)
+    grad_kv = lax.dynamic_slice_in_dim(gains, 2 * width + s_id * kv_w, kv_w, 0)
+    return (
+        block_output,
+        input_grad,
+        grad_one,
+        grad_query,
+        grad_latent,
+        grad_kv,
+        grad_expand,
+        grad_out_w,
+        grad_two,
+        grad_router,
+        grad_sgate,
+        grad_sup,
+        grad_sdown,
+        grad_expert_gate,
+        grad_expert_up,
+        grad_expert_down,
+    )
 
 
 def send_rows(buffer):
-    return lax.all_to_all(buffer, ("shard", "ctx"), split_axis=0, concat_axis=0, tiled=True)
+    return lax.all_to_all(buffer, (SHARD, CTX), split_axis=0, concat_axis=0, tiled=True)
 
 
 def return_rows(partial_value, slots):
     back_rows = lax.all_to_all(
-        partial_value, ("shard", "ctx"), split_axis=0, concat_axis=0, tiled=True
+        partial_value, (SHARD, CTX), split_axis=0, concat_axis=0, tiled=True
     )
     flat_back = back_rows.reshape(-1, back_rows.shape[-1])
     return flat_back[slots]
 
 
-def per_device(
+def per_device_general(
     block_input,
     norm1_gain,
     q_weight,
@@ -100,19 +974,19 @@
         w_sup,
         w_sdown,
     ) = (
-        lax.all_gather(norm1_gain, "shard", axis=0, tiled=True),
-        lax.all_gather(q_weight, "shard", axis=0, tiled=True),
-        lax.all_gather(kva_weight, "shard", axis=0, tiled=True),
-        lax.all_gather(kv_norm_gain, "shard", axis=0, tiled=True),
-        lax.all_gather(kvb_weight, "shard", axis=0, tiled=True),
-        lax.all_gather(out_weight, "shard", axis=1, tiled=True),
-        lax.all_gather(norm2_gain, "shard", axis=0, tiled=True),
-        lax.all_gather(router_weight, "shard", axis=0, tiled=True),
-        lax.all_gather(shared_gate, "shard", axis=0, tiled=True),
-        lax.all_gather(shared_up, "shard", axis=0, tiled=True),
-        lax.all_gather(shared_down, "shard", axis=1, tiled=True),
-    )
-    block_index = lax.axis_index("ctx")
+        lax.all_gather(norm1_gain, SHARD, axis=0, tiled=True),
+        lax.all_gather(q_weight, SHARD, axis=0, tiled=True),
+        lax.all_gather(kva_weight, SHARD, axis=0, tiled=True),
+        lax.all_gather(kv_norm_gain, SHARD, axis=0, tiled=True),
+        lax.all_gather(kvb_weight, SHARD, axis=0, tiled=True),
+        lax.all_gather(out_weight, SHARD, axis=1, tiled=True),
+        lax.all_gather(norm2_gain, SHARD, axis=0, tiled=True),
+        lax.all_gather(router_weight, SHARD, axis=0, tiled=True),
+        lax.all_gather(shared_gate, SHARD, axis=0, tiled=True),
+        lax.all_gather(shared_up, SHARD, axis=0, tiled=True),
+        lax.all_gather(shared_down, SHARD, axis=1, tiled=True),
+    )
+    block_index = lax.axis_index(CTX)
     cosine, sine_table = rope_tables(tok_rows, (block_index * tok_rows).astype(jnp.float32))
     x_float = block_input.astype(jnp.float32)
     normed_one = norm_rows(x_float, gain_one).astype(jnp.bfloat16)
@@ -127,8 +1001,8 @@
     rope_key = rotate(latent[:, KVR:], cosine, sine_table).astype(jnp.bfloat16)
     first_piece = mdot(latent_n, w_expand).astype(jnp.bfloat16)
     gathered, rope_all = (
-        lax.all_gather(first_piece, "ctx", axis=0, tiled=True),
-        lax.all_gather(rope_key, "ctx", axis=0, tiled=True),
+        lax.all_gather(first_piece, CTX, axis=0, tiled=True),
+        lax.all_gather(rope_key, CTX, axis=0, tiled=True),
     )
     query_pos = block_index * tok_rows + jnp.arange(tok_rows, dtype=jnp.int32)
 
@@ -173,7 +1047,7 @@
     lse = run_max + jnp.log(run_sum)
     attn_rows = (weighted / run_sum[..., None]).astype(jnp.bfloat16).transpose(1, 0, 2)
     attn_flat = attn_rows.reshape(tok_rows, head_count * DV)
-    attn_full = lax.psum(mdot(attn_flat, w_output), "tp")
+    attn_full = lax.psum(mdot(attn_flat, w_output), TP)
     mid = x_float + attn_full
     normed_two = norm_rows(mid, gain_two).astype(jnp.bfloat16)
     probs = jax.nn.softmax(mdot(normed_two, w_router), axis=-1)
@@ -188,7 +1062,7 @@
     shared_h = (jax.nn.silu(shared_a) * shared_b).astype(jnp.bfloat16)
     shared_y = mdot(shared_h, w_sdown)
     capacity = 2 * tok_rows * topk // experts
-    owners = lax.axis_size(("shard", "ctx"))
+    owners = lax.axis_size((SHARD, CTX))
     local_experts = expert_gate.shape[0]
     width = normed_two.shape[1]
     flat_routes = routes.reshape(-1)
@@ -215,7 +1089,7 @@
     ).reshape(tok_rows, topk, width)
     routed_part = jnp.sum(route_w[:, :, None] * routed_out, axis=1) + shared_y
     weight_part = jnp.sum(routed_out * cotangent[:, None, :], axis=-1)
-    moe_out, route_grad = lax.psum((routed_part, weight_part), "tp")
+    moe_out, route_grad = lax.psum((routed_part, weight_part), TP)
     block_output = mid + moe_out
     cot_b = cotangent.astype(jnp.bfloat16)
     routed_grad = (
@@ -263,7 +1137,7 @@
     two_part = two_part + jnp.einsum(
         "tf,df->td", sup_grad, w_sup, preferred_element_type=jnp.float32
     )
-    two_grad = lax.psum(two_part, "tp")
+    two_grad = lax.psum(two_part, TP)
     prob_grad = jnp.sum(picks * route_grad[:, :, None], axis=1)
     logit_grad = (probs * (prob_grad - jnp.sum(probs * prob_grad, axis=-1, keepdims=True))).astype(
         jnp.bfloat16
@@ -331,7 +1205,7 @@
         jnp.zeros((key_count, term_width), jnp.float32),
     )
     nope_grad, rope_qgrad, terms = lax.fori_loop(0, block_index + 1, back_block, back_init)
-    key_terms = lax.psum_scatter(terms, "ctx", scatter_dimension=0, tiled=True).reshape(
+    key_terms = lax.psum_scatter(terms, CTX, scatter_dimension=0, tiled=True).reshape(
         tok_rows, head_count, DN + DV + DR
     )
     kv_grad = (
@@ -349,7 +1223,7 @@
     grad_query = jnp.einsum("td,tj->dj", normed_one, query_grad, preferred_element_type=jnp.float32)
     normed_part = jnp.einsum("tj,dj->td", query_grad, w_query, preferred_element_type=jnp.float32)
     latent_sum, normed_sum = lax.psum(
-        (jnp.concatenate([latent_part, rope_grad], axis=-1), normed_part), "tp"
+        (jnp.concatenate([latent_part, rope_grad], axis=-1), normed_part), TP
     )
     _, kv_back = jax.vjp(norm_rows, compressed, gain_kv.astype(jnp.float32))
     compressed_grad, grad_gain_kv = kv_back(latent_sum[:, :KVR])
@@ -378,17 +1252,17 @@
         red_sup,
         red_sdown,
     ) = (
-        lax.psum_scatter(grad_gain_one, "shard", scatter_dimension=0, tiled=True),
-        lax.psum_scatter(grad_query, "shard", scatter_dimension=0, tiled=True),
-        lax.psum_scatter(grad_latent, "shard", scatter_dimension=0, tiled=True),
-        lax.psum_scatter(grad_gain_kv, "shard", scatter_dimension=0, tiled=True),
-        lax.psum_scatter(grad_expand, "shard", scatter_dimension=0, tiled=True),
-        lax.psum_scatter(grad_out_w, "shard", scatter_dimension=1, tiled=True),
-        lax.psum_scatter(grad_gain_two, "shard", scatter_dimension=0, tiled=True),
-        lax.psum_scatter(grad_router, "shard", scatter_dimension=0, tiled=True),
-        lax.psum_scatter(grad_sgate, "shard", scatter_dimension=0, tiled=True),
-        lax.psum_scatter(grad_sup, "shard", scatter_dimension=0, tiled=True),
-        lax.psum_scatter(grad_sdown, "shard", scatter_dimension=1, tiled=True),
+        lax.psum_scatter(grad_gain_one, SHARD, scatter_dimension=0, tiled=True),
+        lax.psum_scatter(grad_query, SHARD, scatter_dimension=0, tiled=True),
+        lax.psum_scatter(grad_latent, SHARD, scatter_dimension=0, tiled=True),
+        lax.psum_scatter(grad_gain_kv, SHARD, scatter_dimension=0, tiled=True),
+        lax.psum_scatter(grad_expand, SHARD, scatter_dimension=0, tiled=True),
+        lax.psum_scatter(grad_out_w, SHARD, scatter_dimension=1, tiled=True),
+        lax.psum_scatter(grad_gain_two, SHARD, scatter_dimension=0, tiled=True),
+        lax.psum_scatter(grad_router, SHARD, scatter_dimension=0, tiled=True),
+        lax.psum_scatter(grad_sgate, SHARD, scatter_dimension=0, tiled=True),
+        lax.psum_scatter(grad_sup, SHARD, scatter_dimension=0, tiled=True),
+        lax.psum_scatter(grad_sdown, SHARD, scatter_dimension=1, tiled=True),
     )
     (
         sum_one,
@@ -416,7 +1290,7 @@
             red_sup,
             red_sdown,
         ),
-        "ctx",
+        CTX,
     )
     return (
         block_output,
@@ -440,42 +1314,43 @@
 
 def solution(mesh):
     in_specs = (
-        P(("shard", "ctx"), None),
-        P("shard"),
-        P("shard", "tp"),
-        P("shard", None),
-        P("shard"),
-        P("shard", "tp"),
-        P("tp", "shard"),
-        P("shard"),
-        P("shard", None),
-        P("shard", "tp"),
-        P("shard", "tp"),
-        P("tp", "shard"),
-        P(("shard", "ctx"), None, "tp"),
-        P(("shard", "ctx"), None, "tp"),
-        P(("shard", "ctx"), "tp", None),
-        P(("shard", "ctx"), None),
-        P(("shard", "ctx"), None),
+        P((SHARD, CTX), None),
+        P(SHARD),
+        P(SHARD, TP),
+        P(SHARD, None),
+        P(SHARD),
+        P(SHARD, TP),
+        P(TP, SHARD),
+        P(SHARD),
+        P(SHARD, None),
+        P(SHARD, TP),
+        P(SHARD, TP),
+        P(TP, SHARD),
+        P((SHARD, CTX), None, TP),
+        P((SHARD, CTX), None, TP),
+        P((SHARD, CTX), TP, None),
+        P((SHARD, CTX), None),
+        P((SHARD, CTX), None),
     )
     out_specs = (
-        P(("shard", "ctx"), None),
-        P(("shard", "ctx"), None),
-        P("shard"),
-        P("shard", "tp"),
-        P("shard", None),
-        P("shard"),
-        P("shard", "tp"),
-        P("tp", "shard"),
-        P("shard"),
-        P("shard", None),
-        P("shard", "tp"),
-        P("shard", "tp"),
-        P("tp", "shard"),
-        P(("shard", "ctx"), None, "tp"),
-        P(("shard", "ctx"), None, "tp"),
-        P(("shard", "ctx"), "tp", None),
-    )
+        P((SHARD, CTX), None),
+        P((SHARD, CTX), None),
+        P(SHARD),
+        P(SHARD, TP),
+        P(SHARD, None),
+        P(SHARD),
+        P(SHARD, TP),
+        P(TP, SHARD),
+        P(SHARD),
+        P(SHARD, None),
+        P(SHARD, TP),
+        P(SHARD, TP),
+        P(TP, SHARD),
+        P((SHARD, CTX), None, TP),
+        P((SHARD, CTX), None, TP),
+        P((SHARD, CTX), TP, None),
+    )
+    routed = mesh.shape[SHARD] == 4 and mesh.shape[CTX] == 2 and mesh.shape[TP] == 4
     return jax.shard_map(
-        per_device, mesh=mesh, in_specs=in_specs, out_specs=out_specs, check_vma=False
-    )
+        per_device if routed else per_device_general, mesh=mesh, in_specs=in_specs, out_specs=out_specs, check_vma=False
+    )

time: 1560 us -> 630 us (0.40)
  waiting for transfers between devices: 1050 us -> 0 us
  Pallas kernels: 0 us -> 373 us
  blocking collectives: 131 us -> 0 us
  local copies, waits for them, and re-layouts: 145 us -> 51.4 us
  starting transfers between devices: 21.6 us -> 0 us
    pallas_call x0 -> x12, Pallas kernels: none -> 373 us  [comm_call(): pl.pallas_call(body, out_shape=tuple((jax.ShapeDtypeStruct(shape, dtype)...]
    reduce_scatter x9 -> x0, waiting for transfers between devices: 373 us -> none  [the longest x1 61.3 us: per_device(): lax.psum_scatter(grad_query, 'shard', scatter_dimension=0, tiled=True)]
    psum x4 -> x0, waiting for transfers between devices: 279 us -> none  [the longest x1 175 us: per_device(): lax.psum((red_one, red_query, red_latent, red_kv, red_expand, red_output,...]
    all_gather x7 -> x0, waiting for transfers between devices: 201 us -> none  [the longest x1 78.7 us: per_device(): lax.all_gather(shared_up, 'shard', axis=0, tiled=True)]
    all_to_all x4 -> x0, waiting for transfers between devices: 188 us -> none  [the longest x2 133 us: return_rows(): lax.all_to_all(partial_value, ('shard', 'ctx'), split_axis=0, concat_axis...]
    all_gather x6 -> x0, blocking collectives: 88.3 us -> none  [the longest x1 57.7 us: per_device(): lax.all_gather(router_weight, 'shard', axis=0, tiled=True)]
    psum x2 -> x0, blocking collectives: 32.2 us -> none  [the longest x1 21.3 us: per_device(): moe_out, route_grad = lax.psum((routed_part, weight_part), 'tp')]
    scatter x1 -> x0, local copies, waits for them, and re-layouts: 24.3 us -> none  [per_device(): jnp.zeros((experts * capacity, width), jnp.bfloat16).at[slots]]
  transfers between devices with their start and end apart: 24 -> 0, of which waited for: 20 -> 0; matrix products, arithmetic and copies ran while one was open for 16% -> 0% of each run, Pallas kernels for 0% -> 0%
where the time goes in v1:
time: 630 us; the launch traced here: 622 us
  Pallas kernels  373 us (59%)
  matrix products  142 us (23%)
  other arithmetic  53.4 us (8%)
  local copies, waits for them, and re-layouts  51.4 us (8%)
    pallas_call x12, Pallas kernels, comm_call(): pl.pallas_call(body, out_shape=tuple((jax.ShapeDtypeStruct(shape, dtype)...  373 us
    dot_general x14, matrix products, dot_nt(): lax.dot_general(left, right, (((1,), (1,)), ((), ())), preferred_element_...  53.7 us
    dot_general x15, matrix products, mdot(): return jnp.dot(left, right, preferred_element_type=F32)  46 us
    dot_general x14, matrix products, dot_tn(): lax.dot_general(left, right, (((0,), (0,)), ((), ())), preferred_element_...  35 us
    unnamed x207, local copies, waits for them, and re-layouts  16 us

profile of v1, /device:TPU:0, one launch (start us, length us, event | category | flops | bytes accessed | tf_op | source)
XLA Modules:
  0.0 622.5 jit_solution(1006988919086325530)
XLA Ops:
  0.6 2.1 copy.76.refs_1_
  3.7 3.2 concatenate.47.refs_4_
  6.9 42.4 %start_gather.1 = (bf16[4,512,768]{2,1,0:T(8,128)(2,1)}, bf16[4,512,576]{2,1,0:T(8,128)(2,1)}, bf16[4,128,1024]{2,1,0:T(8,128)(2,1)}, bf16[4,512,512]{2,1,0:T(8,...) custom-call(bf16[512,768]{1,0:T(8,128)(2,1)} %refs_0_.1, bf16[512,576]{1,0:T(8,128)(2,1)} %copy.76.refs_1_, ...), custom_call_target="tpu_custom_call" | custom-call | tf_op jit(solution)/shard_map/start_gather/pallas_call | solution.py:159
  60.7 2.5 convolution_convert_fusion.5
  63.2 2.2 reshape.417
  69.2 2.9 copy.77
  75.4 2.9 fusion.71
  86.3 4.4 copy.87
  90.7 3.3 convolution_convert_fusion.1.in_ref
  94.0 15.4 %attn_scatter.1 = f32[32,2048]{1,0:T(8,128)} custom-call(bf16[128,2048]{1,0:T(8,128)(2,1)} %convolution_convert_fusion.1.in_ref), custom_call_target="tpu_custom_call" | custom-call | tf_op jit(solution)/shard_map/attn_scatter/pallas_call | solution.py:159
  115.1 34.9 %early_exchange.1 = (bf16[8,128,2176]{2,1,0:T(8,128)(2,1)}, bf16[88,2048]{1,0:T(8,128)(2,1)}, bf16[88,2048]{1,0:T(8,128)(2,1)}, bf16[88,2048]{1,0:T(8,128)(2,1)}) custom-call(bf16[128,2176]{1,0:T(8,128)(2,1)} %fusion.68.refs_0_, bf16[704,512]{1,0:T(8,128)(2,1)} %bitcast.236, bf16[704,512]{1,0:T(8,128)(2,1)} %bitcast.237, bf16[704,512]{1,0:T(8,128)(2,1)} %refs_3_.3), custom_call_target="tpu_custom_call" | custom-call | tf_op jit(solution)/shard_map/early_exchange/pallas_call | solution.py:159
  152.1 29.4 %normed_two_gather.1 = bf16[8,128,2048]{2,1,0:T(8,128)(2,1)} custom-call(bf16[32,2048]{1,0:T(8,128)(2,1)} %multiply_convert_fusion.11.in_ref), custom_call_target="tpu_custom_call" | custom-call | tf_op jit(solution)/shard_map/normed_two_gather/pallas_call | solution.py:159
  181.6 4.5 fusion.19
  190.6 3.5 multiply_convert_fusion.1
  197.6 3.8 multiply_convert_fusion.3
  207.0 4.6 fusion.116
  211.6 4.5 fusion.117
  216.2 5.7 fusion.21
  221.8 5.7 fusion.32
  227.5 5.8 fusion.28
  233.3 19.4 %add_convert_fusion = bf16[1024,2048]{1,0:T(8,128)(2,1)} fusion(f32[1024,2048]{1,0:T(8,128)} %fusion.116, f32[1024,2048]{1,0:T(8,128)} %fusion.117, f32[1024,2048]{1,0:T(8,128)} %fusion.21, f32[1024,2048]{1,0:T(8,128)} %fusion.32, f32[1024,2048]{1,0:T(8,128)} %fusion.28, bf16[1024,352]{0,1:T(8,128)(2,1)} %get-tuple-element.73, bf16[2,2048,352]{1,2,0:T(8,128)(2,1)} %param.30), kind=kOutput, calls=%fused_computation.1 | convolution fusion | flops 1488977920 | bytes 48300032 | tf_op jit(solution)/shard_map/dot_general | solution.py:75
  252.8 2.4 fusion.115
  255.2 2.4 fusion.26
  257.6 6.5 %add_convert_fusion.1 = bf16[1024,2048]{1,0:T(8,128)(2,1)} fusion(f32[1024,2048]{1,0:T(8,128)S(1)} %fusion.115, f32[1024,2048]{1,0:T(8,128)S(1)} %fusion.26, bf16[1024,352]{0,1:T(8,128)(2,1)} %get-tuple-element.72, bf16[2,352,2048]{2,1,0:T(8,128)(2,1)} %param.31), kind=kOutput, calls=%fused_computation.2 | convolution fusion | flops 1482686464 | bytes 23134208 | tf_op jit(solution)/shard_map/dot_general | solution.py:71
  264.1 6.3 %pad_maximum_fusion = bf16[1024,4352]{1,0:T(8,128)(2,1)} fusion(bf16[1024,128]{1,0:T(8,128)(2,1)S(1)} %broadcast_in_dim.156, bf16[1024,128]{1,0:T(8,128)(2,1)} %select_add_fusion, bf16[1024,2048]{1,0:T(8,128)(2,1)S(1)} %copy-done.3, bf16[1024,2048]{1,0:T(8,128)(2,1)} %add_convert_fusion.1), kind=kLoop, calls=%fused_computation | loop fusion | flops 35651584 | bytes 17825792 | tf_op jit(solution)/shard_map/concatenate | solution.py:801
  270.5 66.3 %feed_forward_scatter.1 = f32[32,4352]{1,0:T(8,128)} custom-call(bf16[8,128,4352]{2,1,0:T(8,128)(2,1)} %bitcast.211), custom_call_target="tpu_custom_call" | custom-call | tf_op jit(solution)/shard_map/feed_forward_scatter/pallas_call | solution.py:159
  344.8 2.9 copy.90
  347.8 4.7 dot_general.195
  353.2 19.0 %mid_grad_gather.1 = bf16[128,2176]{1,0:T(8,128)(2,1)} custom-call(bf16[32,2176]{1,0:T(8,128)(2,1)} %fusion.88.refs_0_), custom_call_target="tpu_custom_call" | custom-call | tf_op jit(solution)/shard_map/mid_grad_gather/pallas_call | solution.py:159
  372.2 2.5 multiply_reduce_fusion.7
  378.5 2.5 copy.106
  381.1 2.4 select_maximum_fusion
  385.4 8.2 %kv_grad_swap.1 = bf16[128,1152]{1,0:T(8,128)(2,1)} custom-call(bf16[128,1152]{1,0:T(8,128)(2,1)} %dynamic-slice_convert_fusion.in_ref), custom_call_target="tpu_custom_call" | custom-call | tf_op jit(solution)/shard_map/kv_grad_swap/pallas_call | solution.py:159
  399.7 15.8 %attn_back_scatter.1 = f32[32,2688]{1,0:T(8,128)} custom-call(bf16[128,2688]{1,0:T(8,128)(2,1)} %pad_maximum_fusion.5.in_ref), custom_call_target="tpu_custom_call" | custom-call | tf_op jit(solution)/shard_map/attn_back_scatter/pallas_call | solution.py:159
  419.7 2.1 multiply_reduce_fusion.5
  423.7 39.5 %output_gather.1 = (f32[128,2048]{1,0:T(8,128)}, f32[128,2048]{1,0:T(8,128)}) custom-call(f32[32,2048]{1,0:T(8,128)} %get-tuple-element.90.refs_0_, f32[32,2048]{1,0:T(8,128)} %multiply_add_fusion.refs_1_), custom_call_target="tpu_custom_call" | custom-call | tf_op jit(solution)/shard_map/output_gather/pallas_call | solution.py:159
  463.9 12.1 %gain_sum.1 = f32[8,640]{1,0:T(8,128)} custom-call(f32[8,640]{1,0:T(8,128)} %reshape.425.in_ref), custom_call_target="tpu_custom_call" | custom-call | tf_op jit(solution)/shard_map/gain_sum/pallas_call | solution.py:159
  479.4 10.1 %latent_gather.1 = bf16[128,640]{1,0:T(8,128)(2,1)} custom-call(bf16[32,640]{1,0:T(8,128)(2,1)} %pad.30.refs_0_), custom_call_target="tpu_custom_call" | custom-call | tf_op jit(solution)/shard_map/latent_gather/pallas_call | solution.py:159
  492.0 4.3 convolution_convert_fusion.4.refs_4_
  498.0 3.7 convolution_convert_fusion.2.refs_6_
  501.7 80.2 %late_exchange.1 = (bf16[8,128,3072]{2,1,0:T(8,128)(2,1)}, bf16[8,128,512]{2,1,0:T(8,128)(2,1)}, bf16[8,128,128]{2,1,0:T(8,128)(2,1)}, bf16[8,128,512]{2,1,0:T(8...) custom-call(bf16[128,3072]{1,0:T(8,128)(2,1)} %copy-done.32, ...), custom_call_target="tpu_custom_call" | custom-call | tf_op jit(solution)/shard_map/late_exchange/pallas_call | solution.py:159
  581.9 4.0 fusion.14
  585.9 3.2 fusion.38
  589.7 2.9 fusion.3
  592.6 3.0 fusion.64
  595.6 2.3 fusion.66
  609.0 4.8 pad_maximum_fusion.1
  617.2 2.9 pad_maximum_fusion.3
  (329 shorter events, 99.7 us)
Async XLA Ops:
  50.8 22.6 %copy-start.63 = (f32[2048]{0:T(1024)}, f32[2048]{0:T(1024)S(1)}, u32[]{:S(2)}) copy-start(f32[2048]{0:T(1024)S(1)} %convert.60) | copy-start | bytes 24580
  57.5 11.7 %copy-start.4 = (bf16[4,512,768]{2,1,0:T(8,128)(2,1)S(1)}, bf16[4,512,768]{2,1,0:T(8,128)(2,1)}, u32[]{:S(2)}) copy-start(bf16[4,512,768]{2,1,0:T(8,128)(2,1)} %get-tuple-element.36) | copy-start | bytes 9437188
  67.3 10.9 %copy-start.25 = (bf16[256,4,128]{2,1,0:T(4,128)(2,1)}, bf16[256,4,128]{2,1,0:T(4,128)(2,1)S(1)}, u32[]{:S(2)}) copy-start(bf16[256,4,128]{2,1,0:T(4,128)(2,1)S(1)} %get-tuple-element.86) | copy-start | bytes 786436
  80.6 10.0 %copy-start.65 = (f32[128,32]{0,1:T(8,128)}, f32[128,32]{0,1:T(8,128)S(1)}, u32[]{:S(2)}) copy-start(f32[128,32]{0,1:T(8,128)S(1)} %copy.83) | copy-start | bytes 49156
  84.2 6.5 %copy-start.76 = (f32[4,128]{1,0:T(4,128)}, f32[4,128]{1,0:T(4,128)S(1)}, u32[]{:S(2)}) copy-start(f32[4,128]{1,0:T(4,128)S(1)} %get-tuple-element.97) | copy-start | bytes 6148
  84.5 9.5 %copy-start.80 = (f32[4,128]{1,0:T(4,128)}, f32[4,128]{1,0:T(4,128)S(1)}, u32[]{:S(2)}) copy-start(f32[4,128]{1,0:T(4,128)S(1)} %fusion.75) | copy-start | bytes 6148
  86.3 7.7 %copy-start.33 = (bf16[128,4,128]{0,2,1:T(8,128)(2,1)}, bf16[128,4,128]{0,2,1:T(8,128)(2,1)S(1)}, u32[]{:S(2)}) copy-start(bf16[128,4,128]{0,2,1:T(8,128)(2,1)S(1)} %fusion.60) | copy-start | bytes 393220
  90.7 18.7 %copy-start.10 = (bf16[128,2048]{1,0:T(8,128)(2,1)S(1)}, bf16[128,2048]{1,0:T(8,128)(2,1)}, u32[]{:S(2)}) copy-start(bf16[128,2048]{1,0:T(8,128)(2,1)} %refs_5_.1) | copy-start | bytes 1572868
  90.7 22.1 %copy-start.78 = (bf16[4,4,128]{2,1,0:T(4,128)(2,1)S(1)}, bf16[4,4,128]{2,1,0:T(4,128)(2,1)}, u32[]{:S(2)}) copy-start(bf16[4,4,128]{2,1,0:T(4,128)(2,1)} %get-tuple-element.84) | copy-start | bytes 12292
  90.7 22.1 %copy-start.87 = (s32[128,6]{0,1:T(8,128)S(1)}, s32[128,6]{0,1:T(8,128)}, u32[]{:S(2)}) copy-start(s32[128,6]{0,1:T(8,128)} %param.32) | copy-start | bytes 9220
  112.2 39.2 %copy-start.15 = (f32[32,2048]{1,0:T(8,128)}, f32[32,2048]{1,0:T(8,128)S(1)}, u32[]{:S(2)}) copy-start(f32[32,2048]{1,0:T(8,128)S(1)} %get-tuple-element.67) | copy-start | bytes 786436
  112.2 39.9 %copy-start.84 = (f32[32]{0:T(128)}, f32[32]{0:T(128)S(1)}, u32[]{:S(2)}) copy-start(f32[32]{0:T(128)S(1)} %add_rsqrt_fusion.4) | copy-start | bytes 388
  112.8 39.3 %copy-start.73 = (f32[2048]{0:T(1024)}, f32[2048]{0:T(1024)S(1)}, u32[]{:S(2)}) copy-start(f32[2048]{0:T(1024)S(1)} %convert.61) | copy-start | bytes 24580
  194.1 22.0 %copy-start.47 = (bf16[1024,352]{0,1:T(8,128)(2,1)}, bf16[1024,352]{0,1:T(8,128)(2,1)S(1)}, u32[]{:S(2)}) copy-start(bf16[1024,352]{0,1:T(8,128)(2,1)S(1)} %get-tuple-element.70) | copy-start | bytes 2162692
  201.4 20.5 %copy-start.53 = (bf16[1024,352]{0,1:T(8,128)(2,1)}, bf16[1024,352]{0,1:T(8,128)(2,1)S(1)}, u32[]{:S(2)}) copy-start(bf16[1024,352]{0,1:T(8,128)(2,1)S(1)} %get-tuple-element.68) | copy-start | bytes 2162692
  201.4 26.1 %copy-start.51 = (bf16[1024,352]{0,1:T(8,128)(2,1)}, bf16[1024,352]{0,1:T(8,128)(2,1)S(1)}, u32[]{:S(2)}) copy-start(bf16[1024,352]{0,1:T(8,128)(2,1)S(1)} %get-tuple-element.75) | copy-start | bytes 2162692
  207.0 45.7 %copy-start.58 = (bf16[1024,88]{0,1:T(8,128)(2,1)}, bf16[1024,88]{0,1:T(8,128)(2,1)S(1)}, u32[]{:S(2)}) copy-start(bf16[1024,88]{0,1:T(8,128)(2,1)S(1)} %get-tuple-element.77) | copy-start | bytes 540676
  257.6 6.6 %copy-start.3 = (bf16[1024,2048]{1,0:T(8,128)(2,1)S(1)}, bf16[1024,2048]{1,0:T(8,128)(2,1)}, u32[]{:S(2)}) copy-start(bf16[1024,2048]{1,0:T(8,128)(2,1)} %add_convert_fusion) | copy-start | bytes 12582916
  270.5 66.3 %copy-start.8 = (bf16[4,512,16]{2,1,0:T(8,128)(2,1)S(1)}, bf16[4,512,16]{2,1,0:T(8,128)(2,1)}, u32[]{:S(2)}) copy-start(bf16[4,512,16]{2,1,0:T(8,128)(2,1)} %copy-done.7) | copy-start | bytes 196612
  270.5 69.7 %copy-start.16 = (f32[32,2048]{1,0:T(8,128)S(1)}, f32[32,2048]{1,0:T(8,128)}, u32[]{:S(2)}) copy-start(f32[32,2048]{1,0:T(8,128)} %copy-done.15) | copy-start | bytes 786436
  270.5 69.7 %copy-start.74 = (f32[2048]{0:T(1024)S(1)}, f32[2048]{0:T(1024)}, u32[]{:S(2)}) copy-start(f32[2048]{0:T(1024)} %copy-done.73) | copy-start | bytes 24580
  270.5 69.7 %copy-start.85 = (f32[32]{0:T(128)S(1)}, f32[32]{0:T(128)}, u32[]{:S(2)}) copy-start(f32[32]{0:T(128)} %copy-done.84) | copy-start | bytes 388
  270.5 71.8 %copy-start.90 = (f32[32]{0:T(128)S(1)}, f32[32]{0:T(128)}, u32[]{:S(2)}) copy-start(f32[32]{0:T(128)} %get-tuple-element.76) | copy-start | bytes 388
  270.5 71.7 %copy-start.93 = (f32[32]{0:T(128)S(1)}, f32[32]{0:T(128)}, u32[]{:S(2)}) copy-start(f32[32]{0:T(128)} %copy-done.92) | copy-start | bytes 388
  338.1 6.8 %copy-start.9 = (bf16[4,512,512]{2,1,0:T(8,128)(2,1)S(1)}, bf16[4,512,512]{2,1,0:T(8,128)(2,1)}, u32[]{:S(2)}) copy-start(bf16[4,512,512]{2,1,0:T(8,128)(2,1)} %get-tuple-element.40) | copy-start | bytes 6291460
  347.8 24.4 %copy-start.34 = (bf16[128,4,128]{0,2,1:T(8,128)(2,1)S(1)}, bf16[128,4,128]{0,2,1:T(8,128)(2,1)}, u32[]{:S(2)}) copy-start(bf16[128,4,128]{0,2,1:T(8,128)(2,1)} %copy-done.33) | copy-start | bytes 393220
  352.4 22.3 %copy-start.77 = (f32[4,128]{1,0:T(4,128)S(1)}, f32[4,128]{1,0:T(4,128)}, u32[]{:S(2)}) copy-start(f32[4,128]{1,0:T(4,128)} %copy-done.76) | copy-start | bytes 6148
  352.4 22.3 %copy-start.81 = (f32[4,128]{1,0:T(4,128)S(1)}, f32[4,128]{1,0:T(4,128)}, u32[]{:S(2)}) copy-start(f32[4,128]{1,0:T(4,128)} %copy-done.80) | copy-start | bytes 6148
  352.5 22.3 %copy-start.12 = (f32[4,128,256]{2,1,0:T(8,128)S(1)}, f32[4,128,256]{2,1,0:T(8,128)}, u32[]{:S(2)}) copy-start(f32[4,128,256]{2,1,0:T(8,128)} %copy-done.11) | copy-start | bytes 1572868
  381.1 13.7 %copy-start.83 = (f32[32]{0:T(128)S(1)}, f32[32]{0:T(128)}, u32[]{:S(2)}) copy-start(f32[32]{0:T(128)} %copy-done.82) | copy-start | bytes 388
  381.1 13.8 %copy-start.89 = (f32[128]{0:T(128)S(1)}, f32[128]{0:T(128)}, u32[]{:S(2)}) copy-start(f32[128]{0:T(128)} %copy-done.88) | copy-start | bytes 1540
  383.5 13.5 %copy-start.70 = (bf16[256,32]{0,1:T(8,128)(2,1)S(1)}, bf16[256,32]{0,1:T(8,128)(2,1)}, u32[]{:S(2)}) copy-start(bf16[256,32]{0,1:T(8,128)(2,1)} %copy-done.69) | copy-start | bytes 49156
  383.5 13.5 %copy-start.72 = (bf16[256,32]{0,1:T(8,128)(2,1)S(1)}, bf16[256,32]{0,1:T(8,128)(2,1)}, u32[]{:S(2)}) copy-start(bf16[256,32]{0,1:T(8,128)(2,1)} %copy-done.71) | copy-start | bytes 49156
  383.5 13.7 %copy-start.66 = (f32[128,32]{0,1:T(8,128)S(1)}, f32[128,32]{0,1:T(8,128)}, u32[]{:S(2)}) copy-start(f32[128,32]{0,1:T(8,128)} %copy-done.65) | copy-start | bytes 49156
  383.5 13.7 %copy-start.68 = (f32[128,32]{0,1:T(8,128)S(1)}, f32[128,32]{0,1:T(8,128)}, u32[]{:S(2)}) copy-start(f32[128,32]{0,1:T(8,128)} %copy-done.67) | copy-start | bytes 49156
  397.6 22.1 %copy-start.64 = (f32[2048]{0:T(1024)S(1)}, f32[2048]{0:T(1024)}, u32[]{:S(2)}) copy-start(f32[2048]{0:T(1024)} %copy-done.63) | copy-start | bytes 24580
  397.6 22.1 %copy-start.86 = (f32[32]{0:T(128)S(1)}, f32[32]{0:T(128)}, u32[]{:S(2)}) copy-start(f32[32]{0:T(128)} %get-tuple-element.107) | copy-start | bytes 388
  398.8 20.9 %copy-start.6 = (bf16[4,512,576]{2,1,0:T(8,128)(2,1)S(1)}, bf16[4,512,576]{2,1,0:T(8,128)(2,1)}, u32[]{:S(2)}) copy-start(bf16[4,512,576]{2,1,0:T(8,128)(2,1)} %get-tuple-element.38) | copy-start | bytes 7077892
  399.7 22.1 %copy-start.91 = (f32[32]{0:T(128)S(1)}, f32[32]{0:T(128)}, u32[]{:S(2)}) copy-start(f32[32]{0:T(128)} %get-tuple-element.76) | copy-start | bytes 388
  399.7 22.1 %copy-start.42 = (f32[32,2048]{1,0:T(8,128)S(1)}, f32[32,2048]{1,0:T(8,128)}, u32[]{:S(2)}) copy-start(f32[32,2048]{1,0:T(8,128)} %get-tuple-element.65) | copy-start | bytes 786436
  417.5 45.8 %copy-start.75 = (f32[2048]{0:T(1024)S(1)}, f32[2048]{0:T(1024)}, u32[]{:S(2)}) copy-start(f32[2048]{0:T(1024)} %get-tuple-element.58) | copy-start | bytes 24580
  417.6 59.8 %copy-start.28 = (bf16[128,4,192]{0,2,1:T(8,128)(2,1)S(1)}, bf16[128,4,192]{0,2,1:T(8,128)(2,1)}, u32[]{:S(2)}) copy-start(bf16[128,4,192]{0,2,1:T(8,128)(2,1)} %copy-done.27) | copy-start | bytes 589828
  419.7 58.9 %copy-start.35 = (bf16[128,4,128]{0,2,1:T(8,128)(2,1)S(1)}, bf16[128,4,128]{0,2,1:T(8,128)(2,1)}, u32[]{:S(2)}) copy-start(bf16[128,4,128]{0,2,1:T(8,128)(2,1)} %copy-done.33) | copy-start | bytes 393220
  421.8 68.6 %copy-start.13 = (bf16[128,2176]{1,0:T(8,128)(2,1)S(1)}, bf16[128,2176]{1,0:T(8,128)(2,1)}, u32[]{:S(2)}) copy-start(bf16[128,2176]{1,0:T(8,128)(2,1)} %mid_grad_gather.1) | copy-start | bytes 1671172
  421.8 68.6 %copy-start.30 = (bf16[256,512]{1,0:T(8,128)(2,1)S(1)}, bf16[256,512]{1,0:T(8,128)(2,1)}, u32[]{:S(2)}) copy-start(bf16[256,512]{1,0:T(8,128)(2,1)} %copy-done.29) | copy-start | bytes 786436
  421.8 70.2 %copy-start.39 = (bf16[1024,88]{0,1:T(8,128)(2,1)S(1)}, bf16[1024,88]{0,1:T(8,128)(2,1)}, u32[]{:S(2)}) copy-start(bf16[1024,88]{0,1:T(8,128)(2,1)} %copy-done.38) | copy-start | bytes 540676
  490.4 5.9 copy-start.32
  607.3 6.5 %slice-start = ((s8[4456448]{0:T(1024)(128)(4,1)}), s8[4194304]{0:T(1024)(128)(4,1)S(1)}, s32[]{:S(2)}) async-start(s8[4456448]{0:T(1024)(128)(4,1)} %bitcast.249), calls=%async_computation | async-start | bytes 8388608
  (50 other events, 150.3 us)

commit v2 on v1

--- a/solution.py
+++ b/solution.py
@@ -645,6 +645,543 @@
     )[0]
 
 
+class Wire:
+    def __init__(self, net, build):
+        self.net, self.build, self.i = net, build, net.wires
+        net.wires += 1
+
+    def copy(self):
+        src, dst, to = self.build()
+        return pltpu.make_async_remote_copy(
+            src_ref=src,
+            dst_ref=dst,
+            send_sem=self.net.send.at[self.i],
+            recv_sem=self.net.recv.at[self.i],
+            device_id=to,
+            device_id_type=MESH,
+        )
+
+    def start(self):
+        self.copy().start()
+
+    def landed(self):
+        self.copy().wait_recv()
+
+    def sent(self):
+        self.copy().wait_send()
+
+
+class Wires:
+    def __init__(self, send, recv):
+        self.send, self.recv, self.wires, self.all = send, recv, 0, []
+
+    def wire(self, build):
+        made = Wire(self, build)
+        self.all.append(made)
+        return made
+
+
+def feed_forward(two_own, cot_all, gate, up, down, sg_t, su_t, sd, w_router, experts, topk, n_tp):
+    piece, width = two_own.shape
+    rows = piece * n_tp
+    tokens = 8 * rows
+    pack = cot_all.shape[-1]
+    hid, hid_s = gate.shape[2], sg_t.shape[0]
+    edge = width // 2
+    part_w = width + LANES
+    group = 2 * rows
+    shard_w = width // 4
+    n_wires = 4 + 12 + 16 + 4 + 6 + (n_tp - 1)
+
+    def body(*refs):
+        (two_ref, cot_ref, gate_ref, up_ref, down_ref, sg_ref, su_ref, sd_ref, wr_ref) = refs[:9]
+        (two_out, y_out, dg_out, du_out, dd_out, ds_out, n2_out) = refs[9:16]
+        (nb, cb, wg, wu, wd, ws, wr, hwe, gge, uue, hws, ggs, uus, dnb, yb) = refs[16:31]
+        (rc, rxa, ryb, q0, q1, r0, r1, last, got, dgs, dds, dss) = refs[31:43]
+        send, recv, load, store = refs[43:]
+        me = Place(n_tp)
+        net = Wires(send, recv)
+
+        def chip(dy, dx):
+            return 2 * (me.y + dy * (1 - 2 * me.y)) + me.c + dx * (1 - 2 * me.c)
+
+        def block(ch, core, p=None):
+            start = ch * group + core * rows
+            if p is None:
+                return pl.ds(pl.multiple_of(start, rows), rows)
+            return pl.ds(pl.multiple_of(start + p * piece, piece), piece)
+
+        here = chip(0, 0)
+        pieces = [me.t, lax.rem(me.t + 3, 4), lax.rem(me.t + 1, 4), lax.rem(me.t + 2, 4)]
+        half = piece // 2
+
+        def halves(p, which):
+            start = here * group + me.core * rows + p * piece + which * half
+            return nb.at[pl.ds(pl.multiple_of(start, half), half)]
+
+        def mine(p):
+            return nb.at[block(here, me.core, p)]
+
+        right, left = me.along(1), me.along(-1)
+        z_r = net.wire(lambda: (two_ref, mine(me.t), right))
+        z_l = net.wire(lambda: (two_ref, mine(me.t), left))
+        hop_r = net.wire(lambda: (halves(pieces[1], 0), halves(pieces[1], 0), right))
+        hop_l = net.wire(lambda: (halves(pieces[2], 1), halves(pieces[2], 1), left))
+        to_x, to_y, to_c = [], [], []
+        for j in range(4):
+            src = (lambda: two_ref) if j == 0 else (lambda j=j: mine(pieces[j]))
+            to_x.append(net.wire(lambda j=j, src=src: (src(), mine(pieces[j]), me.over_x)))
+            to_y.append(net.wire(lambda j=j, src=src: (src(), mine(pieces[j]), me.over_y)))
+            to_c.append(net.wire(lambda j=j, src=src: (src(), mine(pieces[j]), me.over_core)))
+        chip_x, chip_y, chip_d = chip(0, 1), chip(1, 0), chip(1, 1)
+        first = 1 - me.core
+        relay_chip = first * chip_x + me.core * chip_y
+        relay_to = me.flip(first, 0, me.core)
+        relay, fwd_x, fwd_y, fwd_d = [], [], [], []
+        for j in range(4):
+            same = lambda ch, j=j: nb.at[block(ch, me.core, pieces[j])]
+            relay.append(net.wire(lambda same=same: (same(relay_chip), same(relay_chip), relay_to)))
+            fwd_x.append(net.wire(lambda same=same: (same(chip_x), same(chip_x), me.over_core)))
+            fwd_y.append(net.wire(lambda same=same: (same(chip_y), same(chip_y), me.over_core)))
+            fwd_d.append(net.wire(lambda same=same: (same(chip_d), same(chip_d), me.over_core)))
+
+        a, b = pl.ds(0, edge), pl.ds(edge, part_w - edge)
+        flips = [(0, 0), (0, 1), (1, 0), (1, 1)]
+        core_w = [
+            net.wire(
+                lambda k=k: (dnb.at[block(chip(*flips[k]), 1 - me.core)], rc.at[k], me.over_core)
+            )
+            for k in range(4)
+        ]
+        ax0 = net.wire(lambda: (dnb.at[block(chip_d, me.core), a], rxa.at[0], me.over_x))
+        by0 = net.wire(lambda: (dnb.at[block(chip_d, me.core), b], ryb.at[0], me.over_y))
+        ax1 = net.wire(lambda: (dnb.at[block(chip_x, me.core), a], rxa.at[1], me.over_x))
+        by1 = net.wire(lambda: (dnb.at[block(chip_y, me.core), b], ryb.at[1], me.over_y))
+        y0 = net.wire(lambda: (q0, r0, me.over_y))
+        x1 = net.wire(lambda: (q1, r1, me.over_x))
+        z_w = []
+        for k in range(1, n_tp):
+            to = lax.rem(me.t + k, n_tp)
+            z_w.append(
+                net.wire(
+                    lambda k=k, to=to: (
+                        last.at[pl.ds(pl.multiple_of(to * piece, piece), piece)],
+                        got.at[k - 1],
+                        me.along(k),
+                    )
+                )
+            )
+
+        loads = [
+            pltpu.make_async_copy(src, dst, load.at[i])
+            for i, (src, dst) in enumerate(
+                [(down_ref, wd), (gate_ref, wg), (up_ref, wu), (wr_ref, wr)]
+                + [(ref, ws.at[i]) for i, ref in enumerate((sg_ref, su_ref, sd_ref))]
+                + [
+                    (cot_ref.at[g], cb.at[pl.ds((2 * (g // 4) + g % 2) * group + (g % 4) // 2 * rows, rows)])
+                    for g in range(8)
+                ]
+            )
+        ]
+        for copy in loads:
+            copy.start()
+        greet([me.over_x, me.over_y, me.over_core] + [me.along(k) for k in range(1, n_tp)])
+        for wire in (z_r, z_l, to_x[0], to_y[0], to_c[0]):
+            wire.start()
+        nb[block(here, me.core, me.t), :] = two_ref[...]
+        z_r.landed()
+        hop_r.start()
+        for wires in (to_x, to_y, to_c):
+            wires[1].start()
+        z_l.landed()
+        hop_l.start()
+        for wires in (to_x, to_y, to_c):
+            wires[2].start()
+        for copy in loads:
+            copy.wait()
+        hop_r.landed()
+        hop_l.landed()
+        for wires in (to_x, to_y, to_c):
+            wires[3].start()
+        for wire in to_c:
+            wire.landed()
+
+        lane = lax.broadcasted_iota(jnp.int32, (group, LANES), 1)
+        e_first = slot(me.s, me.c) * 2
+        lane_row = lax.broadcasted_iota(jnp.int32, (1, LANES), 1)
+
+        def flip_chip(k):
+            return chip(k // 2, lax.rem(k, 2))
+
+        def hidden(k, carry):
+            at = pl.ds(pl.multiple_of(flip_chip(k) * group, group), group)
+
+            @pl.when(k == 1)
+            def _():
+                for j in range(4):
+                    to_x[j].landed()
+                    to_y[j].landed()
+                    relay[j].start()
+                    fwd_x[j].start()
+                    fwd_y[j].start()
+                for j in range(4):
+                    fwd_x[j].landed()
+
+            @pl.when(k == 2)
+            def _():
+                for j in range(4):
+                    fwd_y[j].landed()
+
+            @pl.when(k == 3)
+            def _():
+                for j in range(4):
+                    relay[j].landed()
+                    fwd_d[j].start()
+                for j in range(4):
+                    fwd_d[j].landed()
+
+            logits = jnp.where(lane < experts, mdot(nb[at, :], wr[...]), NEG)
+            e = jnp.exp(logits - jnp.max(logits, axis=1, keepdims=True))
+            probs = e / jnp.sum(e, axis=1, keepdims=True)
+            routed = cb[at, width : width + LANES].astype(F32)
+            pg = jnp.zeros((group, LANES), F32)
+            for j in range(3):
+                shared = j == 2
+                if shared:
+                    g = dot_nt(nb[at, :], ws[0])
+                    u = dot_nt(nb[at, :], ws[1])
+                    back = dot_nt(cb[at, 0:width], ws[2])
+                else:
+                    g = mdot(nb[at, :], wg[j])
+                    u = mdot(nb[at, :], wu[j])
+                    back = dot_nt(cb[at, 0:width], wd[j])
+                sig = 1.0 / (1.0 + jnp.exp(-g))
+                silu = g * sig
+                h = silu * u
+                if not shared:
+                    expert = e_first + j
+                    hit = jnp.where(
+                        (lane < topk) & (routed == expert.astype(F32)), 1.0, 0.0
+                    )
+                    chosen = jnp.max(hit, axis=1, keepdims=True)
+                    weight = chosen * jnp.sum(
+                        jnp.where(lane == expert, probs, 0.0), axis=1, keepdims=True
+                    )
+                    grad = chosen * jnp.sum(h * back, axis=1, keepdims=True)
+                    high = grad.astype(BF).astype(F32)
+                    pg = jnp.where(lane == expert, high, pg)
+                    pg = jnp.where(lane == expert + LANES // 2, grad - high, pg)
+                    h = h * weight
+                    back = back * weight
+                gate_grad = (back * u * (sig * (1.0 + g * (1.0 - sig)))).astype(BF)
+                up_grad = (back * silu).astype(BF)
+                if shared:
+                    hws[at, :] = h.astype(BF)
+                    ggs[at, :] = gate_grad
+                    uus[at, :] = up_grad
+                else:
+                    hwe[j, at, :] = h.astype(BF)
+                    gge[j, at, :] = gate_grad
+                    uue[j, at, :] = up_grad
+            dnb[at, width:part_w] = pg.astype(BF)
+            return carry
+
+        lax.fori_loop(0, 4, hidden, 0)
+
+        n2_copies = []
+        cols_s = pl.ds(pl.multiple_of(me.s * shard_w, shard_w), shard_w)
+        for g in range(8):
+            row = (2 * (g // 4) + g % 2) * group + (g % 4) // 2 * rows
+            n2_copies.append(
+                pltpu.make_async_copy(nb.at[pl.ds(row, rows), cols_s], n2_out.at[g], store.at[g])
+            )
+            n2_copies[-1].start()
+
+        step = 16
+
+        def add(target, t_at, cols, left, right, count):
+            def one(r, carry):
+                at = pl.ds(pl.multiple_of(r * step, step), step)
+                total = left(r).astype(F32) + right(r).astype(F32)
+                target[pl.ds(pl.multiple_of(t_at + r * step, step), step), cols] = total.astype(
+                    target.dtype
+                )
+                return carry
+
+            lax.fori_loop(0, count // step, one, 0)
+
+        def row_at(base, r):
+            return pl.ds(pl.multiple_of(base + r * step, step), step)
+
+        every = pl.ds(0, part_w)
+
+        def sum_cores(k):
+            base = chip(*flips[k]) * group + me.core * rows
+            core_w[k].landed()
+            add(
+                dnb,
+                base,
+                every,
+                lambda r: dnb[row_at(base, r), every],
+                lambda r: rc[k, row_at(0, r), :],
+                rows,
+            )
+
+        n_col = 4
+        col_w = width // n_col
+
+        def normed_grad(i, carry):
+            k = 3 - i
+            at = pl.ds(pl.multiple_of(flip_chip(k) * group, group), group)
+
+            def columns(n, carry):
+                cols = pl.ds(pl.multiple_of(n * col_w, col_w), col_w)
+                total = mdot(ggs[at, :], ws[0, :, cols]) + mdot(uus[at, :], ws[1, :, cols])
+                for j in range(2):
+                    total = total + dot_nt(gge[j, at, :], wg[j, cols, :])
+                    total = total + dot_nt(uue[j, at, :], wu[j, cols, :])
+                dnb[at, cols] = total.astype(BF)
+                return carry
+
+            lax.fori_loop(0, n_col, columns, 0)
+            for kk in range(4):
+
+                @pl.when(k == kk)
+                def _():
+                    core_w[kk].start()
+                    if kk < 3:
+                        sum_cores(kk + 1)
+                    if kk == 2:
+                        ax0.start()
+                        by0.start()
+                    if kk == 1:
+                        by1.start()
+                    if kk == 0:
+                        ax1.start()
+
+            return carry
+
+        lax.fori_loop(0, 4, normed_grad, 0)
+
+        def stage_two():
+            base_y, base_x = chip_y * group + me.core * rows, chip_x * group + me.core * rows
+            ax0.landed()
+            add(q0, 0, pl.ds(0, edge), lambda r: dnb[row_at(base_y, r), a], lambda r: rxa[0, row_at(0, r), :], rows)
+            y0.start()
+            by0.landed()
+            add(
+                q1,
+                0,
+                pl.ds(0, part_w - edge),
+                lambda r: dnb[row_at(base_x, r), b],
+                lambda r: ryb[0, row_at(0, r), :],
+                rows,
+            )
+            x1.start()
+
+        def output(k, carry):
+            at = pl.ds(pl.multiple_of(k * group, group), group)
+
+            @pl.when(k == 1)
+            def _():
+                sum_cores(0)
+
+            @pl.when(k == 3)
+            def _():
+                stage_two()
+
+            def columns(n, carry):
+                cols = pl.ds(pl.multiple_of(n * col_w, col_w), col_w)
+                total = mdot(hws[at, :], ws[2, :, cols])
+                for j in range(2):
+                    total = total + mdot(hwe[j, at, :], wd[j, :, cols])
+                yb[at, cols] = total.astype(BF)
+                return carry
+
+            lax.fori_loop(0, n_col, columns, 0)
+            return carry
+
+        lax.fori_loop(0, 4, output, 0)
+        y_copy = pltpu.make_async_copy(yb, y_out, store.at[8])
+        y_copy.start()
+
+        def finish_plane():
+            base = here * group + me.core * rows
+            for wire in (ax1, by1, y0, x1):
+                wire.landed()
+
+            def final(r, carry):
+                at, big = row_at(0, r), row_at(base, r)
+                one = dnb[big, a].astype(F32) + rxa[1, at, :].astype(F32) + r0[at, :].astype(F32)
+                two = dnb[big, b].astype(F32) + ryb[1, at, :].astype(F32) + r1[at, :].astype(F32)
+                last[at, a] = one.astype(BF)
+                last[at, b] = two.astype(BF)
+                return carry
+
+            lax.fori_loop(0, rows // step, final, 0)
+            for wire in z_w:
+                wire.start()
+
+        m_w = 256
+
+        def stores(m, buf):
+            rows_m = pl.ds(pl.multiple_of(m * m_w, m_w), m_w)
+            made = []
+            for j in range(2):
+                for i, out in enumerate((dg_out, du_out)):
+                    made.append(
+                        pltpu.make_async_copy(
+                            dgs.at[buf, 2 * j + i], out.at[j, rows_m], store.at[9 + 4 * buf + 2 * j + i]
+                        )
+                    )
+            return made
+
+        def gate_up(m, carry):
+            buf = lax.rem(m, 2)
+            cols = pl.ds(pl.multiple_of(m * m_w, m_w), m_w)
+
+            @pl.when(m >= 2)
+            def _():
+                for bb in range(2):
+
+                    @pl.when(buf == bb)
+                    def _():
+                        for copy in stores(m - 2, bb):
+                            copy.wait()
+
+            @pl.when(m == 4)
+            def _():
+                finish_plane()
+
+            left = nb[:, cols]
+            for j in range(2):
+                dgs[buf, 2 * j] = dot_tn(left, gge[j])
+                dgs[buf, 2 * j + 1] = dot_tn(left, uue[j])
+            dss[0, :, cols] = dot_tn(ggs[...], left).astype(BF)
+            dss[1, :, cols] = dot_tn(uus[...], left).astype(BF)
+            for bb in range(2):
+
+                @pl.when(buf == bb)
+                def _():
+                    for copy in stores(m, bb):
+                        copy.start()
+
+            return carry
+
+        n_m = width // m_w
+        lax.fori_loop(0, n_m, gate_up, 0)
+        for m in (n_m - 2, n_m - 1):
+            for copy in stores(m, m % 2):
+                copy.wait()
+
+        def down_stores(m, buf):
+            cols = pl.ds(pl.multiple_of(m * m_w, m_w), m_w)
+            return [
+                pltpu.make_async_copy(dds.at[buf, j], dd_out.at[j, :, cols], store.at[17 + 2 * buf + j])
+                for j in range(2)
+            ]
+
+        def down_grad(m, carry):
+            buf = lax.rem(m, 2)
+            cols = pl.ds(pl.multiple_of(m * m_w, m_w), m_w)
+
+            @pl.when(m >= 2)
+            def _():
+                for bb in range(2):
+
+                    @pl.when(buf == bb)
+                    def _():
+                        for copy in down_stores(m - 2, bb):
+                            copy.wait()
+
+            right_c = cb[:, cols]
+            for j in range(2):
+                dds[buf, j] = dot_tn(hwe[j], right_c)
+            dss[2, :, cols] = dot_tn(hws[...], right_c).astype(BF)
+            for bb in range(2):
+
+                @pl.when(buf == bb)
+                def _():
+                    for copy in down_stores(m, bb):
+                        copy.start()
+
+            return carry
+
+        lax.fori_loop(0, n_m, down_grad, 0)
+        ds_copy = pltpu.make_async_copy(dss, ds_out, store.at[21])
+        ds_copy.start()
+        for m in (n_m - 2, n_m - 1):
+            for copy in down_stores(m, m % 2):
+                copy.wait()
+
+        for wire in z_w:
+            wire.landed()
+        for r in range(piece // step):
+            total = last[row_at(me.t * piece, r), :].astype(F32)
+            for k in range(n_tp - 1):
+                total = total + got[k, r * step : (r + 1) * step, :].astype(F32)
+            two_out[r * step : (r + 1) * step, :] = total
+        for copy in n2_copies:
+            copy.wait()
+        y_copy.wait()
+        ds_copy.wait()
+        for wire in net.all:
+            wire.sent()
+
+    ins = (two_own, cot_all, gate, up, down, sg_t, su_t, sd, w_router)
+    outs = [
+        ((piece, part_w), F32),
+        ((tokens, width), BF),
+        (gate.shape, F32),
+        (up.shape, F32),
+        (down.shape, F32),
+        ((3, hid_s, width), BF),
+        ((8, rows, shard_w), BF),
+    ]
+    scratch = [
+        VMEM((tokens, width), BF),
+        VMEM((tokens, pack), BF),
+        VMEM(gate.shape, BF),
+        VMEM(up.shape, BF),
+        VMEM(down.shape, BF),
+        VMEM((3, hid_s, width), BF),
+        VMEM(w_router.shape, BF),
+        *[VMEM((2, tokens, hid), BF)] * 3,
+        *[VMEM((tokens, hid_s), BF)] * 3,
+        VMEM((tokens, part_w), BF),
+        VMEM((tokens, width), BF),
+        VMEM((4, rows, part_w), BF),
+        VMEM((2, rows, edge), BF),
+        VMEM((2, rows, part_w - edge), BF),
+        VMEM((rows, edge), BF),
+        VMEM((rows, part_w - edge), BF),
+        VMEM((rows, edge), BF),
+        VMEM((rows, part_w - edge), BF),
+        VMEM((rows, part_w), BF),
+        VMEM((n_tp - 1, piece, part_w), BF),
+        VMEM((2, 4, 256, hid), F32),
+        VMEM((2, 2, hid, 256), F32),
+        VMEM((3, hid_s, width), BF),
+    ]
+    return pl.pallas_call(
+        body,
+        out_shape=tuple(jax.ShapeDtypeStruct(*o) for o in outs),
+        in_specs=[pl.BlockSpec(memory_space=VMEM)] + [pl.BlockSpec(memory_space=ANY)] * 8,
+        out_specs=(pl.BlockSpec(memory_space=VMEM), *[pl.BlockSpec(memory_space=ANY)] * 6),
+        scratch_shapes=[
+            *scratch,
+            pltpu.SemaphoreType.DMA((n_wires,)),
+            pltpu.SemaphoreType.DMA((n_wires,)),
+            pltpu.SemaphoreType.DMA((15,)),
+            pltpu.SemaphoreType.DMA((22,)),
+        ],
+        compiler_params=pltpu.CompilerParams(
+            collective_id=4, has_side_effects=True, vmem_limit_bytes=66 * 10**6
+        ),
+        name="feed_forward",
+    )(*ins)
+
+
 def per_device(
     block_input,
     norm1_gain,
@@ -668,7 +1205,6 @@
     rows, width = block_input.shape
     topk = routes.shape[1]
     experts = router_weight.shape[1]
-    local_experts = expert_gate.shape[0]
     heads = q_weight.shape[1] // (DN + DR)
     scale = (DN + DR) ** (-0.5)
     piece = rows // n_tp
@@ -704,9 +1240,6 @@
     cot_all, sg_t, su_t, sd = plane_exchange(
         (cot_pack,), (), (shared_gate.T, shared_up.T, shared_down), n_tp, 1, "early_exchange"
     )
-    cot_all = cot_all.reshape(-1, width + LANES)
-    routes_all = cot_all[:, width : width + topk].astype(jnp.int32)
-    cot_all = cot_all[:, :width]
 
     x_float = block_input.astype(F32)
     cosine, sine = rope_tables(rows, (c_id * rows).astype(F32))
@@ -740,75 +1273,26 @@
     attn_full = tp_reduce_scatter(mdot(attn_flat, w_output).astype(BF), n_tp, 2, "attn_scatter")
     mid = own(x_float) + attn_full
     two_own = norm_rows(mid, gain_two).astype(BF)
-    normed_two = gather_everywhere(two_own, n_tp, 3, "normed_two_gather").reshape(-1, width)
-
-    probs = jax.nn.softmax(mdot(normed_two, w_router), axis=-1)
-    first = slot(s_id, c_id) * local_experts
-    hots = []
-    for j in range(local_experts):
-        chosen = jnp.any(routes_all == first + j, axis=1, keepdims=True)
-        prob = jnp.sum(
-            jnp.where(jnp.arange(experts, dtype=jnp.int32)[None, :] == first + j, probs, 0.0),
-            axis=1,
-            keepdims=True,
-        )
-        hots.append((chosen, jnp.where(chosen, prob, 0.0)))
-    moe_part = None
-    two_part = None
-    pg_cols = []
-    lanes = jnp.arange(LANES, dtype=jnp.int32)[None, :]
-    grads_gate, grads_up, grads_down = [], [], []
-    for j in range(local_experts + 1):
-        shared = j == local_experts
-        if shared:
-            gate_act, up_act = dot_nt(normed_two, sg_t), dot_nt(normed_two, su_t)
-            back = dot_nt(cot_all, sd)
-        else:
-            gate_act = mdot(normed_two, expert_gate[j])
-            up_act = mdot(normed_two, expert_up[j])
-            back = dot_nt(cot_all, expert_down[j])
-        silu = jax.nn.silu(gate_act)
-        hidden = silu * up_act
-        if not shared:
-            chosen, weight = hots[j]
-            hidden_grad = back * weight
-            route_grad = jnp.where(chosen, jnp.sum(hidden * back, axis=1, keepdims=True), 0.0)
-            hidden = hidden * weight
-            high = route_grad.astype(BF)
-            low = (route_grad - high.astype(F32)).astype(BF)
-            pg_cols.append(
-                jnp.where(lanes == first + j, high, jnp.where(lanes == first + j + 64, low, jnp.zeros((), BF)))
-            )
-        else:
-            hidden_grad = back
-        hidden = hidden.astype(BF)
-        gate_grad = (hidden_grad * up_act * silu_slope(gate_act)).astype(BF)
-        up_grad = (hidden_grad * silu).astype(BF)
-        if shared:
-            y = mdot(hidden, sd)
-            dn = mdot(gate_grad, sg_t) + mdot(up_grad, su_t)
-            grads = [dot_tn(gate_grad, normed_two), dot_tn(up_grad, normed_two), dot_tn(hidden, cot_all)]
-            shared_grads = [g.astype(BF) for g in grads]
-        else:
-            y = mdot(hidden, expert_down[j])
-            dn = dot_nt(gate_grad, expert_gate[j]) + dot_nt(up_grad, expert_up[j])
-            grads_gate.append(dot_tn(normed_two, gate_grad))
-            grads_up.append(dot_tn(normed_two, up_grad))
-            grads_down.append(dot_tn(hidden, cot_all))
-        moe_part = y if moe_part is None else moe_part + y
-        two_part = dn if two_part is None else two_part + dn
-    pg_part = functools.reduce(jnp.add, pg_cols)
-    part = jnp.concatenate(
-        [moe_part.astype(BF), two_part.astype(BF), pg_part, jnp.zeros_like(pg_part)], axis=1
-    ).reshape(8, rows, -1)
-    summed = reduce_everywhere(part, n_tp, 4, "feed_forward_scatter")
-    moe_out, two_grad = summed[:, :width], summed[:, width : 2 * width]
-    prob_grad = summed[:, 2 * width : 2 * width + experts]
-    prob_grad = prob_grad + summed[:, 2 * width + 64 : 2 * width + 64 + experts]
-    out_own = mid + moe_out
-    grad_expert_gate, grad_expert_up, grad_expert_down = (
-        jnp.stack(g) for g in (grads_gate, grads_up, grads_down)
-    )
+    summed, y_part, grad_expert_gate, grad_expert_up, grad_expert_down, shared_grads, two_cols = feed_forward(
+        two_own,
+        cot_all,
+        expert_gate,
+        expert_up,
+        expert_down,
+        sg_t,
+        su_t,
+        sd,
+        jnp.pad(w_router, ((0, 0), (0, LANES - experts))),
+        experts,
+        topk,
+        n_tp,
+    )
+    two_grad = summed[:, :width]
+    prob_grad = summed[:, width : width + experts]
+    prob_grad = prob_grad + summed[:, width + LANES // 2 : width + LANES // 2 + experts]
+    y_part = y_part.reshape(2, 2, 2, rows, width).transpose(0, 2, 1, 3, 4).reshape(8, rows, width)
+    out_own = mid + reduce_everywhere(y_part, n_tp, 3, "y_scatter")
+    shared_grads = [shared_grads[i] for i in range(3)]
 
     probs_own = jax.nn.softmax(mdot(two_own, w_router), axis=-1)
     logit_grad = (
@@ -889,8 +1373,7 @@
     grad_latent = dot_tn(one_cols, lat_all[:, : KVR + DR])
     grad_expand = dot_tn(lat_cols, dkv_all)
     grad_out_w = dot_tn(attn_all, mid_cols)
-    two_cols = lax.dynamic_slice_in_dim(normed_two, s_id * shard_w, shard_w, 1)
-    grad_router = dot_tn(two_cols, logit_all[:, :experts])
+    grad_router = dot_tn(two_cols.reshape(8 * rows, -1), logit_all[:, :experts])
     grad_sgate = sg_cols.reshape(-1, shard_w).T.astype(F32)
     grad_sup = su_cols.reshape(-1, shard_w).T.astype(F32)
     grad_sdown = sd_cols.reshape(-1, shard_w).astype(F32)

time: 630 us -> 527 us (0.84)
  matrix products: 142 us -> 26.9 us
  Pallas kernels: 373 us -> 397 us
  other arithmetic: 53.4 us -> 29.5 us
  local copies, waits for them, and re-layouts: 51.4 us -> 69.6 us
    pallas_call x0 -> x1, Pallas kernels: none -> 84.9 us  [feed_forward(): pl.pallas_call(body, out_shape=tuple((jax.ShapeDtypeStruct(*o) for o in o...]
    pallas_call x12 -> x11, Pallas kernels: 373 us -> 313 us  [comm_call(): pl.pallas_call(body, out_shape=tuple((jax.ShapeDtypeStruct(shape, dtype)...]
    dot_general x14 -> x5, matrix products: 53.7 us -> 7.26 us  [dot_nt(): lax.dot_general(left, right, (((1,), (1,)), ((), ())), preferred_element_...]
    dot_general x15 -> x5, matrix products: 46 us -> 6.55 us  [mdot(): return jnp.dot(left, right, preferred_element_type=F32)]
    dot_general x14 -> x5, matrix products: 35 us -> 10.6 us  [dot_tn(): lax.dot_general(left, right, (((0,), (0,)), ((), ())), preferred_element_...]
    unnamed x207 -> x178, local copies, waits for them, and re-layouts: 16 us -> 32.6 us
    another operation x6 -> x4, other arithmetic: 10.8 us -> 2.08 us  [the longest x2 7.68 us: per_device(): jnp.stack(g)]
    concatenate x1 -> x0, other arithmetic: 6.31 us -> none  [per_device(): jnp.concatenate([moe_part.astype(BF), two_part.astype(BF), pg_part, jnp.z...]
where the time goes in v2:
time: 527 us; the launch traced here: 525 us
  Pallas kernels  397 us (75%)
  local copies, waits for them, and re-layouts  69.6 us (13%)
  other arithmetic  29.5 us (6%)
  matrix products  26.9 us (5%)
    pallas_call x11, Pallas kernels, comm_call(): pl.pallas_call(body, out_shape=tuple((jax.ShapeDtypeStruct(shape, dtype)...  313 us
    pallas_call x1, Pallas kernels, feed_forward(): pl.pallas_call(body, out_shape=tuple((jax.ShapeDtypeStruct(*o) for o in o...  84.9 us
    unnamed x178, local copies, waits for them, and re-layouts  32.6 us
    dot_general x5, matrix products, dot_tn(): lax.dot_general(left, right, (((0,), (0,)), ((), ())), preferred_element_...  10.6 us

profile of v2, /device:TPU:0, one launch (start us, length us, event | category | flops | bytes accessed | tf_op | source)
XLA Modules:
  0.0 525.3 jit_solution(5071136947993393443)
XLA Ops:
  0.7 1.3 multiply_reduce_fusion
  4.5 3.2 concatenate.44.refs_4_
  9.1 2.4 copy.86.refs_1_
  12.5 2.8 copy.99.refs_2_
  15.3 4.6 copy.100.refs_3_
  19.9 37.4 %early_exchange.1 = (bf16[8,128,2176]{2,1,0:T(8,128)(2,1)}, bf16[88,2048]{1,0:T(8,128)(2,1)}, bf16[88,2048]{1,0:T(8,128)(2,1)}, bf16[88,2048]{1,0:T(8,128)(2,1)}) custom-call(bf16[128,2176]{1,0:T(8,128)(2,1)} %fusion.23.refs_0_, bf16[704,512]{1,0:T(8,128)(2,1)} %bitcast.151, bf16[704,512]{1,0:T(8,128)(2,1)} %bitcast.152, bf16[704,512]{1,0:T(8,128)(2,1)} %refs_3_.4), custom_call_target="tpu_custom_call" | custom-call | tf_op jit(solution)/shard_map/early_exchange/pallas_call | solution.py:159
  57.2 40.6 %start_gather.1 = (bf16[4,512,768]{2,1,0:T(8,128)(2,1)}, bf16[4,512,576]{2,1,0:T(8,128)(2,1)}, bf16[4,128,1024]{2,1,0:T(8,128)(2,1)}, bf16[4,512,512]{2,1,0:T(8,...) custom-call(bf16[512,768]{1,0:T(8,128)(2,1)} %refs_0_.1, bf16[512,576]{1,0:T(8,128)(2,1)} %copy.86.refs_1_, ...), custom_call_target="tpu_custom_call" | custom-call | tf_op jit(solution)/shard_map/start_gather/pallas_call | solution.py:159
  97.8 1.7 fusion
  102.4 1.1 fusion.62
  107.6 1.2 reshape.337
  108.8 2.1 fusion.58
  110.8 1.9 copy.125
  114.6 2.9 copy.103
  117.6 2.4 copy.97
  120.0 4.6 dot_general.92
  124.6 2.9 copy.87
  127.5 3.1 fusion.26
  132.6 1.6 convolution_convert_fusion.1.in_ref
  134.2 15.4 %attn_scatter.1 = f32[32,2048]{1,0:T(8,128)} custom-call(bf16[128,2048]{1,0:T(8,128)(2,1)} %convolution_convert_fusion.1.in_ref), custom_call_target="tpu_custom_call" | custom-call | tf_op jit(solution)/shard_map/attn_scatter/pallas_call | solution.py:159
  149.7 1.8 multiply_reduce_fusion.8
  153.9 84.9 %feed_forward.1 = (f32[32,2176]{1,0:T(8,128)}, bf16[1024,2048]{1,0:T(8,128)(2,1)}, f32[2,2048,352]{2,1,0:T(8,128)}, f32[2,2048,352]{2,1,0:T(8,128)}, f32[2,352,2...) custom-call(bf16[32,2048]{1,0:T(8,128)(2,1)} %copy-done.26, ...), custom_call_target="tpu_custom_call" | custom-call | tf_op jit(solution)/shard_map/feed_forward/pallas_call | solution.py:1166
  238.8 4.8 copy.101
  243.6 37.3 %y_scatter.1 = f32[32,2048]{1,0:T(8,128)} custom-call(bf16[8,128,2048]{2,1,0:T(8,128)(2,1)} %bitcast.122), custom_call_target="tpu_custom_call" | custom-call | tf_op jit(solution)/shard_map/y_scatter/pallas_call | solution.py:159
  282.7 1.9 fusion.56
  285.2 16.2 %mid_grad_gather.1 = bf16[128,2176]{1,0:T(8,128)(2,1)} custom-call(bf16[32,2176]{1,0:T(8,128)(2,1)} %fusion.41.refs_0_), custom_call_target="tpu_custom_call" | custom-call | tf_op jit(solution)/shard_map/mid_grad_gather/pallas_call | solution.py:159
  301.4 1.8 multiply_reduce_fusion.5
  305.6 2.0 convolution_convert_fusion
  307.8 1.3 copy.121
  309.1 1.4 select_maximum_fusion
  311.3 8.7 %kv_grad_swap.1 = bf16[128,1152]{1,0:T(8,128)(2,1)} custom-call(bf16[128,1152]{1,0:T(8,128)(2,1)} %dynamic-slice_convert_fusion.in_ref), custom_call_target="tpu_custom_call" | custom-call | tf_op jit(solution)/shard_map/kv_grad_swap/pallas_call | solution.py:159
  323.2 16.2 %attn_back_scatter.1 = f32[32,2688]{1,0:T(8,128)} custom-call(bf16[128,2688]{1,0:T(8,128)(2,1)} %pad_maximum_fusion.1.in_ref), custom_call_target="tpu_custom_call" | custom-call | tf_op jit(solution)/shard_map/attn_back_scatter/pallas_call | solution.py:159
  342.2 2.1 multiply_reduce_fusion.3
  345.5 12.6 %gain_sum.1 = f32[8,640]{1,0:T(8,128)} custom-call(f32[8,640]{1,0:T(8,128)} %reshape.344.in_ref), custom_call_target="tpu_custom_call" | custom-call | tf_op jit(solution)/shard_map/gain_sum/pallas_call | solution.py:159
  360.1 1.8 multiply_add_fusion.refs_1_
  361.9 10.2 %latent_gather.1 = bf16[128,640]{1,0:T(8,128)(2,1)} custom-call(bf16[32,640]{1,0:T(8,128)(2,1)} %pad.35.refs_0_), custom_call_target="tpu_custom_call" | custom-call | tf_op jit(solution)/shard_map/latent_gather/pallas_call | solution.py:159
  375.3 38.1 %output_gather.1 = (f32[128,2048]{1,0:T(8,128)}, f32[128,2048]{1,0:T(8,128)}) custom-call(f32[32,2048]{1,0:T(8,128)} %get-tuple-element.140.refs_0_, f32[32,2048]{1,0:T(8,128)} %multiply_add_fusion.refs_1_), custom_call_target="tpu_custom_call" | custom-call | tf_op jit(solution)/shard_map/output_gather/pallas_call | solution.py:159
  413.4 6.4 %copy.112 = f32[2,2048,352]{1,2,0:T(8,128)} copy(f32[2,2048,352]{2,1,0:T(8,128)} %get-tuple-element.113) | data formatting | bytes 11534336
  419.8 6.4 %copy.113 = f32[2,2048,352]{1,2,0:T(8,128)} copy(f32[2,2048,352]{2,1,0:T(8,128)} %get-tuple-element.114) | data formatting | bytes 11534336
  426.2 80.0 %late_exchange.1 = (bf16[8,128,3072]{2,1,0:T(8,128)(2,1)}, bf16[8,128,512]{2,1,0:T(8,128)(2,1)}, bf16[8,128,128]{2,1,0:T(8,128)(2,1)}, bf16[8,128,512]{2,1,0:T(8...) custom-call(bf16[128,3072]{1,0:T(8,128)(2,1)} %copy-done.25, ...), custom_call_target="tpu_custom_call" | custom-call | tf_op jit(solution)/shard_map/late_exchange/pallas_call | solution.py:159
  506.2 2.0 fusion.34
  508.2 3.3 fusion.21
  511.5 1.3 fusion.3
  512.7 1.8 fusion.7
  514.6 2.2 fusion.5
  516.8 1.3 convert_bitcast_fusion.1
  518.1 1.3 convert_bitcast_fusion
  519.5 1.3 bitcast_convert_fusion
  522.8 2.5 copy.141
  (255 shorter events, 37.7 us)
Async XLA Ops:
  0.6 7.5 %copy-start.24 = (f32[128,2048]{1,0:T(8,128)S(1)}, f32[128,2048]{1,0:T(8,128)}, u32[]{:S(2)}) copy-start(f32[128,2048]{1,0:T(8,128)} %param.33) | copy-start | bytes 3145732
  0.7 7.4 %copy-start.69 = (f32[128]{0:T(128)}, f32[128]{0:T(128)S(1)}, u32[]{:S(2)}) copy-start(f32[128]{0:T(128)S(1)} %iota_add_fusion) | copy-start | bytes 1540
  0.7 103.5 %copy-start.63 = (f32[32]{0:T(128)}, f32[32]{0:T(128)S(1)}, u32[]{:S(2)}) copy-start(f32[32]{0:T(128)S(1)} %negate_power_fusion) | copy-start | bytes 388
  8.1 122.5 %copy-start.46 = (f32[128,32]{0,1:T(8,128)}, f32[128,32]{0,1:T(8,128)S(1)}, u32[]{:S(2)}) copy-start(f32[128,32]{0,1:T(8,128)S(1)} %copy.92) | copy-start | bytes 49156
  8.2 122.4 %copy-start.48 = (f32[128,32]{0,1:T(8,128)}, f32[128,32]{0,1:T(8,128)S(1)}, u32[]{:S(2)}) copy-start(f32[128,32]{0,1:T(8,128)S(1)} %copy.93) | copy-start | bytes 49156
  8.2 4.3 copy-start.18
  97.8 4.3 copy-start.16
  97.8 4.6 copy-start.2
  100.2 6.1 %copy-start.58 = (f32[4,1,128]{2,1,0:T(1,128)}, f32[4,1,128]{2,1,0:T(1,128)S(1)}, u32[]{:S(2)}) copy-start(f32[4,1,128]{2,1,0:T(1,128)S(1)} %slice_convert_fusion.6) | copy-start | bytes 6148
  102.1 11.6 %copy-start.9 = (bf16[4,512,16]{2,1,0:T(8,128)(2,1)}, bf16[4,512,16]{2,1,0:T(8,128)(2,1)S(1)}, u32[]{:S(2)}) copy-start(bf16[4,512,16]{2,1,0:T(8,128)(2,1)S(1)} %slice.131) | copy-start | bytes 196612
  107.1 5.6 %copy-start.8 = (bf16[128,2048]{1,0:T(8,128)(2,1)S(1)}, bf16[128,2048]{1,0:T(8,128)(2,1)}, u32[]{:S(2)}) copy-start(bf16[128,2048]{1,0:T(8,128)(2,1)} %refs_5_.1) | copy-start | bytes 1572868
  108.8 5.9 %copy-start.5 = (bf16[4,512,512]{2,1,0:T(8,128)(2,1)S(1)}, bf16[4,512,512]{2,1,0:T(8,128)(2,1)}, u32[]{:S(2)}) copy-start(bf16[4,512,512]{2,1,0:T(8,128)(2,1)} %get-tuple-element.47) | copy-start | bytes 6291460
  110.8 19.8 %copy-start.21 = (bf16[256,4,128]{2,1,0:T(4,128)(2,1)}, bf16[256,4,128]{2,1,0:T(4,128)(2,1)S(1)}, u32[]{:S(2)}) copy-start(bf16[256,4,128]{2,1,0:T(4,128)(2,1)S(1)} %get-tuple-element.136) | copy-start | bytes 786436
  120.0 4.6 copy-start
  132.6 20.6 %copy-start.27 = (bf16[128,4,128]{0,2,1:T(8,128)(2,1)}, bf16[128,4,128]{0,2,1:T(8,128)(2,1)S(1)}, u32[]{:S(2)}) copy-start(bf16[128,4,128]{0,2,1:T(8,128)(2,1)S(1)} %fusion.17) | copy-start | bytes 393220
  132.6 18.9 %copy-start.54 = (f32[2048]{0:T(1024)S(1)}, f32[2048]{0:T(1024)}, u32[]{:S(2)}) copy-start(f32[2048]{0:T(1024)} %convert.61) | copy-start | bytes 24580
  132.6 19.0 %copy-start.10 = (bf16[4,512,16]{2,1,0:T(8,128)(2,1)S(1)}, bf16[4,512,16]{2,1,0:T(8,128)(2,1)}, u32[]{:S(2)}) copy-start(bf16[4,512,16]{2,1,0:T(8,128)(2,1)} %copy-done.9) | copy-start | bytes 196612
  243.5 37.3 %copy-start.42 = (f32[32,2176]{1,0:T(8,128)S(1)}, f32[32,2176]{1,0:T(8,128)}, u32[]{:S(2)}) copy-start(f32[32,2176]{1,0:T(8,128)} %get-tuple-element.53) | copy-start | bytes 835588
  243.5 37.3 %copy-start.62 = (f32[32]{0:T(128)S(1)}, f32[32]{0:T(128)}, u32[]{:S(2)}) copy-start(f32[32]{0:T(128)} %copy-done.61) | copy-start | bytes 388
  243.6 37.3 %copy-start.67 = (f32[32]{0:T(128)S(1)}, f32[32]{0:T(128)}, u32[]{:S(2)}) copy-start(f32[32]{0:T(128)} %fusion.51) | copy-start | bytes 388
  243.6 37.7 %copy-start.55 = (f32[2048]{0:T(1024)S(1)}, f32[2048]{0:T(1024)}, u32[]{:S(2)}) copy-start(f32[2048]{0:T(1024)} %convert.61) | copy-start | bytes 24580
  243.6 37.7 %copy-start.66 = (f32[32]{0:T(128)S(1)}, f32[32]{0:T(128)}, u32[]{:S(2)}) copy-start(f32[32]{0:T(128)} %copy-done.65) | copy-start | bytes 388
  243.6 38.6 %copy-start.72 = (f32[32]{0:T(128)S(1)}, f32[32]{0:T(128)}, u32[]{:S(2)}) copy-start(f32[32]{0:T(128)} %get-tuple-element.129) | copy-start | bytes 388
  243.6 38.6 %copy-start.75 = (f32[32]{0:T(128)S(1)}, f32[32]{0:T(128)}, u32[]{:S(2)}) copy-start(f32[32]{0:T(128)} %copy-done.74) | copy-start | bytes 388
  280.9 20.5 %copy-start.4 = (bf16[4,128,2048]{2,1,0:T(8,128)(2,1)S(1)}, bf16[4,128,2048]{2,1,0:T(8,128)(2,1)}, u32[]{:S(2)}) copy-start(bf16[4,128,2048]{2,1,0:T(8,128)(2,1)} %dot_general.92) | copy-start | bytes 6291460
  280.9 20.5 %copy-start.28 = (bf16[128,4,128]{0,2,1:T(8,128)(2,1)S(1)}, bf16[128,4,128]{0,2,1:T(8,128)(2,1)}, u32[]{:S(2)}) copy-start(bf16[128,4,128]{0,2,1:T(8,128)(2,1)} %copy-done.27) | copy-start | bytes 393220
  284.5 18.8 %copy-start.12 = (f32[4,128,256]{2,1,0:T(8,128)S(1)}, f32[4,128,256]{2,1,0:T(8,128)}, u32[]{:S(2)}) copy-start(f32[4,128,256]{2,1,0:T(8,128)} %copy-done.11) | copy-start | bytes 1572868
  284.5 18.8 %copy-start.35 = (bf16[256,4,128]{0,2,1:T(8,128)(2,1)S(1)}, bf16[256,4,128]{0,2,1:T(8,128)(2,1)}, u32[]{:S(2)}) copy-start(bf16[256,4,128]{0,2,1:T(8,128)(2,1)} %copy.125) | copy-start | bytes 786436
  284.5 18.8 %copy-start.60 = (f32[4,128]{1,0:T(4,128)S(1)}, f32[4,128]{1,0:T(4,128)}, u32[]{:S(2)}) copy-start(f32[4,128]{1,0:T(4,128)} %log_add_fusion) | copy-start | bytes 6148
  309.1 11.9 %copy-start.15 = (bf16[4,128,1024]{2,1,0:T(8,128)(2,1)S(1)}, bf16[4,128,1024]{2,1,0:T(8,128)(2,1)}, u32[]{:S(2)}) copy-start(bf16[4,128,1024]{2,1,0:T(8,128)(2,1)} %get-tuple-element.46) | copy-start | bytes 3145732
  310.5 11.4 %copy-start.64 = (f32[32]{0:T(128)S(1)}, f32[32]{0:T(128)}, u32[]{:S(2)}) copy-start(f32[32]{0:T(128)} %copy-done.63) | copy-start | bytes 388
  310.5 11.4 %copy-start.70 = (f32[128]{0:T(128)S(1)}, f32[128]{0:T(128)}, u32[]{:S(2)}) copy-start(f32[128]{0:T(128)} %copy-done.69) | copy-start | bytes 1540
  321.0 18.3 %copy-start.59 = (f32[4,1,128]{2,1,0:T(1,128)S(1)}, f32[4,1,128]{2,1,0:T(1,128)}, u32[]{:S(2)}) copy-start(f32[4,1,128]{2,1,0:T(1,128)} %copy-done.58) | copy-start | bytes 6148
  321.1 18.3 %copy-start.71 = (f32[32]{0:T(128)S(1)}, f32[32]{0:T(128)}, u32[]{:S(2)}) copy-start(f32[32]{0:T(128)} %add_rsqrt_fusion.2) | copy-start | bytes 388
  321.1 19.4 %copy-start.77 = (f32[32]{0:T(128)S(1)}, f32[32]{0:T(128)}, u32[]{:S(2)}) copy-start(f32[32]{0:T(128)} %copy-done.76) | copy-start | bytes 388
  321.1 21.1 %copy-start.3 = (bf16[4,512,576]{2,1,0:T(8,128)(2,1)S(1)}, bf16[4,512,576]{2,1,0:T(8,128)(2,1)}, u32[]{:S(2)}) copy-start(bf16[4,512,576]{2,1,0:T(8,128)(2,1)} %get-tuple-element.45) | copy-start | bytes 7077892
  321.1 21.1 %copy-start.68 = (f32[32]{0:T(128)S(1)}, f32[32]{0:T(128)}, u32[]{:S(2)}) copy-start(f32[32]{0:T(128)} %get-tuple-element.155) | copy-start | bytes 388
  339.4 5.5 %copy-start.57 = (f32[2048]{0:T(1024)S(1)}, f32[2048]{0:T(1024)}, u32[]{:S(2)}) copy-start(f32[2048]{0:T(1024)} %get-tuple-element.118) | copy-start | bytes 24580
  339.4 20.7 %copy-start.73 = (f32[32]{0:T(128)S(1)}, f32[32]{0:T(128)}, u32[]{:S(2)}) copy-start(f32[32]{0:T(128)} %get-tuple-element.129) | copy-start | bytes 388
  339.4 20.7 %copy-start.33 = (f32[32,2048]{1,0:T(8,128)S(1)}, f32[32,2048]{1,0:T(8,128)}, u32[]{:S(2)}) copy-start(f32[32,2048]{1,0:T(8,128)} %get-tuple-element.123) | copy-start | bytes 786436
  342.2 30.0 %copy-start.13 = (bf16[128,2176]{1,0:T(8,128)(2,1)S(1)}, bf16[128,2176]{1,0:T(8,128)(2,1)}, u32[]{:S(2)}) copy-start(bf16[128,2176]{1,0:T(8,128)(2,1)} %mid_grad_gather.1) | copy-start | bytes 1671172
  344.3 29.9 %copy-start.41 = (bf16[128,512]{1,0:T(8,128)(2,1)S(1)}, bf16[128,512]{1,0:T(8,128)(2,1)}, u32[]{:S(2)}) copy-start(bf16[128,512]{1,0:T(8,128)(2,1)} %copy.120) | copy-start | bytes 393220
  344.3 29.9 %copy-start.29 = (bf16[3,88,2048]{2,1,0:T(8,128)(2,1)S(1)}, bf16[3,88,2048]{2,1,0:T(8,128)(2,1)}, u32[]{:S(2)}) copy-start(bf16[3,88,2048]{2,1,0:T(8,128)(2,1)} %get-tuple-element.56) | copy-start | bytes 3244036
  374.2 45.6 %copy-start.25 = (bf16[128,3072]{1,0:T(8,128)(2,1)}, bf16[128,3072]{1,0:T(8,128)(2,1)S(1)}, u32[]{:S(2)}) copy-start(bf16[128,3072]{1,0:T(8,128)(2,1)S(1)} %slice_dynamic-update-slice_fusion.refs_0_) | copy-start | bytes 2359300
  426.2 80.0 %copy-start.30 = (bf16[8,128,512]{2,1,0:T(8,128)(2,1)S(1)}, bf16[8,128,512]{2,1,0:T(8,128)(2,1)}, u32[]{:S(2)}) copy-start(bf16[8,128,512]{2,1,0:T(8,128)(2,1)} %get-tuple-element.61) | copy-start | bytes 3145732
  506.2 5.3 %copy-start.36 = (bf16[8,128,3072]{2,1,0:T(8,128)(2,1)S(1)}, bf16[8,128,3072]{2,1,0:T(8,128)(2,1)}, u32[]{:S(2)}) copy-start(bf16[8,128,3072]{2,1,0:T(8,128)(2,1)} %get-tuple-element.58) | copy-start | bytes 18874372
  514.6 8.2 %slice-start = ((s8[5767168]{0:T(1024)(128)(4,1)}), s8[4194304]{0:T(1024)(128)(4,1)S(1)}, s32[]{:S(2)}) async-start(s8[5767168]{0:T(1024)(128)(4,1)} %bitcast.134), calls=%async_computation | async-start | bytes 8388608
  518.1 4.6 slice-start.1
  (33 other events, 62.7 us)

commit v3 on v2

--- a/solution.py
+++ b/solution.py
@@ -87,30 +87,33 @@
         self.core = lax.rem(self.s, 2)
         self.y = self.s // 2
         self.n_tp = n_tp
-
-    def at(self, s, c, t):
-        return {SHARD: s, CTX: c, TP: t}
-
-    @property
-    def over_x(self):
-        return self.at(self.s, 1 - self.c, self.t)
-
-    @property
-    def over_y(self):
-        return self.at(lax.rem(self.s + 2, 4), self.c, self.t)
-
-    @property
-    def over_core(self):
-        return self.at(self.s + 1 - 2 * self.core, self.c, self.t)
+        self.over_x = self.flip(0, 0, 1)
+        self.over_y = self.flip(1, 0, 0)
+        self.over_core = self.flip(0, 1, 0)
 
     def along(self, step):
-        return self.at(self.s, self.c, lax.rem(self.t + step + self.n_tp, self.n_tp))
+        t = lax.rem(self.t + step + self.n_tp, self.n_tp)
+        return {SHARD: self.s, CTX: self.c, TP: t}
 
     def flip(self, dy, dcore, dx):
         y = self.y + dy * (1 - 2 * self.y)
         core = self.core + dcore * (1 - 2 * self.core)
         x = self.c + dx * (1 - 2 * self.c)
-        return self.at(2 * y + core, x, self.t)
+        return {SHARD: 2 * y + core, CTX: x, TP: self.t}
+
+    def peers(self, kinds):
+        flips = []
+        if "p" in kinds:
+            flips = FLIPS
+        else:
+            flips = [f for kind, f in (("x", FLIPS[0]), ("k", FLIPS[1]), ("y", FLIPS[3])) if kind in kinds]
+        out = [self.flip(*f) for f in flips]
+        if "z" in kinds:
+            out += [self.along(k) for k in range(1, self.n_tp)]
+        return out
+
+
+FLIPS = [(dy, dk, dx) for dy in (0, 1) for dk in (0, 1) for dx in (0, 1)][1:]
 
 
 def slot(s, c):
@@ -120,7 +123,7 @@
 class Net:
     def __init__(self, send, recv, local):
         self.send, self.recv, self.local = send, recv, local
-        self.puts, self.locals = [], []
+        self.puts = []
         self.n_local = 0
 
     def put(self, src, dst, to):
@@ -155,190 +158,186 @@
     pl.semaphore_wait(barrier, len(peers))
 
 
-def comm_call(body, ins, outs, scratch, n_put, n_local, collective_id, name, in_space, out_space):
-    return pl.pallas_call(
+class Job:
+    def __init__(self, run, ins, outs, scratch, n_put, n_local, peers):
+        self.run, self.ins, self.outs, self.scratch = run, ins, outs, scratch
+        self.n_put, self.n_local, self.peers = n_put, n_local, peers
+
+
+def comm_kernel(jobs, n_tp, collective_id, name):
+    ins = [i for job in jobs for i in job.ins]
+    outs = [o for job in jobs for o in job.outs]
+    scratch = [s for job in jobs for s in job.scratch]
+    n_put = sum(job.n_put for job in jobs)
+    n_local = max(sum(job.n_local for job in jobs), 1)
+    kinds = "".join(sorted(set("".join(job.peers for job in jobs))))
+
+    def body(*refs):
+        in_refs, out_refs = refs[: len(ins)], refs[len(ins) : len(ins) + len(outs)]
+        rest = refs[len(ins) + len(outs) :]
+        me = Place(n_tp)
+        net = Net(*rest[len(scratch) :])
+        greet(me.peers(kinds))
+        running = []
+        i = o = s = 0
+        for job in jobs:
+            ni, no, ns = len(job.ins), len(job.outs), len(job.scratch)
+            running.append(
+                job.run(net, me, in_refs[i : i + ni], out_refs[o : o + no], rest[s : s + ns])
+            )
+            i, o, s = i + ni, o + no, s + ns
+        while running:
+            running = [r for r in running if next(r, None) is not None]
+        net.finish()
+
+    got = pl.pallas_call(
         body,
-        out_shape=tuple(jax.ShapeDtypeStruct(shape, dtype) for shape, dtype in outs),
-        in_specs=[pl.BlockSpec(memory_space=space) for space in in_space],
-        out_specs=tuple(pl.BlockSpec(memory_space=space) for space in out_space),
+        out_shape=tuple(jax.ShapeDtypeStruct(shape, dtype) for shape, dtype, _ in outs),
+        in_specs=[pl.BlockSpec(memory_space=space) for _, space in ins],
+        out_specs=tuple(pl.BlockSpec(memory_space=space) for _, _, space in outs),
         scratch_shapes=[
             *scratch,
             pltpu.SemaphoreType.DMA((n_put,)),
             pltpu.SemaphoreType.DMA((n_put,)),
-            pltpu.SemaphoreType.DMA((max(n_local, 1),)),
+            pltpu.SemaphoreType.DMA((n_local,)),
         ],
         compiler_params=pltpu.CompilerParams(
             collective_id=collective_id, has_side_effects=True, vmem_limit_bytes=60 * 2**20
         ),
         name=name,
-    )(*ins)
-
-
-def start_gather(weights, small, block, n_tp):
-    shapes = [w.shape for w in weights]
-
-    def body(*refs):
+    )(*[a for a, _ in ins])
+    split, o = [], 0
+    for job in jobs:
+        split.append(got[o : o + len(job.outs)])
+        o += len(job.outs)
+    return split
+
+
+def shard_gather(weights, block):
+    shapes = [w.shape for w, _ in weights]
+    side = [by for _, by in weights]
+
+    def run(net, me, ins, outs, bounce):
         n = len(shapes)
-        w_in, (small_in, x_in) = refs[:n], refs[n : n + 2]
-        w_out, (small_out, x_out) = refs[n + 2 : 2 * n + 2], refs[2 * n + 2 : 2 * n + 4]
-        bounce = refs[2 * n + 4 : 3 * n + 6]
-        send, recv, local = refs[3 * n + 6 :]
-        me = Place(n_tp)
-        net = Net(send, recv, local)
-        greet([me.over_x, me.over_y, me.over_core])
-
-        def half(ref, index, which, rows):
-            return ref.at[index, pl.ds(which * (rows // 2), rows // 2)]
-
+        x_in, x_out = ins[n], outs[n]
         other = lax.rem(me.s + 2, 4)
-        loads = [net.move(src, b) for src, b in zip((*w_in, small_in, x_in), bounce)]
+
+        def place(i, s, which=None):
+            rows, cols = shapes[i]
+            at = pl.ds(0, rows)
+            if which is not None:
+                at = pl.ds(pl.multiple_of(which * (rows // 2), rows // 2), rows // 2)
+            if side[i]:
+                return outs[i].at[at, pl.ds(pl.multiple_of(s * cols, LANES), cols)]
+            return outs[i].at[s, at]
+
+        loads = [net.move(src, b) for src, b in zip(ins, bounce)]
         from_y, own = [], []
-        for ref, out, shape in zip(w_in, w_out, shapes):
-            rows = shape[0]
-            from_y.append(
-                net.put(ref.at[pl.ds(me.c * (rows // 2), rows // 2)], half(out, me.s, me.c, rows), me.over_y)
-            )
-            if ref is w_in[0]:
+        for i in range(n):
+            rows = shapes[i][0]
+            at = pl.ds(pl.multiple_of(me.c * (rows // 2), rows // 2), rows // 2)
+            from_y.append(net.put(ins[i].at[at], place(i, me.s, me.c), me.over_y))
+            if i == 0:
                 wait_x = net.put(x_in, x_out.at[me.c], me.over_x)
-        for ref, out in zip(w_in, w_out):
-            own.append(net.put(ref, out.at[me.s], me.over_core))
-        small_y = net.put(small_in, small_out.at[me.s], me.over_y)
-        small_c = net.put(small_in, small_out.at[me.s], me.over_core)
+        for i in range(n):
+            own.append(net.put(ins[i], place(i, me.s), me.over_core))
+        yield 1
         stores = []
-        outs = [o.at[me.s] for o in (*w_out, small_out)] + [x_out.at[me.c]]
-        for load, b, out in zip(loads, bounce, outs):
+        for i, (load, b) in enumerate(zip(loads, bounce)):
             load.wait()
-            stores.append(net.move(b, out))
+            stores.append(net.move(b, place(i, me.s) if i < n else x_out.at[me.c]))
         from_x, relays = [], []
-        for got, out, shape in zip(from_y, w_out, shapes):
-            rows = shape[0]
-            got.wait_recv()
-            piece = half(out, other, me.c, rows)
+        for i in range(n):
+            from_y[i].wait_recv()
+            piece = place(i, other, me.c)
             from_x.append(net.put(piece, piece, me.over_x))
             relays.append(net.put(piece, piece, me.over_core))
-        small_y.wait_recv()
-        relays.append(net.put(small_out.at[other], small_out.at[other], me.over_core))
-        for got, out, shape in zip(from_x, w_out, shapes):
-            rows = shape[0]
-            got.wait_recv()
-            piece = half(out, other, 1 - me.c, rows)
+            yield 1
+        for i in range(n):
+            from_x[i].wait_recv()
+            piece = place(i, other, 1 - me.c)
             relays.append(net.put(piece, piece, me.over_core))
+            yield 1
         wait_x.wait_recv()
-        small_c.wait_recv()
         for got in own + relays:
             got.wait_recv()
         for store in stores:
             store.wait()
-        net.finish()
 
     n = len(weights)
-    outs = [((4, *w.shape), BF) for w in weights] + [((4, *small.shape), small.dtype), ((2, *block.shape), BF)]
-    return comm_call(
-        body,
-        (*weights, small, block),
+    outs = []
+    for (rows, cols), by in zip(shapes, side):
+        outs.append(((rows, 4 * cols) if by else (4, rows, cols), BF, ANY))
+    outs.append(((2, *block.shape), BF, ANY))
+    return Job(
+        run,
+        [(w, ANY) for w, _ in weights] + [(block, ANY)],
         outs,
-        [VMEM(w.shape, w.dtype) for w in (*weights, small, block)],
-        5 * n + 4,
-        2 * n + 4,
-        0,
-        "start_gather",
-        [ANY] * (n + 2),
-        [ANY] * (n + 2),
-    )
-
-
-def tp_reduce_scatter(part, n_tp, collective_id, name):
+        [VMEM(w.shape, w.dtype) for w, _ in weights] + [VMEM(block.shape, BF)],
+        5 * n + 1,
+        2 * n + 2,
+        "xyk",
+    )
+
+
+def tp_reduce_scatter(part, n_tp):
     rows, width = part.shape
     piece = rows // n_tp
 
-    def body(in_ref, out_ref, got, send, recv, local):
-        me = Place(n_tp)
-        net = Net(send, recv, local)
-        greet([me.along(k) for k in range(1, n_tp)])
+    def run(net, me, ins, outs, scratch):
+        (src,), (out,), (got,) = ins, outs, scratch
         waits = []
         for k in range(1, n_tp):
-            to = lax.rem(me.t + k, n_tp)
-            waits.append(
-                net.put(in_ref.at[pl.ds(to * piece, piece)], got.at[k - 1], me.along(k))
-            )
+            to = pl.multiple_of(lax.rem(me.t + k, n_tp) * piece, piece)
+            waits.append(net.put(src.at[pl.ds(to, piece)], got.at[k - 1], me.along(k)))
+        yield 1
         for wait in waits:
             wait.wait_recv()
-        total = in_ref[pl.ds(pl.multiple_of(me.t * piece, piece), piece), :].astype(F32)
+        total = src[pl.ds(pl.multiple_of(me.t * piece, piece), piece), :].astype(F32)
         for k in range(1, n_tp):
             total = total + got[k - 1].astype(F32)
-        out_ref[...] = total
-        net.finish()
-
-    return comm_call(
-        body,
-        (part,),
-        [((piece, width), F32)],
+        out[...] = total
+
+    return Job(
+        run,
+        [(part, VMEM)],
+        [((piece, width), F32, VMEM)],
         [VMEM((n_tp - 1, piece, width), BF)],
         n_tp - 1,
         0,
-        collective_id,
-        name,
-        [VMEM],
-        [VMEM],
-    )[0]
-
-
-def tp_ring(net, me, own, out, base):
-    piece = own.shape[0]
-    half = piece // 2
-
-    def rows(p, which=None):
-        start = base + p * piece
-        if which is None:
-            return out.at[pl.ds(start, piece)]
-        return out.at[pl.ds(start + which * half, half)]
-
-    right, left = me.along(1), me.along(-1)
-    p_left, p_right = lax.rem(me.t + 3, 4), lax.rem(me.t + 1, 4)
-    far = lax.rem(me.t + 2, 4)
-    to_right = net.put(own, rows(me.t), right)
-    to_left = net.put(own, rows(me.t), left)
-    to_right.wait_recv()
-    hop_right = net.put(rows(p_left, 0), rows(p_left, 0), right)
-    yield p_left
-    to_left.wait_recv()
-    hop_left = net.put(rows(p_right, 1), rows(p_right, 1), left)
-    yield p_right
-    hop_right.wait_recv()
-    hop_left.wait_recv()
-    yield far
-
-
-def tp_all_gather(pieces, n_tp, collective_id, name):
-    def body(*refs):
-        n = len(pieces)
-        ins, outs, (send, recv, local) = refs[:n], refs[n : 2 * n], refs[2 * n :]
-        me = Place(n_tp)
-        net = Net(send, recv, local)
-        greet([me.along(1), me.along(-1)])
-        rings = []
-        for src, dst in zip(ins, outs):
-            size = src.shape[0]
-            rings.append(tp_ring(net, me, src, dst, 0))
-        for _ in range(3):
-            for ring in rings:
-                next(ring)
-        for src, dst in zip(ins, outs):
-            size = src.shape[0]
-            dst[pl.ds(pl.multiple_of(me.t * size, size), size), :] = src[...]
-        net.finish()
-
-    return comm_call(
-        body,
-        pieces,
-        [((n_tp * p.shape[0], p.shape[1]), p.dtype) for p in pieces],
-        [],
-        4 * len(pieces),
-        0,
-        collective_id,
-        name,
-        [VMEM] * len(pieces),
-        [VMEM] * len(pieces),
+        "z",
+    )
+
+
+def tp_all_gather(own, n_tp):
+    size, width = own.shape
+    half = size // 2
+
+    def run(net, me, ins, outs, scratch):
+        (src,), (out,) = ins, outs
+
+        def rows(p, which=None):
+            if which is None:
+                return out.at[pl.ds(pl.multiple_of(p * size, size), size)]
+            return out.at[pl.ds(pl.multiple_of(p * size + which * half, half), half)]
+
+        right, left = me.along(1), me.along(-1)
+        p_left, p_right = lax.rem(me.t + 3, 4), lax.rem(me.t + 1, 4)
+        to_right = net.put(src, rows(me.t), right)
+        to_left = net.put(src, rows(me.t), left)
+        out[pl.ds(pl.multiple_of(me.t * size, size), size), :] = src[...]
+        yield 1
+        to_right.wait_recv()
+        hop_right = net.put(rows(p_left, 0), rows(p_left, 0), right)
+        to_left.wait_recv()
+        hop_left = net.put(rows(p_right, 1), rows(p_right, 1), left)
+        yield 1
+        yield 1
+        hop_right.wait_recv()
+        hop_left.wait_recv()
+
+    return Job(
+        run, [(own, VMEM)], [((n_tp * size, width), own.dtype, VMEM)], [], 4, 0, "z"
     )
 
 
@@ -349,7 +348,7 @@
     relay_slot = first * g_x + me.core * g_y
     relay_to = me.flip(first, 0, me.core)
     diags, waits = [], []
-    for from_x, from_y, (start, size) in chunks:
+    for from_x, from_y, start, size in chunks:
         from_x.wait_recv()
         from_y.wait_recv()
         src = out.at[relay_slot, pl.ds(start, size)]
@@ -357,205 +356,187 @@
         for g in (g_x, g_y):
             piece = out.at[g, pl.ds(start, size)]
             waits.append(net.put(piece, piece, me.over_core))
-    for diag, (_, _, (start, size)) in zip(diags, chunks):
+        yield 1
+    for diag, (_, _, start, size) in zip(diags, chunks):
         diag.wait_recv()
         piece = out.at[g_d, pl.ds(start, size)]
         waits.append(net.put(piece, piece, me.over_core))
-    return waits
-
-
-def gather_everywhere(own, n_tp, collective_id, name):
-    piece, width = own.shape
-
-    def body(in_ref, out_ref, bounce, send, recv, local):
-        me = Place(n_tp)
-        net = Net(send, recv, local)
-        greet([me.over_x, me.over_y, me.over_core, me.along(1), me.along(-1)])
-        load = net.move(in_ref, bounce)
+        yield 1
+    for wait in waits:
+        wait.wait_recv()
+
+
+def plane_gather(own, n_chunk=4):
+    rows, width = own.shape
+    size = rows // n_chunk
+
+    def run(net, me, ins, outs, scratch):
+        (src,), (out,), (bounce,) = ins, outs, scratch
         g_me = slot(me.s, me.c)
+        load = net.move(src, bounce)
         chunks, cores = [], []
-
-        def spread(src, p):
-            dst = out_ref.at[g_me, pl.ds(p * piece, piece)]
-            from_x = net.put(src, dst, me.over_x)
-            from_y = net.put(src, dst, me.over_y)
-            cores.append(net.put(src, dst, me.over_core))
-            chunks.append((from_x, from_y, (p * piece, piece)))
-
-        spread(in_ref, me.t)
-        ring = tp_ring(net, me, in_ref, out_ref.at[g_me], 0)
+        for j in range(n_chunk):
+            part = src.at[pl.ds(j * size, size)]
+            to = out.at[g_me, pl.ds(j * size, size)]
+            chunks.append(
+                (net.put(part, to, me.over_x), net.put(part, to, me.over_y), j * size, size)
+            )
+            cores.append(net.put(part, to, me.over_core))
+        yield 1
         load.wait()
-        store = net.move(bounce, out_ref.at[g_me, pl.ds(me.t * piece, piece)])
-        for p in ring:
-            spread(out_ref.at[g_me, pl.ds(p * piece, piece)], p)
-        waits = cores + relay_chunks(net, me, out_ref, chunks)
+        store = net.move(bounce, out.at[g_me])
+        yield from relay_chunks(net, me, out, chunks)
+        for core in cores:
+            core.wait_recv()
+        store.wait()
+
+    return Job(
+        run,
+        [(own, ANY)],
+        [((8, rows, width), own.dtype, ANY)],
+        [VMEM(own.shape, own.dtype)],
+        7 * n_chunk,
+        2,
+        "xyk",
+    )
+
+
+def plane_columns(array):
+    rows, width = array.shape
+    w = width // 4
+
+    def run(net, me, ins, outs, scratch):
+        (src,), (out,), (bounce,) = ins, outs, scratch
+        g_me = slot(me.s, me.c)
+
+        def cols(s):
+            return src.at[:, pl.ds(pl.multiple_of(s * w, LANES), w)]
+
+        load = net.move(cols(me.s), bounce)
+        waits = []
+        for f in FLIPS:
+            peer = me.flip(*f)
+            waits.append(net.put(cols(peer[SHARD]), out.at[g_me], peer))
+        yield 1
+        load.wait()
+        store = net.move(bounce, out.at[g_me])
+        for wait in waits:
+            yield 1
+            wait.wait_recv()
+        store.wait()
+
+    return Job(
+        run,
+        [(array, ANY)],
+        [((8, rows, w), array.dtype, ANY)],
+        [VMEM((rows, w), array.dtype)],
+        7,
+        2,
+        "p",
+    )
+
+
+def shard_rows(array):
+    h, w = array.shape[0] // 8, array.shape[1]
+
+    def run(net, me, ins, outs, scratch):
+        (src,), (out,), (bounce,) = ins, outs, scratch
+
+        def rows(s):
+            return src.at[pl.ds(pl.multiple_of(slot(s, me.c) * h, 8), h)]
+
+        to = out.at[:, pl.ds(pl.multiple_of(me.s * w, LANES), w)]
+        load = net.move(rows(me.s), bounce)
+        waits = []
+        for f in FLIPS:
+            if f[2] == 0:
+                peer = me.flip(*f)
+                waits.append(net.put(rows(peer[SHARD]), to, peer))
+        yield 1
+        load.wait()
+        store = net.move(bounce, to)
+        yield 1
         for wait in waits:
             wait.wait_recv()
         store.wait()
-        net.finish()
-
-    return comm_call(
-        body,
-        (own,),
-        [((8, n_tp * piece, width), own.dtype)],
-        [VMEM(own.shape, own.dtype)],
-        4 * 7 + 4,
+
+    return Job(
+        run,
+        [(array, ANY)],
+        [((h, 4 * w), array.dtype, ANY)],
+        [VMEM((h, w), array.dtype)],
+        3,
         2,
-        collective_id,
-        name,
-        [ANY],
-        [ANY],
-    )[0]
-
-
-def plane_exchange(gathers, columns, rows88, n_tp, collective_id, name, n_chunk=4):
-    ng, nc, nr = len(gathers), len(columns), len(rows88)
-    ins = (*gathers, *columns, *rows88)
-
-    def body(*refs):
-        n = ng + nc + nr
-        src, dst, bounce = refs[:n], refs[n : 2 * n], refs[2 * n : 3 * n]
-        send, recv, local = refs[3 * n :]
-        me = Place(n_tp)
-        net = Net(send, recv, local)
-        flips = [(dy, dk, dx) for dy in (0, 1) for dk in (0, 1) for dx in (0, 1)][1:]
-        if nc or nr:
-            greet([me.flip(*f) for f in flips])
-        else:
-            greet([me.over_x, me.over_y, me.over_core])
-        g_me = slot(me.s, me.c)
-        loads, waits, work = [], [], []
-        for i in range(n):
-            s, d, b = src[i], dst[i], bounce[i]
-            if i < ng:
-                rows = s.shape[0]
-                size = rows // n_chunk
-                chunks = []
-                for j in range(n_chunk):
-                    part = s.at[pl.ds(j * size, size)]
-                    to = d.at[g_me, pl.ds(j * size, size)]
-                    chunks.append((net.put(part, to, me.over_x), net.put(part, to, me.over_y), (j * size, size)))
-                    waits.append(net.put(part, to, me.over_core))
-                work.append((d, chunks))
-                loads.append((net.move(s, b), b, d.at[g_me]))
-            elif i < ng + nc:
-                w = s.shape[1] // 4
-                for f in flips:
-                    peer = me.flip(*f)
-                    part = s.at[:, pl.ds(pl.multiple_of(peer[SHARD] * w, LANES), w)]
-                    waits.append(net.put(part, d.at[g_me], peer))
-                part = s.at[:, pl.ds(pl.multiple_of(me.s * w, LANES), w)]
-                loads.append((net.move(part, b), b, d.at[g_me]))
-            else:
-                h, w = s.shape[0] // 8, s.shape[1]
-                to = d.at[:, pl.ds(pl.multiple_of(me.s * w, LANES), w)]
-                for f in ((0, 1, 0), (1, 0, 0), (1, 1, 0)):
-                    peer = me.flip(*f)
-                    row = pl.multiple_of(slot(peer[SHARD], peer[CTX]) * h, 8)
-                    waits.append(net.put(s.at[pl.ds(row, h)], to, peer))
-                row = pl.multiple_of(g_me * h, 8)
-                loads.append((net.move(s.at[pl.ds(row, h)], b), b, to))
-        stores = []
-        for load, b, to in loads:
-            load.wait()
-            stores.append(net.move(b, to))
-        for d, chunks in work:
-            waits += relay_chunks(net, me, d, chunks)
-        for wait in waits:
-            wait.wait_recv()
-        for store in stores:
-            store.wait()
-        net.finish()
-
-    outs, scratch = [], []
-    for a in gathers:
-        outs.append(((8, *a.shape), a.dtype))
-        scratch.append(VMEM(a.shape, a.dtype))
-    for a in columns:
-        outs.append(((8, a.shape[0], a.shape[1] // 4), a.dtype))
-        scratch.append(VMEM((a.shape[0], a.shape[1] // 4), a.dtype))
-    for a in rows88:
-        outs.append(((a.shape[0] // 8, a.shape[1] * 4), a.dtype))
-        scratch.append(VMEM((a.shape[0] // 8, a.shape[1]), a.dtype))
-    return comm_call(
-        body,
-        ins,
-        outs,
-        scratch,
-        ng * 7 * n_chunk + nc * 7 + nr * 3,
-        2 * len(ins),
-        collective_id,
-        name,
-        [ANY] * len(ins),
-        [ANY] * len(ins),
-    )
-
-
-def ctx_swap(block, collective_id, name):
-    def body(in_ref, out_ref, send, recv, local):
-        me = Place(1)
-        net = Net(send, recv, local)
-        greet([me.over_x])
-        net.put(in_ref, out_ref, me.over_x).wait_recv()
-        net.finish()
-
-    return comm_call(
-        body, (block,), [(block.shape, block.dtype)], [], 1, 0, collective_id, name, [ANY], [ANY]
-    )[0]
-
-
-def reduce_everywhere(part, n_tp, collective_id, name):
-    _, rows, width = part.shape
+        "p",
+    )
+
+
+def ctx_swap(block):
+    def run(net, me, ins, outs, scratch):
+        (src,), (out,) = ins, outs
+        got = net.put(src, out, me.over_x)
+        yield 1
+        yield 1
+        got.wait_recv()
+
+    return Job(run, [(block, ANY)], [(block.shape, block.dtype, ANY)], [], 1, 0, "x")
+
+
+def reduce_everywhere(part, n_tp):
+    tokens, width = part.shape
+    rows = tokens // 8
     half = width // 2
     piece = rows // n_tp
     step = 16
 
-    def body(in_ref, out_ref, mine, rc, rx, ry, q0, q1, r0, r1, last, got, send, recv, local):
-        me = Place(n_tp)
-        net = Net(send, recv, local)
-        greet([me.over_x, me.over_y, me.over_core] + [me.along(k) for k in range(1, n_tp)])
+    def run(net, me, ins, outs, scratch):
+        (src,), (out,) = ins, outs
+        mine, rc, rx, ry, q0, q1, r0, r1, last, got = scratch
         a, b = pl.ds(0, half), pl.ds(half, half)
         order = [(1, 1), (0, 1), (1, 0), (0, 0)]
-        pairs = []
+        chips, loads, cores = [], [], []
         for dy, dx in order:
-            y, x = me.y + dy * (1 - 2 * me.y), me.c + dx * (1 - 2 * me.c)
-            pairs.append((2 * y + x, slot(2 * y + me.core, x), slot(2 * y + 1 - me.core, x)))
-        loads, cores = [], []
-        for i, g_mine, g_other in pairs:
-            cores.append(net.put(in_ref.at[g_other], rc.at[i], me.over_core))
-            loads.append(net.move(in_ref.at[g_mine], mine.at[i]))
+            ch = 2 * (me.y + dy * (1 - 2 * me.y)) + me.c + dx * (1 - 2 * me.c)
+            chips.append(ch)
+            base = ch * 2 * rows
+            theirs = src.at[pl.ds(pl.multiple_of(base + (1 - me.core) * rows, rows), rows)]
+            ours = src.at[pl.ds(pl.multiple_of(base + me.core * rows, rows), rows)]
+            cores.append(net.put(theirs, rc.at[ch], me.over_core))
+            loads.append(net.move(ours, mine.at[ch]))
+        yield 1
 
         def add(target, cols, left, right):
             def one(r, carry):
                 at = pl.ds(pl.multiple_of(r * step, step), step)
-                total = left(at).astype(F32) + right(at).astype(F32)
-                target[at, cols] = total.astype(target.dtype)
+                target[at, cols] = (left(at).astype(F32) + right(at).astype(F32)).astype(BF)
                 return carry
 
             lax.fori_loop(0, rows // step, one, 0)
 
         def sum_cores(k):
-            i = pairs[k][0]
+            ch = chips[k]
             loads[k].wait()
             cores[k].wait_recv()
-            add(mine.at[i], pl.ds(0, width), lambda at: mine[i, at, :], lambda at: rc[i, at, :])
-            return i
-
-        i_yx = sum_cores(0)
-        ax0 = net.put(mine.at[i_yx, :, a], rx.at[1 - me.y], me.over_x)
-        by0 = net.put(mine.at[i_yx, :, b], ry.at[1 - me.c], me.over_y)
-        i_x = sum_cores(1)
-        ax1 = net.put(mine.at[i_x, :, a], rx.at[me.y], me.over_x)
-        i_y = sum_cores(2)
-        by1 = net.put(mine.at[i_y, :, b], ry.at[me.c], me.over_y)
-        i_me = sum_cores(3)
+            add(mine.at[ch], pl.ds(0, width), lambda at: mine[ch, at, :], lambda at: rc[ch, at, :])
+            return ch
+
+        c_d = sum_cores(0)
+        ax0 = net.put(mine.at[c_d, :, a], rx.at[0], me.over_x)
+        by0 = net.put(mine.at[c_d, :, b], ry.at[0], me.over_y)
+        c_x = sum_cores(1)
+        ax1 = net.put(mine.at[c_x, :, a], rx.at[1], me.over_x)
+        c_y = sum_cores(2)
+        by1 = net.put(mine.at[c_y, :, b], ry.at[1], me.over_y)
+        c_me = sum_cores(3)
+        yield 1
         every = pl.ds(0, half)
         ax0.wait_recv()
-        add(q0, every, lambda at: mine[i_y, at, a], lambda at: rx[1 - me.y, at, :])
+        add(q0, every, lambda at: mine[c_y, at, a], lambda at: rx[0, at, :])
         y0 = net.put(q0, r0, me.over_y)
         by0.wait_recv()
-        add(q1, every, lambda at: mine[i_x, at, b], lambda at: ry[1 - me.c, at, :])
+        add(q1, every, lambda at: mine[c_x, at, b], lambda at: ry[0, at, :])
         x1 = net.put(q1, r1, me.over_x)
+        yield 1
         ax1.wait_recv()
         by1.wait_recv()
         y0.wait_recv()
@@ -563,8 +544,8 @@
 
         def final(r, carry):
             at = pl.ds(pl.multiple_of(r * step, step), step)
-            left = mine[i_me, at, a].astype(F32) + rx[me.y, at, :].astype(F32) + r0[at, :].astype(F32)
-            right = mine[i_me, at, b].astype(F32) + ry[me.c, at, :].astype(F32) + r1[at, :].astype(F32)
+            left = mine[c_me, at, a].astype(F32) + rx[1, at, :].astype(F32) + r0[at, :].astype(F32)
+            right = mine[c_me, at, b].astype(F32) + ry[1, at, :].astype(F32) + r1[at, :].astype(F32)
             last[at, a] = left.astype(BF)
             last[at, b] = right.astype(BF)
             return carry
@@ -572,8 +553,9 @@
         lax.fori_loop(0, rows // step, final, 0)
         waits = []
         for k in range(1, n_tp):
-            to = lax.rem(me.t + k, n_tp)
-            waits.append(net.put(last.at[pl.ds(to * piece, piece)], got.at[k - 1], me.along(k)))
+            to = pl.multiple_of(lax.rem(me.t + k, n_tp) * piece, piece)
+            waits.append(net.put(last.at[pl.ds(to, piece)], got.at[k - 1], me.along(k)))
+        yield 1
         for wait in waits:
             wait.wait_recv()
         for r in range(piece // step):
@@ -581,14 +563,13 @@
             total = last[at, :].astype(F32)
             for k in range(n_tp - 1):
                 total = total + got[k, r * step : (r + 1) * step, :].astype(F32)
-            out_ref[r * step : (r + 1) * step, :] = total
-        net.finish()
+            out[r * step : (r + 1) * step, :] = total
 
     block = (rows, width)
-    return comm_call(
-        body,
-        (part,),
-        [((piece, width), F32)],
+    return Job(
+        run,
+        [(part, ANY)],
+        [((piece, width), F32, VMEM)],
         [
             VMEM((4, *block), BF),
             VMEM((4, *block), BF),
@@ -603,52 +584,104 @@
         ],
         10 + n_tp - 1,
         4,
-        collective_id,
-        name,
-        [ANY],
-        [VMEM],
-    )[0]
-
-
-def sum_everywhere(part, n_tp, collective_id, name):
-    def body(in_ref, out_ref, from_tp, mid, from_plane, send, recv, local):
-        me = Place(n_tp)
-        net = Net(send, recv, local)
-        flips = [(dy, dk, dx) for dy in (0, 1) for dk in (0, 1) for dx in (0, 1)][1:]
-        greet([me.along(k) for k in range(1, n_tp)] + [me.flip(*f) for f in flips])
-        waits = [net.put(in_ref, from_tp.at[k - 1], me.along(k)) for k in range(1, n_tp)]
+        "xykz",
+    )
+
+
+def sum_everywhere(part, n_tp):
+    def run(net, me, ins, outs, scratch):
+        (src,), (out,) = ins, outs
+        from_tp, mid, from_plane = scratch
+        waits = [net.put(src, from_tp.at[k - 1], me.along(k)) for k in range(1, n_tp)]
+        yield 1
         for wait in waits:
             wait.wait_recv()
-        total = in_ref[...]
+        total = src[...]
         for k in range(n_tp - 1):
             total = total + from_tp[k]
         mid[...] = total
-        waits = [net.put(mid, from_plane.at[i], me.flip(*f)) for i, f in enumerate(flips)]
+        waits = [net.put(mid, from_plane.at[i], me.flip(*f)) for i, f in enumerate(FLIPS)]
+        yield 1
+        yield 1
         for wait in waits:
             wait.wait_recv()
+        total = mid[...]
         for i in range(7):
             total = total + from_plane[i]
-        out_ref[...] = total
-        net.finish()
-
-    return comm_call(
-        body,
-        (part,),
-        [(part.shape, F32)],
+        out[...] = total
+
+    return Job(
+        run,
+        [(part, VMEM)],
+        [(part.shape, F32, VMEM)],
         [VMEM((n_tp - 1, *part.shape), F32), VMEM(part.shape, F32), VMEM((7, *part.shape), F32)],
         n_tp - 1 + 7,
         0,
-        collective_id,
-        name,
-        [VMEM],
-        [VMEM],
-    )[0]
+        "zp",
+    )
+
+
+def gather_rows(own, n_tp):
+    piece, width = own.shape
+    half = piece // 2
+
+    def run(net, me, ins, outs, scratch):
+        (src,), (out,), (bounce,) = ins, outs, scratch
+        load = net.move(src, bounce)
+        g_me = slot(me.s, me.c)
+        chunks, cores = [], []
+
+        def rows(p, which=None):
+            if which is None:
+                return out.at[g_me, pl.ds(pl.multiple_of(p * piece, piece), piece)]
+            return out.at[g_me, pl.ds(pl.multiple_of(p * piece + which * half, half), half)]
+
+        def spread(ref, p):
+            dst = rows(p)
+            chunks.append(
+                (net.put(ref, dst, me.over_x), net.put(ref, dst, me.over_y), pl.multiple_of(p * piece, piece), piece)
+            )
+            cores.append(net.put(ref, dst, me.over_core))
+
+        right, left = me.along(1), me.along(-1)
+        p_left, p_right = lax.rem(me.t + 3, 4), lax.rem(me.t + 1, 4)
+        far = lax.rem(me.t + 2, 4)
+        to_right = net.put(src, rows(me.t), right)
+        to_left = net.put(src, rows(me.t), left)
+        spread(src, me.t)
+        load.wait()
+        store = net.move(bounce, rows(me.t))
+        yield 1
+        to_right.wait_recv()
+        hop_right = net.put(rows(p_left, 0), rows(p_left, 0), right)
+        spread(rows(p_left), p_left)
+        to_left.wait_recv()
+        hop_left = net.put(rows(p_right, 1), rows(p_right, 1), left)
+        spread(rows(p_right), p_right)
+        yield 1
+        hop_right.wait_recv()
+        hop_left.wait_recv()
+        spread(rows(far), far)
+        yield from relay_chunks(net, me, out, chunks)
+        for core in cores:
+            core.wait_recv()
+        store.wait()
+
+    return Job(
+        run,
+        [(own, ANY)],
+        [((8, n_tp * piece, width), own.dtype, ANY)],
+        [VMEM(own.shape, own.dtype)],
+        4 * 7 + 4,
+        2,
+        "xykz",
+    )
 
 
 class Wire:
     def __init__(self, net, build):
-        self.net, self.build, self.i = net, build, net.wires
-        net.wires += 1
+        self.net, self.build, self.i = net, build, len(net.all)
+        net.all.append(self)
 
     def copy(self):
         src, dst, to = self.build()
@@ -673,32 +706,49 @@
 
 class Wires:
     def __init__(self, send, recv):
-        self.send, self.recv, self.wires, self.all = send, recv, 0, []
+        self.send, self.recv, self.all = send, recv, []
 
     def wire(self, build):
-        made = Wire(self, build)
-        self.all.append(made)
-        return made
-
-
-def feed_forward(two_own, cot_all, gate, up, down, sg_t, su_t, sd, w_router, experts, topk, n_tp):
+        return Wire(self, build)
+
+
+def padded(count, to=LANES):
+    return -(-count // to) * to
+
+
+def feed_forward(
+    two_own, mid_own, cot_own, gain_two, cot_all, gate, up, down, sg_t, su_t, sd, router_t, attn, normed, latent, topk, n_tp
+):
     piece, width = two_own.shape
     rows = piece * n_tp
     tokens = 8 * rows
     pack = cot_all.shape[-1]
-    hid, hid_s = gate.shape[2], sg_t.shape[0]
+    hid, hid_s = gate.shape[1], sg_t.shape[0]
+    experts = router_t.shape[0]
+    used = 2 * hid + hid_s
+    H = padded(used)
+    tile = H - LANES
+    off = used - tile
     edge = width // 2
     part_w = width + LANES
     group = 2 * rows
     shard_w = width // 4
-    n_wires = 4 + 12 + 16 + 4 + 6 + (n_tp - 1)
+    lat_w = latent.shape[1] // 4
+    attn_w = attn.shape[1]
+    n_wires = 4 + 12 + 16 + 4 + 6 + (n_tp - 1) + 7 + 14 + 4
+    n_col = 4
+    col_w = width // n_col
+    m_w = 256
+    n_m = width // m_w
 
     def body(*refs):
-        (two_ref, cot_ref, gate_ref, up_ref, down_ref, sg_ref, su_ref, sd_ref, wr_ref) = refs[:9]
-        (two_out, y_out, dg_out, du_out, dd_out, ds_out, n2_out) = refs[9:16]
-        (nb, cb, wg, wu, wd, ws, wr, hwe, gge, uue, hws, ggs, uus, dnb, yb) = refs[16:31]
-        (rc, rxa, ryb, q0, q1, r0, r1, last, got, dgs, dds, dss) = refs[31:43]
-        send, recv, load, store = refs[43:]
+        (two_ref, mid_ref, cot_own_ref, gain_ref) = refs[:4]
+        (cot_ref, gate_ref, up_ref, down_ref, sg_ref, su_ref, sd_ref, wr_ref, attn_ref, one_ref, lat_ref) = refs[4:15]
+        (mid_out, gain_out, mid_pack, ya_out, yb_out, dg_out, du_out, dd_out, ds_out, n2_out) = refs[15:25]
+        (attn_out, one_out, lat_out) = refs[25:28]
+        (nb, cb, wgu, wd, gu, gut, hw, hwt, dnb, yb) = refs[28:38]
+        (rc, rxa, ryb, q0, q1, r0, r1, last, got, gus, dds, dss) = refs[38:50]
+        send, recv, load, store = refs[50:]
         me = Place(n_tp)
         net = Wires(send, recv)
 
@@ -712,8 +762,10 @@
             return pl.ds(pl.multiple_of(start + p * piece, piece), piece)
 
         here = chip(0, 0)
+        g_me = slot(me.s, me.c)
         pieces = [me.t, lax.rem(me.t + 3, 4), lax.rem(me.t + 1, 4), lax.rem(me.t + 2, 4)]
         half = piece // 2
+        right, left = me.along(1), me.along(-1)
 
         def halves(p, which):
             start = here * group + me.core * rows + p * piece + which * half
@@ -722,7 +774,6 @@
         def mine(p):
             return nb.at[block(here, me.core, p)]
 
-        right, left = me.along(1), me.along(-1)
         z_r = net.wire(lambda: (two_ref, mine(me.t), right))
         z_l = net.wire(lambda: (two_ref, mine(me.t), left))
         hop_r = net.wire(lambda: (halves(pieces[1], 0), halves(pieces[1], 0), right))
@@ -744,6 +795,31 @@
             fwd_x.append(net.wire(lambda same=same: (same(chip_x), same(chip_x), me.over_core)))
             fwd_y.append(net.wire(lambda same=same: (same(chip_y), same(chip_y), me.over_core)))
             fwd_d.append(net.wire(lambda same=same: (same(chip_d), same(chip_d), me.over_core)))
+
+        g_x, g_y = slot(me.s, 1 - me.c), slot(lax.rem(me.s + 2, 4), me.c)
+        g_d = slot(lax.rem(me.s + 2, 4), 1 - me.c)
+        g_relay = first * g_x + me.core * g_y
+        at_direct = [
+            net.wire(lambda to=to: (attn_ref, attn_out.at[g_me], to))
+            for to in (me.over_x, me.over_y, me.over_core)
+        ]
+        at_relay = net.wire(lambda: (attn_out.at[g_relay], attn_out.at[g_relay], relay_to))
+        at_fwd = [
+            net.wire(lambda g=g: (attn_out.at[g], attn_out.at[g], me.over_core)) for g in (g_x, g_y, g_d)
+        ]
+        cols_w = []
+        for f in FLIPS:
+            peer = me.flip(*f)
+            for src, dst, w in ((one_ref, one_out, shard_w), (lat_ref, lat_out, lat_w)):
+                cols_w.append(
+                    net.wire(
+                        lambda src=src, dst=dst, w=w, peer=peer: (
+                            src.at[:, pl.ds(pl.multiple_of(peer[SHARD] * w, LANES), w)],
+                            dst.at[g_me],
+                            peer,
+                        )
+                    )
+                )
 
         a, b = pl.ds(0, edge), pl.ds(edge, part_w - edge)
         flips = [(0, 0), (0, 1), (1, 0), (1, 1)]
@@ -772,23 +848,41 @@
                 )
             )
 
-        loads = [
-            pltpu.make_async_copy(src, dst, load.at[i])
-            for i, (src, dst) in enumerate(
-                [(down_ref, wd), (gate_ref, wg), (up_ref, wu), (wr_ref, wr)]
-                + [(ref, ws.at[i]) for i, ref in enumerate((sg_ref, su_ref, sd_ref))]
-                + [
-                    (cot_ref.at[g], cb.at[pl.ds((2 * (g // 4) + g % 2) * group + (g % 4) // 2 * rows, rows)])
-                    for g in range(8)
-                ]
-            )
+        def packed(p, which=None):
+            if which is None:
+                return mid_pack.at[pl.ds(pl.multiple_of(p * piece, piece), piece)]
+            return mid_pack.at[pl.ds(pl.multiple_of(p * piece + which * half, half), half)]
+
+        m_r = net.wire(lambda: (packed(me.t), packed(me.t), right))
+        m_l = net.wire(lambda: (packed(me.t), packed(me.t), left))
+        m_hr = net.wire(lambda: (packed(pieces[1], 0), packed(pieces[1], 0), right))
+        m_hl = net.wire(lambda: (packed(pieces[2], 1), packed(pieces[2], 1), left))
+
+        moves = [
+            (down_ref.at[0], wd.at[pl.ds(0, hid)]),
+            (down_ref.at[1], wd.at[pl.ds(hid, hid)]),
+            (sd_ref, wd.at[pl.ds(2 * hid, hid_s)]),
+            (gate_ref.at[0], wgu.at[pl.ds(0, hid)]),
+            (gate_ref.at[1], wgu.at[pl.ds(hid, hid)]),
+            (sg_ref, wgu.at[pl.ds(2 * hid, hid_s)]),
+            (wr_ref, wgu.at[pl.ds(used, experts)]),
+            (up_ref.at[0], wgu.at[pl.ds(H, hid)]),
+            (up_ref.at[1], wgu.at[pl.ds(H + hid, hid)]),
+            (su_ref, wgu.at[pl.ds(H + 2 * hid, hid_s)]),
         ]
+        for g in range(8):
+            row = (2 * (g // 4) + g % 2) * group + (g % 4) // 2 * rows
+            moves.append((cot_ref.at[g], cb.at[pl.ds(row, rows)]))
+        loads = [pltpu.make_async_copy(src, dst, load.at[i]) for i, (src, dst) in enumerate(moves)]
         for copy in loads:
             copy.start()
-        greet([me.over_x, me.over_y, me.over_core] + [me.along(k) for k in range(1, n_tp)])
+        greet(me.peers("xykzp"))
         for wire in (z_r, z_l, to_x[0], to_y[0], to_c[0]):
             wire.start()
         nb[block(here, me.core, me.t), :] = two_ref[...]
+        wgu[used + experts : H, :] = jnp.zeros((H - used - experts, width), BF)
+        wgu[H + used :, :] = jnp.zeros((H - used, width), BF)
+        wd[used:, :] = jnp.zeros((H - used, width), BF)
         z_r.landed()
         hop_r.start()
         for wires in (to_x, to_y, to_c):
@@ -807,8 +901,13 @@
             wire.landed()
 
         lane = lax.broadcasted_iota(jnp.int32, (group, LANES), 1)
-        e_first = slot(me.s, me.c) * 2
-        lane_row = lax.broadcasted_iota(jnp.int32, (1, LANES), 1)
+        unit = lax.broadcasted_iota(jnp.int32, (group, H), 1)
+        e_first = g_me * 2
+
+        def softmax_tile(logits, lanes):
+            logits = jnp.where((lanes >= off) & (lanes < off + experts), logits, NEG)
+            e = jnp.exp(logits - jnp.max(logits, axis=1, keepdims=True))
+            return e / jnp.sum(e, axis=1, keepdims=True)
 
         def flip_chip(k):
             return chip(k // 2, lax.rem(k, 2))
@@ -837,81 +936,76 @@
                 for j in range(4):
                     relay[j].landed()
                     fwd_d[j].start()
+                for wire in at_direct + cols_w:
+                    wire.start()
                 for j in range(4):
                     fwd_d[j].landed()
 
-            logits = jnp.where(lane < experts, mdot(nb[at, :], wr[...]), NEG)
-            e = jnp.exp(logits - jnp.max(logits, axis=1, keepdims=True))
-            probs = e / jnp.sum(e, axis=1, keepdims=True)
+            acts = dot_nt(nb[at, :], wgu[...])
+            back = dot_nt(cb[at, 0:width], wd[...])
+            probs = softmax_tile(acts[:, tile:H], lane)
             routed = cb[at, width : width + LANES].astype(F32)
+            chosen, weight = [], []
+            for j in range(2):
+                expert = e_first + j
+                hit = jnp.where((lane < topk) & (routed == expert.astype(F32)), 1.0, 0.0)
+                chosen.append(jnp.max(hit, axis=1, keepdims=True))
+                weight.append(
+                    chosen[j]
+                    * jnp.sum(jnp.where(lane == off + expert, probs, 0.0), axis=1, keepdims=True)
+                )
+            scale = jnp.where(unit < hid, weight[0], jnp.where(unit < 2 * hid, weight[1], 1.0))
+            g, u = acts[:, :H], acts[:, H:]
+            sig = 1.0 / (1.0 + jnp.exp(-g))
+            silu = g * sig
+            h = silu * u
+            terms = h * back
             pg = jnp.zeros((group, LANES), F32)
-            for j in range(3):
-                shared = j == 2
-                if shared:
-                    g = dot_nt(nb[at, :], ws[0])
-                    u = dot_nt(nb[at, :], ws[1])
-                    back = dot_nt(cb[at, 0:width], ws[2])
-                else:
-                    g = mdot(nb[at, :], wg[j])
-                    u = mdot(nb[at, :], wu[j])
-                    back = dot_nt(cb[at, 0:width], wd[j])
-                sig = 1.0 / (1.0 + jnp.exp(-g))
-                silu = g * sig
-                h = silu * u
-                if not shared:
-                    expert = e_first + j
-                    hit = jnp.where(
-                        (lane < topk) & (routed == expert.astype(F32)), 1.0, 0.0
-                    )
-                    chosen = jnp.max(hit, axis=1, keepdims=True)
-                    weight = chosen * jnp.sum(
-                        jnp.where(lane == expert, probs, 0.0), axis=1, keepdims=True
-                    )
-                    grad = chosen * jnp.sum(h * back, axis=1, keepdims=True)
-                    high = grad.astype(BF).astype(F32)
-                    pg = jnp.where(lane == expert, high, pg)
-                    pg = jnp.where(lane == expert + LANES // 2, grad - high, pg)
-                    h = h * weight
-                    back = back * weight
-                gate_grad = (back * u * (sig * (1.0 + g * (1.0 - sig)))).astype(BF)
-                up_grad = (back * silu).astype(BF)
-                if shared:
-                    hws[at, :] = h.astype(BF)
-                    ggs[at, :] = gate_grad
-                    uus[at, :] = up_grad
-                else:
-                    hwe[j, at, :] = h.astype(BF)
-                    gge[j, at, :] = gate_grad
-                    uue[j, at, :] = up_grad
+            for j in range(2):
+                own = (unit >= j * hid) & (unit < (j + 1) * hid)
+                grad = chosen[j] * jnp.sum(jnp.where(own, terms, 0.0), axis=1, keepdims=True)
+                high = grad.astype(BF).astype(F32)
+                pg = jnp.where(lane == off + e_first + j, high, pg)
+                pg = jnp.where(lane == off + e_first + j + LANES // 2, grad - high, pg)
             dnb[at, width:part_w] = pg.astype(BF)
+            h = (h * scale).astype(BF)
+            back = back * scale
+            gate_grad = (back * u * (sig * (1.0 + g * (1.0 - sig)))).astype(BF)
+            up_grad = (back * silu).astype(BF)
+            hw[at, :] = h
+            gu[at, 0:H] = gate_grad
+            gu[at, H:] = up_grad
+            hwt[:, at] = h.T
+            gut[0:H, at] = gate_grad.T
+            gut[H:, at] = up_grad.T
             return carry
 
         lax.fori_loop(0, 4, hidden, 0)
 
-        n2_copies = []
         cols_s = pl.ds(pl.multiple_of(me.s * shard_w, shard_w), shard_w)
+        locals_ = []
         for g in range(8):
             row = (2 * (g // 4) + g % 2) * group + (g % 4) // 2 * rows
-            n2_copies.append(
-                pltpu.make_async_copy(nb.at[pl.ds(row, rows), cols_s], n2_out.at[g], store.at[g])
-            )
-            n2_copies[-1].start()
+            locals_.append((nb.at[pl.ds(row, rows), cols_s], n2_out.at[g]))
+        locals_.append((attn_ref, attn_out.at[g_me]))
+        locals_.append((one_ref.at[:, cols_s], one_out.at[g_me]))
+        locals_.append((lat_ref.at[:, pl.ds(pl.multiple_of(me.s * lat_w, LANES), lat_w)], lat_out.at[g_me]))
+        local_copies = [pltpu.make_async_copy(src, dst, store.at[i]) for i, (src, dst) in enumerate(locals_)]
+        for copy in local_copies:
+            copy.start()
 
         step = 16
+
+        def row_at(base, r):
+            return pl.ds(pl.multiple_of(base + r * step, step), step)
 
         def add(target, t_at, cols, left, right, count):
             def one(r, carry):
-                at = pl.ds(pl.multiple_of(r * step, step), step)
                 total = left(r).astype(F32) + right(r).astype(F32)
-                target[pl.ds(pl.multiple_of(t_at + r * step, step), step), cols] = total.astype(
-                    target.dtype
-                )
+                target[row_at(t_at, r), cols] = total.astype(BF)
                 return carry
 
             lax.fori_loop(0, count // step, one, 0)
-
-        def row_at(base, r):
-            return pl.ds(pl.multiple_of(base + r * step, step), step)
 
         every = pl.ds(0, part_w)
 
@@ -927,20 +1021,13 @@
                 rows,
             )
 
-        n_col = 4
-        col_w = width // n_col
-
         def normed_grad(i, carry):
             k = 3 - i
             at = pl.ds(pl.multiple_of(flip_chip(k) * group, group), group)
 
             def columns(n, carry):
                 cols = pl.ds(pl.multiple_of(n * col_w, col_w), col_w)
-                total = mdot(ggs[at, :], ws[0, :, cols]) + mdot(uus[at, :], ws[1, :, cols])
-                for j in range(2):
-                    total = total + dot_nt(gge[j, at, :], wg[j, cols, :])
-                    total = total + dot_nt(uue[j, at, :], wu[j, cols, :])
-                dnb[at, cols] = total.astype(BF)
+                dnb[at, cols] = mdot(gu[at, :], wgu[:, cols]).astype(BF)
                 return carry
 
             lax.fori_loop(0, n_col, columns, 0)
@@ -956,6 +1043,11 @@
                         by0.start()
                     if kk == 1:
                         by1.start()
+                        at_direct[0].landed()
+                        at_direct[1].landed()
+                        at_relay.start()
+                        at_fwd[0].start()
+                        at_fwd[1].start()
                     if kk == 0:
                         ax1.start()
 
@@ -989,21 +1081,24 @@
             @pl.when(k == 3)
             def _():
                 stage_two()
+                at_relay.landed()
+                at_fwd[2].start()
 
             def columns(n, carry):
                 cols = pl.ds(pl.multiple_of(n * col_w, col_w), col_w)
-                total = mdot(hws[at, :], ws[2, :, cols])
-                for j in range(2):
-                    total = total + mdot(hwe[j, at, :], wd[j, :, cols])
-                yb[at, cols] = total.astype(BF)
+                yb[at, cols] = mdot(hw[at, :], wd[:, cols]).astype(BF)
                 return carry
 
             lax.fori_loop(0, n_col, columns, 0)
             return carry
 
         lax.fori_loop(0, 4, output, 0)
-        y_copy = pltpu.make_async_copy(yb, y_out, store.at[8])
-        y_copy.start()
+        y_copies = [
+            pltpu.make_async_copy(yb.at[:, pl.ds(i * edge, edge)], out, store.at[11 + i])
+            for i, out in enumerate((ya_out, yb_out))
+        ]
+        for copy in y_copies:
+            copy.start()
 
         def finish_plane():
             base = here * group + me.core * rows
@@ -1022,21 +1117,44 @@
             for wire in z_w:
                 wire.start()
 
-        m_w = 256
+        def router_and_norm():
+            for wire in z_w:
+                wire.landed()
+            total = last[pl.ds(pl.multiple_of(me.t * piece, piece), piece), :].astype(F32)
+            for k in range(n_tp - 1):
+                total = total + got[k].astype(F32)
+            small = lax.broadcasted_iota(jnp.int32, (piece, LANES), 1)
+            probs = softmax_tile(dot_nt(two_ref[...], wgu[tile:H, :]), small)
+            pg = total[:, width:]
+            pg = pg + pltpu.roll(pg, LANES // 2, 1)
+            pg = jnp.where((small >= off) & (small < off + experts), pg, 0.0)
+            logit_grad = (probs * (pg - jnp.sum(probs * pg, axis=1, keepdims=True))).astype(BF)
+            grad = total[:, :width] + mdot(logit_grad, wgu[tile:H, :])
+            value = mid_ref[...]
+            back, terms = norm_back(value, gain_ref[...], grad)
+            mid_grad = cot_own_ref[...] + back
+            mid_out[...] = mid_grad
+            gain_out[...] = jnp.sum(terms, axis=0, keepdims=True)
+            at = pl.ds(pl.multiple_of(me.t * piece, piece), piece)
+            mid_pack[at, 0:width] = mid_grad.astype(BF)
+            mid_pack[at, width:] = logit_grad
+            m_r.start()
+            m_l.start()
 
         def stores(m, buf):
-            rows_m = pl.ds(pl.multiple_of(m * m_w, m_w), m_w)
+            cols = pl.ds(pl.multiple_of(m * m_w, m_w), m_w)
             made = []
             for j in range(2):
-                for i, out in enumerate((dg_out, du_out)):
-                    made.append(
-                        pltpu.make_async_copy(
-                            dgs.at[buf, 2 * j + i], out.at[j, rows_m], store.at[9 + 4 * buf + 2 * j + i]
-                        )
-                    )
-            return made
-
-        def gate_up(m, carry):
+                at = pl.ds(j * hid, hid)
+                made.append((gus.at[buf, at], dg_out.at[j, :, cols]))
+                made.append((gus.at[buf, pl.ds(H + j * hid, hid)], du_out.at[j, :, cols]))
+                made.append((dds.at[buf, at], dd_out.at[j, :, cols]))
+            return [
+                pltpu.make_async_copy(src, dst, store.at[14 + 6 * buf + i])
+                for i, (src, dst) in enumerate(made)
+            ]
+
+        def weight_grad(m, carry):
             buf = lax.rem(m, 2)
             cols = pl.ds(pl.multiple_of(m * m_w, m_w), m_w)
 
@@ -1049,16 +1167,21 @@
                         for copy in stores(m - 2, bb):
                             copy.wait()
 
-            @pl.when(m == 4)
+            @pl.when(m == 2)
             def _():
                 finish_plane()
 
-            left = nb[:, cols]
-            for j in range(2):
-                dgs[buf, 2 * j] = dot_tn(left, gge[j])
-                dgs[buf, 2 * j + 1] = dot_tn(left, uue[j])
-            dss[0, :, cols] = dot_tn(ggs[...], left).astype(BF)
-            dss[1, :, cols] = dot_tn(uus[...], left).astype(BF)
+            @pl.when(m == 6)
+            def _():
+                router_and_norm()
+
+            both = mdot(gut[...], nb[:, cols])
+            gus[buf] = both
+            dss[0, :, cols] = both[2 * hid : used].astype(BF)
+            dss[1, :, cols] = both[H + 2 * hid : H + used].astype(BF)
+            third = mdot(hwt[...], cb[:, cols])
+            dds[buf] = third
+            dss[2, :, cols] = third[2 * hid : used].astype(BF)
             for bb in range(2):
 
                 @pl.when(buf == bb)
@@ -1068,86 +1191,52 @@
 
             return carry
 
-        n_m = width // m_w
-        lax.fori_loop(0, n_m, gate_up, 0)
+        lax.fori_loop(0, n_m, weight_grad, 0)
+        m_r.landed()
+        m_hr.start()
+        m_l.landed()
+        m_hl.start()
+        ds_copy = pltpu.make_async_copy(dss, ds_out, store.at[13])
+        ds_copy.start()
         for m in (n_m - 2, n_m - 1):
             for copy in stores(m, m % 2):
                 copy.wait()
-
-        def down_stores(m, buf):
-            cols = pl.ds(pl.multiple_of(m * m_w, m_w), m_w)
-            return [
-                pltpu.make_async_copy(dds.at[buf, j], dd_out.at[j, :, cols], store.at[17 + 2 * buf + j])
-                for j in range(2)
-            ]
-
-        def down_grad(m, carry):
-            buf = lax.rem(m, 2)
-            cols = pl.ds(pl.multiple_of(m * m_w, m_w), m_w)
-
-            @pl.when(m >= 2)
-            def _():
-                for bb in range(2):
-
-                    @pl.when(buf == bb)
-                    def _():
-                        for copy in down_stores(m - 2, bb):
-                            copy.wait()
-
-            right_c = cb[:, cols]
-            for j in range(2):
-                dds[buf, j] = dot_tn(hwe[j], right_c)
-            dss[2, :, cols] = dot_tn(hws[...], right_c).astype(BF)
-            for bb in range(2):
-
-                @pl.when(buf == bb)
-                def _():
-                    for copy in down_stores(m, bb):
-                        copy.start()
-
-            return carry
-
-        lax.fori_loop(0, n_m, down_grad, 0)
-        ds_copy = pltpu.make_async_copy(dss, ds_out, store.at[21])
-        ds_copy.start()
-        for m in (n_m - 2, n_m - 1):
-            for copy in down_stores(m, m % 2):
-                copy.wait()
-
-        for wire in z_w:
+        for wire in [at_direct[2], *at_fwd, *cols_w, m_hr, m_hl]:
             wire.landed()
-        for r in range(piece // step):
-            total = last[row_at(me.t * piece, r), :].astype(F32)
-            for k in range(n_tp - 1):
-                total = total + got[k, r * step : (r + 1) * step, :].astype(F32)
-            two_out[r * step : (r + 1) * step, :] = total
-        for copy in n2_copies:
+        for copy in local_copies + y_copies:
             copy.wait()
-        y_copy.wait()
         ds_copy.wait()
         for wire in net.all:
             wire.sent()
 
-    ins = (two_own, cot_all, gate, up, down, sg_t, su_t, sd, w_router)
+    ins = (
+        two_own, mid_own, cot_own, gain_two,
+        cot_all, gate, up, down, sg_t, su_t, sd, router_t, attn, normed, latent,
+    )
     outs = [
-        ((piece, part_w), F32),
-        ((tokens, width), BF),
+        ((piece, width), F32),
+        ((1, width), F32),
+        ((rows, part_w), BF),
+        ((tokens, edge), BF),
+        ((tokens, edge), BF),
         (gate.shape, F32),
         (up.shape, F32),
         (down.shape, F32),
         ((3, hid_s, width), BF),
         ((8, rows, shard_w), BF),
+        ((8, rows, attn_w), BF),
+        ((8, rows, shard_w), BF),
+        ((8, rows, lat_w), BF),
     ]
     scratch = [
         VMEM((tokens, width), BF),
         VMEM((tokens, pack), BF),
-        VMEM(gate.shape, BF),
-        VMEM(up.shape, BF),
-        VMEM(down.shape, BF),
-        VMEM((3, hid_s, width), BF),
-        VMEM(w_router.shape, BF),
-        *[VMEM((2, tokens, hid), BF)] * 3,
-        *[VMEM((tokens, hid_s), BF)] * 3,
+        VMEM((2 * H, width), BF),
+        VMEM((H, width), BF),
+        VMEM((tokens, 2 * H), BF),
+        VMEM((2 * H, tokens), BF),
+        VMEM((tokens, H), BF),
+        VMEM((H, tokens), BF),
         VMEM((tokens, part_w), BF),
         VMEM((tokens, width), BF),
         VMEM((4, rows, part_w), BF),
@@ -1159,24 +1248,24 @@
         VMEM((rows, part_w - edge), BF),
         VMEM((rows, part_w), BF),
         VMEM((n_tp - 1, piece, part_w), BF),
-        VMEM((2, 4, 256, hid), F32),
-        VMEM((2, 2, hid, 256), F32),
+        VMEM((2, 2 * H, m_w), F32),
+        VMEM((2, H, m_w), F32),
         VMEM((3, hid_s, width), BF),
     ]
     return pl.pallas_call(
         body,
         out_shape=tuple(jax.ShapeDtypeStruct(*o) for o in outs),
-        in_specs=[pl.BlockSpec(memory_space=VMEM)] + [pl.BlockSpec(memory_space=ANY)] * 8,
-        out_specs=(pl.BlockSpec(memory_space=VMEM), *[pl.BlockSpec(memory_space=ANY)] * 6),
+        in_specs=[pl.BlockSpec(memory_space=VMEM)] * 4 + [pl.BlockSpec(memory_space=ANY)] * 11,
+        out_specs=(*[pl.BlockSpec(memory_space=VMEM)] * 3, *[pl.BlockSpec(memory_space=ANY)] * 10),
         scratch_shapes=[
             *scratch,
             pltpu.SemaphoreType.DMA((n_wires,)),
             pltpu.SemaphoreType.DMA((n_wires,)),
-            pltpu.SemaphoreType.DMA((15,)),
-            pltpu.SemaphoreType.DMA((22,)),
+            pltpu.SemaphoreType.DMA((18,)),
+            pltpu.SemaphoreType.DMA((26,)),
         ],
         compiler_params=pltpu.CompilerParams(
-            collective_id=4, has_side_effects=True, vmem_limit_bytes=66 * 10**6
+            collective_id=4, has_side_effects=True, vmem_limit_bytes=67 * 10**6
         ),
         name="feed_forward",
     )(*ins)
@@ -1211,6 +1300,7 @@
     s_id, c_id, t_id = lax.axis_index(SHARD), lax.axis_index(CTX), lax.axis_index(TP)
     shard_w = width // 4
     kv_w = KVR // 4
+    pad = LANES - experts
 
     small = jnp.concatenate(
         [
@@ -1218,28 +1308,32 @@
             norm2_gain.reshape(-1, LANES),
             kv_norm_gain.reshape(-1, LANES),
             jnp.zeros((7, LANES), BF),
-            jnp.pad(router_weight, ((0, 0), (0, LANES - experts))),
         ]
     )
-    w_query, w_latent, w_expand, w_output, small_all, x_pair = start_gather(
-        (q_weight, kva_weight, kvb_weight, out_weight), small, block_input, n_tp
-    )
+    (gathered,) = comm_kernel(
+        [
+            shard_gather(
+                [
+                    (q_weight, False),
+                    (kva_weight.T, True),
+                    (kvb_weight, False),
+                    (small, False),
+                    (out_weight, True),
+                    (router_weight.T, True),
+                ],
+                block_input,
+            )
+        ],
+        n_tp,
+        0,
+        "start",
+    )
+    w_query, w_latent_t, w_expand, small_all, w_output, router_t, x_pair = gathered
     w_query = w_query.reshape(width, -1)
-    w_latent = w_latent.reshape(width, -1)
     w_expand = w_expand.reshape(KVR, -1)
-    w_output = w_output.transpose(1, 0, 2).reshape(-1, width)
     gain_one = small_all[:, 0:4].reshape(-1)
     gain_two = small_all[:, 4:8].reshape(-1)
     gain_kv = small_all[:, 8:9].reshape(-1)
-    w_router = small_all[:, 16:, :experts].reshape(width, experts)
-
-    cot_b = cotangent.astype(BF)
-    cot_pack = jnp.concatenate(
-        [cot_b, jnp.pad(routes.astype(BF), ((0, 0), (0, LANES - topk)))], axis=1
-    )
-    cot_all, sg_t, su_t, sd = plane_exchange(
-        (cot_pack,), (), (shared_gate.T, shared_up.T, shared_down), n_tp, 1, "early_exchange"
-    )
 
     x_float = block_input.astype(F32)
     cosine, sine = rope_tables(rows, (c_id * rows).astype(F32))
@@ -1249,7 +1343,7 @@
     query = mdot(normed_one, w_query).reshape(rows, heads, DN + DR)
     query_nope = query[..., :DN].astype(BF)
     query_rope = rotate(query[..., DN:], cosine[:, None, :], sine[:, None, :]).astype(BF)
-    latent = mdot(normed_pair, w_latent)
+    latent = dot_nt(normed_pair, w_latent_t)
     latent_pair = norm_rows(latent[:, :KVR], gain_kv).astype(BF)
     rope_pair = rotate(latent[:, KVR:], cos_all, sin_all).astype(BF)
     kv_pair = mdot(latent_pair, w_expand).astype(BF).reshape(2 * rows, heads, DN + DV)
@@ -1270,41 +1364,47 @@
     def own(a):
         return lax.dynamic_slice_in_dim(a, t_id * piece, piece, 0)
 
-    attn_full = tp_reduce_scatter(mdot(attn_flat, w_output).astype(BF), n_tp, 2, "attn_scatter")
+    cot_pack = jnp.concatenate(
+        [cotangent.astype(BF), jnp.pad(routes.astype(BF), ((0, 0), (0, LANES - topk)))], axis=1
+    )
+    (attn_full,), (cot_all,), (sg_t,), (su_t,), (sd,) = comm_kernel(
+        [
+            tp_reduce_scatter(mdot(attn_flat, w_output).astype(BF), n_tp),
+            plane_gather(cot_pack),
+            shard_rows(shared_gate.T),
+            shard_rows(shared_up.T),
+            shard_rows(shared_down),
+        ],
+        n_tp,
+        1,
+        "middle",
+    )
     mid = own(x_float) + attn_full
     two_own = norm_rows(mid, gain_two).astype(BF)
-    summed, y_part, grad_expert_gate, grad_expert_up, grad_expert_down, shared_grads, two_cols = feed_forward(
+    latent_own = lax.dynamic_slice_in_dim(latent_pair, c_id * rows, rows, 0)
+
+    (
+        mid_grad, gain_two_sum, mid_pack, y_left, y_right, grad_gate, grad_up, grad_expert_down, shared_grads,
+        two_cols, attn_all, one_cols, lat_cols,
+    ) = feed_forward(
         two_own,
+        mid,
+        own(cotangent),
+        gain_two.astype(F32)[None, :],
         cot_all,
-        expert_gate,
-        expert_up,
+        expert_gate.transpose(0, 2, 1),
+        expert_up.transpose(0, 2, 1),
         expert_down,
         sg_t,
         su_t,
         sd,
-        jnp.pad(w_router, ((0, 0), (0, LANES - experts))),
-        experts,
+        router_t,
+        attn_flat,
+        normed_one,
+        latent_own,
         topk,
         n_tp,
     )
-    two_grad = summed[:, :width]
-    prob_grad = summed[:, width : width + experts]
-    prob_grad = prob_grad + summed[:, width + LANES // 2 : width + LANES // 2 + experts]
-    y_part = y_part.reshape(2, 2, 2, rows, width).transpose(0, 2, 1, 3, 4).reshape(8, rows, width)
-    out_own = mid + reduce_everywhere(y_part, n_tp, 3, "y_scatter")
-    shared_grads = [shared_grads[i] for i in range(3)]
-
-    probs_own = jax.nn.softmax(mdot(two_own, w_router), axis=-1)
-    logit_grad = (
-        probs_own * (prob_grad - jnp.sum(probs_own * prob_grad, axis=-1, keepdims=True))
-    ).astype(BF)
-    two_grad = two_grad + dot_nt(logit_grad, w_router)
-    mid_norm_grad, gain_two_terms = norm_back(mid, gain_two, two_grad)
-    mid_grad = own(cotangent) + mid_norm_grad
-    mid_pack = jnp.concatenate(
-        [mid_grad.astype(BF), jnp.pad(logit_grad, ((0, 0), (0, LANES - experts)))], axis=1
-    )
-    (mid_pack,) = tp_all_gather((mid_pack,), n_tp, 5, "mid_grad_gather")
     mid_b = mid_pack[:, :width]
 
     out_grad = dot_nt(mid_b, w_output).reshape(rows, heads, DV)
@@ -1329,7 +1429,18 @@
     )
     mine = lax.dynamic_slice_in_dim(kv_terms, c_id * rows, rows, 0)
     other = lax.dynamic_slice_in_dim(kv_terms, (1 - c_id) * rows, rows, 0).astype(BF)
-    kv_sum = mine + ctx_swap(other, 6, "kv_grad_swap").astype(F32)
+    (swapped,), (y_left,), (mid_cols,), (logit_all,) = comm_kernel(
+        [
+            ctx_swap(other),
+            reduce_everywhere(y_left, n_tp),
+            plane_columns(mid_b),
+            plane_gather(mid_pack[:, width:], 1),
+        ],
+        n_tp,
+        2,
+        "swap",
+    )
+    kv_sum = mine + swapped.astype(F32)
     kv_grad = kv_sum[:, : heads * (DN + DV)].astype(BF)
     rope_part = rotate_back(kv_sum[:, heads * (DN + DV) :][:, :DR], cosine, sine)
     rope_qback = rotate_back(rope_qgrad, cosine[:, None, :], sine[:, None, :])
@@ -1339,60 +1450,70 @@
     back_part = jnp.concatenate(
         [one_part, latent_part, jnp.pad(rope_part, ((0, 0), (0, LANES - DR)))], axis=1
     ).astype(BF)
-    back = tp_reduce_scatter(back_part, n_tp, 7, "attn_back_scatter")
+    (back,), (y_right,), (shared_cols,) = comm_kernel(
+        [
+            tp_reduce_scatter(back_part, n_tp),
+            reduce_everywhere(y_right, n_tp),
+            plane_columns(shared_grads.reshape(-1, width)),
+        ],
+        n_tp,
+        3,
+        "back",
+    )
+    out_own = mid + jnp.concatenate([y_left, y_right], axis=1)
 
     compressed = own(lax.dynamic_slice_in_dim(latent, c_id * rows, rows, 0))[:, :KVR]
     compressed_grad, gain_kv_terms = norm_back(compressed, gain_kv, back[:, width : width + KVR])
     latent_grad = jnp.concatenate(
         [compressed_grad, back[:, width + KVR : width + KVR + DR]], axis=1
     ).astype(BF)
-    one_grad = back[:, :width] + dot_nt(latent_grad, w_latent)
+    one_grad = back[:, :width] + mdot(latent_grad, w_latent_t)
     input_norm_grad, gain_one_terms = norm_back(own(x_float), gain_one, one_grad)
     input_own = mid_grad + input_norm_grad
 
-    block_output, input_grad = tp_all_gather((out_own, input_own), n_tp, 8, "output_gather")
     lat_pack = jnp.pad(latent_grad, ((0, 0), (0, 5 * LANES - KVR - DR)))
-    (latent_rows,) = tp_all_gather((lat_pack,), n_tp, 9, "latent_gather")
-    latent_own = lax.dynamic_slice_in_dim(latent_pair, c_id * rows, rows, 0)
-    head_pack = jnp.concatenate(
-        [query_grad, kv_grad, attn_flat, latent_rows, mid_pack[:, width:]], axis=1
-    )
-    head_all, one_cols, lat_cols, mid_cols, sg_cols, su_cols, sd_cols = plane_exchange(
-        (head_pack,), (normed_one, latent_own, mid_b, *shared_grads), (), n_tp, 10, "late_exchange"
-    )
-    head_all = head_all.reshape(8 * rows, -1)
-    edges = [0, heads * (DN + DR), heads * (DN + DV), heads * DV, 5 * LANES, LANES]
-    edges = [sum(edges[: i + 1]) for i in range(len(edges))]
-    dq_all, dkv_all, attn_all, lat_all, logit_all = (
-        head_all[:, a:b] for a, b in zip(edges[:-1], edges[1:])
-    )
-    one_cols = one_cols.reshape(8 * rows, -1)
-    lat_cols = lat_cols.reshape(8 * rows, -1)
-    mid_cols = mid_cols.reshape(8 * rows, -1)
-    grad_query = dot_tn(one_cols, dq_all)
-    grad_latent = dot_tn(one_cols, lat_all[:, : KVR + DR])
-    grad_expand = dot_tn(lat_cols, dkv_all)
-    grad_out_w = dot_tn(attn_all, mid_cols)
-    grad_router = dot_tn(two_cols.reshape(8 * rows, -1), logit_all[:, :experts])
-    grad_sgate = sg_cols.reshape(-1, shard_w).T.astype(F32)
-    grad_sup = su_cols.reshape(-1, shard_w).T.astype(F32)
-    grad_sdown = sd_cols.reshape(-1, shard_w).astype(F32)
-
     gains = jnp.concatenate(
         [
             jnp.sum(gain_one_terms, axis=0),
-            jnp.sum(gain_two_terms, axis=0),
+            gain_two_sum[0],
             jnp.sum(gain_kv_terms, axis=0),
             jnp.zeros((512,), F32),
         ]
     ).reshape(8, -1)
-    gains = sum_everywhere(gains, n_tp, 11, "gain_sum").reshape(-1)
+    (lat_all,), (head_all,), (block_output,), (input_grad,), (gains,) = comm_kernel(
+        [
+            gather_rows(lat_pack, n_tp),
+            plane_gather(jnp.concatenate([query_grad, kv_grad], axis=1)),
+            tp_all_gather(out_own.astype(BF), n_tp),
+            tp_all_gather(input_own.astype(BF), n_tp),
+            sum_everywhere(gains, n_tp),
+        ],
+        n_tp,
+        5,
+        "finish",
+    )
+    head_all = head_all.reshape(8 * rows, -1)
+    split = heads * (DN + DR)
+    lat_all = lat_all.reshape(8 * rows, -1)[:, : KVR + DR]
+    one_cols = one_cols.reshape(8 * rows, -1)
+    grad_query = dot_tn(one_cols, head_all[:, :split])
+    grad_latent = dot_tn(lat_all, one_cols).T
+    grad_expand = dot_tn(lat_cols.reshape(8 * rows, -1), head_all[:, split:])
+    grad_out_w = dot_tn(attn_all.reshape(8 * rows, -1), mid_cols.reshape(8 * rows, -1))
+    off = (2 * expert_gate.shape[2] + sg_t.shape[0]) % LANES
+    logit_all = logit_all.reshape(8 * rows, -1)[:, off : off + experts]
+    grad_router = dot_tn(logit_all, two_cols.reshape(8 * rows, -1)).T
+    shared_cols = shared_cols.reshape(8, 3, -1, shard_w)
+    grad_sgate, grad_sup, grad_sdown = (
+        shared_cols[:, i].reshape(-1, shard_w).astype(F32) for i in range(3)
+    )
+    gains = gains.reshape(-1)
     grad_one = lax.dynamic_slice_in_dim(gains, s_id * shard_w, shard_w, 0)
     grad_two = lax.dynamic_slice_in_dim(gains, width + s_id * shard_w, shard_w, 0)
     grad_kv = lax.dynamic_slice_in_dim(gains, 2 * width + s_id * kv_w, kv_w, 0)
     return (
-        block_output,
-        input_grad,
+        block_output.astype(F32),
+        input_grad.astype(F32),
         grad_one,
         grad_query,
         grad_latent,
@@ -1401,11 +1522,11 @@
         grad_out_w,
         grad_two,
         grad_router,
-        grad_sgate,
-        grad_sup,
+        grad_sgate.T,
+        grad_sup.T,
         grad_sdown,
-        grad_expert_gate,
-        grad_expert_up,
+        grad_gate.transpose(0, 2, 1),
+        grad_up.transpose(0, 2, 1),
         grad_expert_down,
     )
 

time: 527 us -> 390 us (0.74)
  Pallas kernels: 397 us -> 297 us
  local copies, waits for them, and re-layouts: 69.6 us -> 30 us
    pallas_call x11 -> x5, Pallas kernels: 313 us -> 202 us  [comm_kernel(): pl.pallas_call(body, out_shape=tuple((jax.ShapeDtypeStruct(shape, dtype)...]
    unnamed x178 -> x132, local copies, waits for them, and re-layouts: 32.6 us -> 13.1 us
    pallas_call x1, Pallas kernels: 84.9 us -> 94.8 us  [feed_forward(): pl.pallas_call(body, out_shape=tuple((jax.ShapeDtypeStruct(*o) for o in o...]
    transpose x2 -> x0, local copies, waits for them, and re-layouts: 5.38 us -> none  [per_device(): w_output = w_output.transpose(1, 0, 2).reshape(-1, width)]
where the time goes in v3:
time: 390 us; the launch traced here: 389 us
  Pallas kernels  297 us (76%)
  other arithmetic  32.3 us (8%)
  local copies, waits for them, and re-layouts  30 us (8%)
  matrix products  28.1 us (7%)
    pallas_call x5, Pallas kernels, comm_kernel(): pl.pallas_call(body, out_shape=tuple((jax.ShapeDtypeStruct(shape, dtype)...  202 us
    pallas_call x1, Pallas kernels, feed_forward(): pl.pallas_call(body, out_shape=tuple((jax.ShapeDtypeStruct(*o) for o in o...  94.8 us
    dot_general x5, matrix products, dot_tn(): lax.dot_general(left, right, (((0,), (0,)), ((), ())), preferred_element_...  13.9 us
    unnamed x132, local copies, waits for them, and re-layouts  13.1 us

profile of v3, /device:TPU:0, one launch (start us, length us, event | category | flops | bytes accessed | tf_op | source)
XLA Modules:
  0.0 388.8 jit_solution(488932657914612033)
XLA Ops:
  0.7 1.3 multiply_reduce_fusion.1
  2.8 1.4 maximum_maximum_fusion.refs_3_
  5.5 1.3 convert_element_type.177
  6.8 0.8 fusion.20.refs_1_
  7.6 1.1 convert_element_type.171
  8.7 42.0 %start.1 = (bf16[4,512,768]{2,1,0:T(8,128)(2,1)}, bf16[576,2048]{1,0:T(8,128)(2,1)}, bf16[4,128,1024]{2,1,0:T(8,128)(2,1)}, bf16[4,16,128]{2,1,0:T(8,128)(2,1)},...) custom-call(bf16[512,768]{1,0:T(8,128)(2,1)} %refs_0_.1, ...), custom_call_target="tpu_custom_call" | custom-call | tf_op jit(solution)/shard_map/start/pallas_call | solution.py:193
  50.7 1.7 multiply_reduce_fusion
  53.1 0.8 slice_convert_fusion.5
  53.9 1.5 fusion.3
  55.4 0.8 fusion.53
  58.6 1.2 convolution_convert_fusion.2
  59.8 2.4 reshape.320
  62.2 1.9 fusion.49
  64.1 1.9 copy.107
  66.0 2.0 multiply_convert_fusion.refs_13_
  68.1 2.9 copy.74
  70.9 3.0 fusion.21
  76.0 0.8 copy.100.refs_12_
  76.7 1.3 convolution_convert_fusion.1.refs_0_
  78.0 39.3 %middle.1 = (f32[32,2048]{1,0:T(8,128)}, bf16[8,128,2176]{2,1,0:T(8,128)(2,1)}, bf16[88,2048]{1,0:T(8,128)(2,1)}, bf16[88,2048]{1,0:T(8,128)(2,1)}, bf16[88,2048]{1,0:T(8,128)(2,1)}) custom-call(bf16[128,2048]{1,0:T(8,128)(2,1)} %convolution_convert_fusion.1.refs_0_, bf16[128,2176]{1,0:T(8,128)(2,1)} %fusion.20.refs_1_, bf16[704,512]{1,0:T(8,128)(2,1)} %bitcast.148, ...), custom_call_target="tpu_custom_call" | custom-call | tf_op jit(solution)/shard_map/middle/pallas_call | solution.py:193
  117.3 2.0 multiply_reduce_fusion.7
  121.2 94.8 %feed_forward.1 = (f32[32,2048]{1,0:T(8,128)}, f32[1,2048]{1,0:T(1,128)}, bf16[128,2176]{1,0:T(8,128)(2,1)}, bf16[1024,1024]{1,0:T(8,128)(2,1)}, bf16[1024,1024]...) custom-call(bf16[32,2048]{1,0:T(8,128)(2,1)} %multiply_convert_fusio, ...), custom_call_target="tpu_custom_call" | custom-call | tf_op jit(solution)/shard_map/feed_forward/pallas_call | solution.py:1255
  216.1 2.5 multiply_reduce_fusion.6
  220.2 0.8 slice.113.refs_2_
  221.9 1.2 convolution_convert_fusion
  224.5 39.6 %swap.1 = (bf16[128,1152]{1,0:T(8,128)(2,1)}, f32[32,1024]{1,0:T(8,128)}, bf16[8,128,512]{2,1,0:T(8,128)(2,1)}, bf16[8,128,128]{2,1,0:T(8,128)(2,1)}) custom-call(bf16[128,1152]{1,0:T(8,128)(2,1)} %dynamic-slice_convert_fusion.refs_0_, bf16[1024,1024]{1,0:T(8,128)(2,1)} %get-tuple-element.66.refs_1_, bf16[128,2048]{1,0:T(8,128)(2,1)} %slice.113.refs_2_, ...), custom_call_target="tpu_custom_call" | custom-call | tf_op jit(solution)/shard_map/swap/pallas_call | solution.py:193
  264.1 2.0 fusion.28
  266.1 3.4 convolution_bitcast_fusion
  270.5 0.8 pad_maximum_fusion.2.refs_1_
  271.4 0.9 pad_maximum_fusion.1.refs_0_
  272.3 45.3 %back.1 = (f32[32,2688]{1,0:T(8,128)}, f32[32,1024]{1,0:T(8,128)}, bf16[8,264,512]{2,1,0:T(8,128)(2,1)}) custom-call(bf16[128,2688]{1,0:T(8,128)(2,1)} %pad_maximum_fusion.1.refs_0_, bf16[1024,1024]{1,0:T(8,128)(2,1)} %get-tuple-element.68.refs_1_, bf16[264,2048]{1,0:T(8,128)(2,1)} %bitcast.146), custom_call_target="tpu_custom_call" | custom-call | tf_op jit(solution)/shard_map/back/pallas_call | solution.py:193
  317.7 1.6 fusion.30.refs_2_
  319.3 1.9 fusion.48
  322.1 1.2 multiply_reduce_fusion.3
  325.2 1.7 add_convert_fusion.refs_3_
  326.9 1.3 bitcast_convert_fusion
  328.2 1.3 convert_bitcast_fusion
  329.6 1.3 convert_bitcast_fusion.1
  330.9 35.7 %finish.1 = (bf16[8,128,640]{2,1,0:T(8,128)(2,1)}, bf16[8,128,1792]{2,1,0:T(8,128)(2,1)}, bf16[128,2048]{1,0:T(8,128)(2,1)}, bf16[128,2048]{1,0:T(8,128)(2,1)}, f32[8,640]{1,0:T(8,128)}) custom-call(bf16[32,640]{1,0:T(8,128)(2,1)} %pad.20.refs_0_, bf16[128,1792]{1,0:T(8,128)(2,1)} %pad_maximum_fusion.2.refs_1_, bf16[32,2048]{1,0:T(8,128)(2,1)} %fusion.30.refs_2_, ...), custom_call_target="tpu_custom_call" | custom-call | tf_op jit(solution)/shard_map/finish/pallas_call | solution.py:193
  368.6 3.0 fusion
  371.6 3.7 fusion.4
  375.4 1.8 fusion.6
  377.2 1.1 convert_element_type.194
  378.3 1.1 convert_element_type.195
  379.4 2.9 copy.115
  382.3 2.9 copy.116
  385.2 1.0 slice-done.1
  386.3 2.5 copy.117
  (195 shorter events, 18.4 us)
Async XLA Ops:
  0.6 7.0 %copy-start.3 = (bf16[128,2048]{1,0:T(8,128)(2,1)S(1)}, bf16[128,2048]{1,0:T(8,128)(2,1)}, u32[]{:S(2)}) copy-start(bf16[128,2048]{1,0:T(8,128)(2,1)} %refs_6_.1) | copy-start | bytes 1572868
  0.7 8.0 %copy-start.48 = (f32[128]{0:T(128)}, f32[128]{0:T(128)S(1)}, u32[]{:S(2)}) copy-start(f32[128]{0:T(128)S(1)} %iota_add_fusion) | copy-start | bytes 1540
  0.7 55.5 %copy-start.46 = (f32[32]{0:T(128)}, f32[32]{0:T(128)S(1)}, u32[]{:S(2)}) copy-start(f32[32]{0:T(128)S(1)} %negate_power_fusion) | copy-start | bytes 388
  5.4 68.6 %copy-start.31 = (f32[128,32]{0,1:T(8,128)}, f32[128,32]{0,1:T(8,128)S(1)}, u32[]{:S(2)}) copy-start(f32[128,32]{0,1:T(8,128)S(1)} %copy.77) | copy-start | bytes 49156
  5.5 68.5 %copy-start.33 = (f32[128,32]{0,1:T(8,128)}, f32[128,32]{0,1:T(8,128)S(1)}, u32[]{:S(2)}) copy-start(f32[128,32]{0,1:T(8,128)S(1)} %copy.78) | copy-start | bytes 49156
  50.7 4.7 %copy-start.13 = (bf16[576,2048]{1,0:T(8,128)(2,1)S(1)}, bf16[576,2048]{1,0:T(8,128)(2,1)}, u32[]{:S(2)}) copy-start(bf16[576,2048]{1,0:T(8,128)(2,1)} %get-tuple-element.55) | copy-start | bytes 7077892
  53.1 4.7 %copy-start.42 = (f32[4,1,128]{2,1,0:T(1,128)}, f32[4,1,128]{2,1,0:T(1,128)S(1)}, u32[]{:S(2)}) copy-start(f32[4,1,128]{2,1,0:T(1,128)S(1)} %slice_convert_fusion.6) | copy-start | bytes 6148
  53.9 66.6 %copy-start.41 = (f32[4,4,128]{2,1,0:T(4,128)}, f32[4,4,128]{2,1,0:T(4,128)S(1)}, u32[]{:S(2)}) copy-start(f32[4,4,128]{2,1,0:T(4,128)S(1)} %get-tuple-element.112) | copy-start | bytes 24580
  56.5 17.9 %copy-start.35 = (bf16[256,32]{0,1:T(8,128)(2,1)}, bf16[256,32]{0,1:T(8,128)(2,1)S(1)}, u32[]{:S(2)}) copy-start(bf16[256,32]{0,1:T(8,128)(2,1)S(1)} %get-tuple-element.102) | copy-start | bytes 49156
  56.5 17.9 %copy-start.37 = (bf16[256,32]{0,1:T(8,128)(2,1)}, bf16[256,32]{0,1:T(8,128)(2,1)S(1)}, u32[]{:S(2)}) copy-start(bf16[256,32]{0,1:T(8,128)(2,1)S(1)} %get-tuple-element.103) | copy-start | bytes 49156
  56.6 2.0 copy-start.8
  59.8 8.2 %copy-start = (bf16[4,512,768]{2,1,0:T(8,128)(2,1)S(1)}, bf16[4,512,768]{2,1,0:T(8,128)(2,1)}, u32[]{:S(2)}) copy-start(bf16[4,512,768]{2,1,0:T(8,128)(2,1)} %get-tuple-element.57) | copy-start | bytes 9437188
  64.1 9.9 %copy-start.15 = (bf16[256,4,128]{2,1,0:T(4,128)(2,1)}, bf16[256,4,128]{2,1,0:T(4,128)(2,1)S(1)}, u32[]{:S(2)}) copy-start(bf16[256,4,128]{2,1,0:T(4,128)(2,1)S(1)} %get-tuple-element.104) | copy-start | bytes 786436
  70.9 3.5 copy-start.40
  74.1 2.7 copy-start.2
  76.0 41.4 %copy-start.18 = (bf16[128,4,128]{0,2,1:T(8,128)(2,1)}, bf16[128,4,128]{0,2,1:T(8,128)(2,1)S(1)}, u32[]{:S(2)}) copy-start(bf16[128,4,128]{0,2,1:T(8,128)(2,1)S(1)} %fusion.16) | copy-start | bytes 393220
  216.0 2.6 copy-start.5
  216.0 2.6 copy-start.23
  216.0 2.6 copy-start.44
  216.0 3.2 copy-start.16
  218.6 2.5 copy-start.28
  218.6 2.7 copy-start.36
  218.6 2.7 copy-start.38
  218.9 2.6 copy-start.12
  219.3 2.5 copy-start.32
  219.3 2.5 copy-start.34
  219.3 2.6 copy-start.1
  223.7 40.4 %copy-start.19 = (bf16[8,128,512]{2,1,0:T(8,128)(2,1)S(1)}, bf16[8,128,512]{2,1,0:T(8,128)(2,1)}, u32[]{:S(2)}) copy-start(bf16[8,128,512]{2,1,0:T(8,128)(2,1)} %get-tuple-element.84) | copy-start | bytes 3145732
  266.1 3.4 copy-start.29
  266.1 3.4 copy-start.9
  272.3 45.4 %copy-start.7 = (f32[32,2048]{1,0:T(8,128)S(1)}, f32[32,2048]{1,0:T(8,128)}, u32[]{:S(2)}) copy-start(f32[32,2048]{1,0:T(8,128)} %copy-done.6) | copy-start | bytes 786436
  272.3 45.4 %copy-start.39 = (f32[32,1024]{1,0:T(8,128)S(1)}, f32[32,1024]{1,0:T(8,128)}, u32[]{:S(2)}) copy-start(f32[32,1024]{1,0:T(8,128)} %get-tuple-element.71) | copy-start | bytes 393220
  319.3 2.0 copy-start.50
  319.3 2.1 copy-start.53
  319.3 2.2 copy-start.10
  319.3 2.8 copy-start.14
  319.3 2.8 copy-start.51
  321.2 2.7 copy-start.45
  328.2 40.4 %copy-start.30 = (bf16[8,128,128]{2,1,0:T(8,128)(2,1)S(1)}, bf16[8,128,128]{2,1,0:T(8,128)(2,1)}, u32[]{:S(2)}) copy-start(bf16[8,128,128]{2,1,0:T(8,128)(2,1)} %get-tuple-element.81) | copy-start | bytes 786436
  330.9 40.7 %copy-start.56 = (bf16[8,128,512]{2,1,0:T(8,128)(2,1)S(1)}, bf16[8,128,512]{2,1,0:T(8,128)(2,1)}, u32[]{:S(2)}) copy-start(bf16[8,128,512]{2,1,0:T(8,128)(2,1)} %get-tuple-element.78) | copy-start | bytes 3145732
  368.6 6.8 %copy-start.55 = (bf16[8,128,640]{2,1,0:T(8,128)(2,1)S(1)}, bf16[8,128,640]{2,1,0:T(8,128)(2,1)}, u32[]{:S(2)}) copy-start(bf16[8,128,640]{2,1,0:T(8,128)(2,1)} %get-tuple-element.80) | copy-start | bytes 3932164
  368.6 10.8 %slice-start.4 = ((s8[5767168]{0:T(1024)(128)(4,1)}), s8[4194304]{0:T(1024)(128)(4,1)S(1)}, s32[]{:S(2)}) async-start(s8[5767168]{0:T(1024)(128)(4,1)} %bitcast.129), calls=%async_computation.4 | async-start | bytes 8388608
  371.6 10.7 %slice-start.2 = ((s8[5767168]{0:T(1024)(128)(4,1)}), s8[4194304]{0:T(1024)(128)(4,1)S(1)}, s32[]{:S(2)}) async-start(s8[5767168]{0:T(1024)(128)(4,1)} %bitcast.126), calls=%async_computation.2 | async-start | bytes 8388608
  375.4 2.9 copy-start.24
  375.4 4.0 %slice-start.5 = ((s8[5767168]{0:T(1024)(128)(4,1)}), s8[1572864]{0:T(1024)(128)(4,1)S(1)}, s32[]{:S(2)}) async-start(s8[5767168]{0:T(1024)(128)(4,1)} %bitcast.129), calls=%async_computation.5 | async-start | bytes 3145728
  378.3 4.0 %slice-start.3 = ((s8[5767168]{0:T(1024)(128)(4,1)}), s8[1572864]{0:T(1024)(128)(4,1)S(1)}, s32[]{:S(2)}) async-start(s8[5767168]{0:T(1024)(128)(4,1)} %bitcast.126), calls=%async_computation.3 | async-start | bytes 3145728
  379.4 5.8 %slice-start = ((s8[5767168]{0:T(1024)(128)(4,1)}), s8[4194304]{0:T(1024)(128)(4,1)S(1)}, s32[]{:S(2)}) async-start(s8[5767168]{0:T(1024)(128)(4,1)} %bitcast.124), calls=%async_computation | async-start | bytes 8388608
  382.3 3.9 %slice-start.1 = ((s8[5767168]{0:T(1024)(128)(4,1)}), s8[1572864]{0:T(1024)(128)(4,1)S(1)}, s32[]{:S(2)}) async-start(s8[5767168]{0:T(1024)(128)(4,1)} %bitcast.124), calls=%async_computation.1 | async-start | bytes 3145728
  (15 other events, 20.5 us)

commit v4 on v3

--- a/solution.py
+++ b/solution.py
@@ -712,6 +712,105 @@
         return Wire(self, build)
 
 
+class PlaneSum:
+    def __init__(self, net, me, data, buffers, edge, chip, block, rows):
+        self.data, self.rows, self.block, self.me, self.chip = data, rows, block, me, chip
+        self.rc, self.rxa, self.ryb, self.q0, self.q1, self.r0, self.r1 = buffers
+        self.width = data.shape[1]
+        self.edge = edge
+        self.a, self.b = pl.ds(0, edge), pl.ds(edge, self.width - edge)
+        part = lambda ch, cols: data.at[block(ch, me.core), cols]
+        self.cores = [
+            net.wire(
+                lambda k=k: (data.at[block(chip[k], 1 - me.core)], self.rc.at[k], me.over_core)
+            )
+            for k in range(4)
+        ]
+        self.ax0 = net.wire(lambda: (part(chip[3], self.a), self.rxa.at[0], me.over_x))
+        self.by0 = net.wire(lambda: (part(chip[3], self.b), self.ryb.at[0], me.over_y))
+        self.ax1 = net.wire(lambda: (part(chip[1], self.a), self.rxa.at[1], me.over_x))
+        self.by1 = net.wire(lambda: (part(chip[2], self.b), self.ryb.at[1], me.over_y))
+        self.y0 = net.wire(lambda: (self.q0, self.r0, me.over_y))
+        self.x1 = net.wire(lambda: (self.q1, self.r1, me.over_x))
+
+    def base(self, k):
+        return (self.chip[k] * 2 + self.me.core) * self.rows
+
+    def add(self, target, t_at, cols, left, right):
+        def one(r, carry):
+            total = left(r).astype(F32) + right(r).astype(F32)
+            target[row_at(t_at, r), cols] = total.astype(BF)
+            return carry
+
+        lax.fori_loop(0, self.rows // STEP, one, 0)
+
+    def sum_cores(self, k):
+        base, every = self.base(k), pl.ds(0, self.width)
+        self.cores[k].landed()
+        self.add(
+            self.data,
+            base,
+            every,
+            lambda r: self.data[row_at(base, r), every],
+            lambda r: self.rc[k, row_at(0, r), :],
+        )
+
+    def stage_two(self):
+        over_y, over_x = self.base(2), self.base(1)
+        self.ax0.landed()
+        self.add(
+            self.q0,
+            0,
+            pl.ds(0, self.edge),
+            lambda r: self.data[row_at(over_y, r), self.a],
+            lambda r: self.rxa[0, row_at(0, r), :],
+        )
+        self.y0.start()
+        self.by0.landed()
+        self.add(
+            self.q1,
+            0,
+            pl.ds(0, self.width - self.edge),
+            lambda r: self.data[row_at(over_x, r), self.b],
+            lambda r: self.ryb[0, row_at(0, r), :],
+        )
+        self.x1.start()
+
+    def finish(self, last):
+        base = self.base(0)
+        for wire in (self.ax1, self.by1, self.y0, self.x1):
+            wire.landed()
+
+        def final(r, carry):
+            at, big = row_at(0, r), row_at(base, r)
+            one = self.data[big, self.a].astype(F32) + self.rxa[1, at, :].astype(F32)
+            last[at, self.a] = (one + self.r0[at, :].astype(F32)).astype(BF)
+            two = self.data[big, self.b].astype(F32) + self.ryb[1, at, :].astype(F32)
+            last[at, self.b] = (two + self.r1[at, :].astype(F32)).astype(BF)
+            return carry
+
+        lax.fori_loop(0, self.rows // STEP, final, 0)
+
+
+def plane_sum_scratch(rows, width, edge):
+    return [
+        VMEM((4, rows, width), BF),
+        VMEM((2, rows, edge), BF),
+        VMEM((2, rows, width - edge), BF),
+        VMEM((rows, edge), BF),
+        VMEM((rows, width - edge), BF),
+        VMEM((rows, edge), BF),
+        VMEM((rows, width - edge), BF),
+    ]
+
+
+STEP = 16
+
+
+def row_at(base, r):
+    return pl.ds(pl.multiple_of(base + r * STEP, STEP), STEP)
+
+
 def padded(count, to=LANES):
     return -(-count // to) * to
 
@@ -735,7 +834,7 @@
     shard_w = width // 4
     lat_w = latent.shape[1] // 4
     attn_w = attn.shape[1]
-    n_wires = 4 + 12 + 16 + 4 + 6 + (n_tp - 1) + 7 + 14 + 4
+    n_wires = 4 + 12 + 16 + 10 + 10 + (n_tp - 1) + 7 + 14 + 4
     n_col = 4
     col_w = width // n_col
     m_w = 256
@@ -744,11 +843,11 @@
     def body(*refs):
         (two_ref, mid_ref, cot_own_ref, gain_ref) = refs[:4]
         (cot_ref, gate_ref, up_ref, down_ref, sg_ref, su_ref, sd_ref, wr_ref, attn_ref, one_ref, lat_ref) = refs[4:15]
-        (mid_out, gain_out, mid_pack, ya_out, yb_out, dg_out, du_out, dd_out, ds_out, n2_out) = refs[15:25]
-        (attn_out, one_out, lat_out) = refs[25:28]
-        (nb, cb, wgu, wd, gu, gut, hw, hwt, dnb, yb) = refs[28:38]
-        (rc, rxa, ryb, q0, q1, r0, r1, last, got, gus, dds, dss) = refs[38:50]
-        send, recv, load, store = refs[50:]
+        (mid_out, gain_out, mid_pack, y_out, dg_out, du_out, dd_out, ds_out, n2_out) = refs[15:24]
+        (attn_out, one_out, lat_out) = refs[24:27]
+        (nb, cb, wgu, wd, gu, gut, hw, hwt, dnb, yb) = refs[27:37]
+        two_buf, y_buf, (last, got, gus, dds, dss) = refs[37:44], refs[44:51], refs[51:56]
+        send, recv, load, store = refs[56:]
         me = Place(n_tp)
         net = Wires(send, recv)
 
@@ -821,20 +920,9 @@
                     )
                 )
 
-        a, b = pl.ds(0, edge), pl.ds(edge, part_w - edge)
-        flips = [(0, 0), (0, 1), (1, 0), (1, 1)]
-        core_w = [
-            net.wire(
-                lambda k=k: (dnb.at[block(chip(*flips[k]), 1 - me.core)], rc.at[k], me.over_core)
-            )
-            for k in range(4)
-        ]
-        ax0 = net.wire(lambda: (dnb.at[block(chip_d, me.core), a], rxa.at[0], me.over_x))
-        by0 = net.wire(lambda: (dnb.at[block(chip_d, me.core), b], ryb.at[0], me.over_y))
-        ax1 = net.wire(lambda: (dnb.at[block(chip_x, me.core), a], rxa.at[1], me.over_x))
-        by1 = net.wire(lambda: (dnb.at[block(chip_y, me.core), b], ryb.at[1], me.over_y))
-        y0 = net.wire(lambda: (q0, r0, me.over_y))
-        x1 = net.wire(lambda: (q1, r1, me.over_x))
+        chips = [here, chip_x, chip_y, chip_d]
+        two_sum = PlaneSum(net, me, dnb, two_buf, edge, chips, block, rows)
+        y_sum = PlaneSum(net, me, yb, y_buf, edge, chips, block, rows)
         z_w = []
         for k in range(1, n_tp):
             to = lax.rem(me.t + k, n_tp)
@@ -994,33 +1082,6 @@
         for copy in local_copies:
             copy.start()
 
-        step = 16
-
-        def row_at(base, r):
-            return pl.ds(pl.multiple_of(base + r * step, step), step)
-
-        def add(target, t_at, cols, left, right, count):
-            def one(r, carry):
-                total = left(r).astype(F32) + right(r).astype(F32)
-                target[row_at(t_at, r), cols] = total.astype(BF)
-                return carry
-
-            lax.fori_loop(0, count // step, one, 0)
-
-        every = pl.ds(0, part_w)
-
-        def sum_cores(k):
-            base = chip(*flips[k]) * group + me.core * rows
-            core_w[k].landed()
-            add(
-                dnb,
-                base,
-                every,
-                lambda r: dnb[row_at(base, r), every],
-                lambda r: rc[k, row_at(0, r), :],
-                rows,
-            )
-
         def normed_grad(i, carry):
             k = 3 - i
             at = pl.ds(pl.multiple_of(flip_chip(k) * group, group), group)
@@ -1035,54 +1096,28 @@
 
                 @pl.when(k == kk)
                 def _():
-                    core_w[kk].start()
+                    two_sum.cores[kk].start()
                     if kk < 3:
-                        sum_cores(kk + 1)
+                        two_sum.sum_cores(kk + 1)
                     if kk == 2:
-                        ax0.start()
-                        by0.start()
+                        two_sum.ax0.start()
+                        two_sum.by0.start()
                     if kk == 1:
-                        by1.start()
-                        at_direct[0].landed()
-                        at_direct[1].landed()
-                        at_relay.start()
-                        at_fwd[0].start()
-                        at_fwd[1].start()
+                        two_sum.by1.start()
                     if kk == 0:
-                        ax1.start()
+                        two_sum.ax1.start()
 
             return carry
 
         lax.fori_loop(0, 4, normed_grad, 0)
-
-        def stage_two():
-            base_y, base_x = chip_y * group + me.core * rows, chip_x * group + me.core * rows
-            ax0.landed()
-            add(q0, 0, pl.ds(0, edge), lambda r: dnb[row_at(base_y, r), a], lambda r: rxa[0, row_at(0, r), :], rows)
-            y0.start()
-            by0.landed()
-            add(
-                q1,
-                0,
-                pl.ds(0, part_w - edge),
-                lambda r: dnb[row_at(base_x, r), b],
-                lambda r: ryb[0, row_at(0, r), :],
-                rows,
-            )
-            x1.start()
 
         def output(k, carry):
             at = pl.ds(pl.multiple_of(k * group, group), group)
 
             @pl.when(k == 1)
             def _():
-                sum_cores(0)
-
-            @pl.when(k == 3)
-            def _():
-                stage_two()
-                at_relay.landed()
-                at_fwd[2].start()
+                two_sum.sum_cores(0)
+                two_sum.stage_two()
 
             def columns(n, carry):
                 cols = pl.ds(pl.multiple_of(n * col_w, col_w), col_w)
@@ -1093,29 +1128,11 @@
             return carry
 
         lax.fori_loop(0, 4, output, 0)
-        y_copies = [
-            pltpu.make_async_copy(yb.at[:, pl.ds(i * edge, edge)], out, store.at[11 + i])
-            for i, out in enumerate((ya_out, yb_out))
-        ]
-        for copy in y_copies:
-            copy.start()
-
-        def finish_plane():
-            base = here * group + me.core * rows
-            for wire in (ax1, by1, y0, x1):
-                wire.landed()
-
-            def final(r, carry):
-                at, big = row_at(0, r), row_at(base, r)
-                one = dnb[big, a].astype(F32) + rxa[1, at, :].astype(F32) + r0[at, :].astype(F32)
-                two = dnb[big, b].astype(F32) + ryb[1, at, :].astype(F32) + r1[at, :].astype(F32)
-                last[at, a] = one.astype(BF)
-                last[at, b] = two.astype(BF)
-                return carry
-
-            lax.fori_loop(0, rows // step, final, 0)
-            for wire in z_w:
-                wire.start()
+        two_sum.finish(last)
+        for wire in z_w:
+            wire.start()
+        for wire in y_sum.cores:
+            wire.start()
 
         def router_and_norm():
             for wire in z_w:
@@ -1167,13 +1184,26 @@
                         for copy in stores(m - 2, bb):
                             copy.wait()
 
-            @pl.when(m == 2)
+            @pl.when(m == 1)
             def _():
-                finish_plane()
+                for k in range(4):
+                    y_sum.sum_cores(k)
+                for wire in (y_sum.ax0, y_sum.by0, y_sum.ax1, y_sum.by1):
+                    wire.start()
+                at_direct[0].landed()
+                at_direct[1].landed()
+                for wire in (at_relay, at_fwd[0], at_fwd[1]):
+                    wire.start()
+
+            @pl.when(m == 5)
+            def _():
+                router_and_norm()
 
             @pl.when(m == 6)
             def _():
-                router_and_norm()
+                y_sum.stage_two()
+                at_relay.landed()
+                at_fwd[2].start()
 
             both = mdot(gut[...], nb[:, cols])
             gus[buf] = both
@@ -1196,6 +1226,7 @@
         m_hr.start()
         m_l.landed()
         m_hl.start()
+        y_sum.finish(y_out)
         ds_copy = pltpu.make_async_copy(dss, ds_out, store.at[13])
         ds_copy.start()
         for m in (n_m - 2, n_m - 1):
@@ -1203,7 +1234,7 @@
                 copy.wait()
         for wire in [at_direct[2], *at_fwd, *cols_w, m_hr, m_hl]:
             wire.landed()
-        for copy in local_copies + y_copies:
+        for copy in local_copies:
             copy.wait()
         ds_copy.wait()
         for wire in net.all:
@@ -1217,8 +1248,7 @@
         ((piece, width), F32),
         ((1, width), F32),
         ((rows, part_w), BF),
-        ((tokens, edge), BF),
-        ((tokens, edge), BF),
+        ((rows, width), BF),
         (gate.shape, F32),
         (up.shape, F32),
         (down.shape, F32),
@@ -1239,13 +1269,8 @@
         VMEM((H, tokens), BF),
         VMEM((tokens, part_w), BF),
         VMEM((tokens, width), BF),
-        VMEM((4, rows, part_w), BF),
-        VMEM((2, rows, edge), BF),
-        VMEM((2, rows, part_w - edge), BF),
-        VMEM((rows, edge), BF),
-        VMEM((rows, part_w - edge), BF),
-        VMEM((rows, edge), BF),
-        VMEM((rows, part_w - edge), BF),
+        *plane_sum_scratch(rows, part_w, edge),
+        *plane_sum_scratch(rows, width, edge),
         VMEM((rows, part_w), BF),
         VMEM((n_tp - 1, piece, part_w), BF),
         VMEM((2, 2 * H, m_w), F32),
@@ -1256,7 +1281,7 @@
         body,
         out_shape=tuple(jax.ShapeDtypeStruct(*o) for o in outs),
         in_specs=[pl.BlockSpec(memory_space=VMEM)] * 4 + [pl.BlockSpec(memory_space=ANY)] * 11,
-        out_specs=(*[pl.BlockSpec(memory_space=VMEM)] * 3, *[pl.BlockSpec(memory_space=ANY)] * 10),
+        out_specs=(*[pl.BlockSpec(memory_space=VMEM)] * 4, *[pl.BlockSpec(memory_space=ANY)] * 8),
         scratch_shapes=[
             *scratch,
             pltpu.SemaphoreType.DMA((n_wires,)),
@@ -1269,6 +1294,474 @@
         ),
         name="feed_forward",
     )(*ins)
+
+
+class Background:
+    def __init__(self):
+        self.runs = []
+
+    def add(self, run):
+        next(run)
+        self.runs.append(run)
+
+    def step(self):
+        self.runs = [r for r in self.runs if next(r, None) is not None]
+
+    def drain(self):
+        while self.runs:
+            self.step()
+
+
+def fold_heads(a, b, lane):
+    def fold(v):
+        v = v + pltpu.roll(v, 64, 1)
+        return v + pltpu.roll(v, 32, 1)
+
+    return jnp.where(lane < DR // 2, fold(a), jnp.where(lane < DR, fold(b), 0.0))
+
+
+def attention_back(
+    mid_pack, attn, prob, kv, keys_rope, q_nope, q_rope, tables, compressed, gains_in, rows_in, y_part, shared_grads,
+    w_output, w_expand, w_query, w_latent_t, gain_two_sum, n_tp,
+):
+    rows, part_w = mid_pack.shape
+    width = w_output.shape[1]
+    piece = rows // n_tp
+    n_head = prob.shape[0]
+    nope_w = n_head * DN
+    q_w = nope_w + 2 * LANES
+    kv_w = kv.shape[1]
+    lat_w = 5 * LANES
+    back_w = width + KVR + LANES
+    scale = (DN + DR) ** (-0.5)
+    f32 = lambda *shape: jax.ShapeDtypeStruct(shape, F32)
+    bf = lambda *shape: jax.ShapeDtypeStruct(shape, BF)
+    subs = dict(
+        y=tp_reduce_scatter(bf(rows, width), n_tp),
+        mid=plane_columns(bf(rows, width)),
+        logit=plane_gather(bf(rows, part_w - width), 1),
+        shared=plane_columns(shared_grads),
+        head=plane_gather(bf(rows, q_w + kv_w)),
+        back=tp_reduce_scatter(bf(rows, back_w), n_tp),
+        out=tp_all_gather(bf(piece, width), n_tp),
+        inp=tp_all_gather(bf(piece, width), n_tp),
+        lat=gather_rows(bf(piece, lat_w), n_tp),
+        gain=sum_everywhere(f32(16, 512), n_tp),
+    )
+    own_scratch = [
+        VMEM(w_output.shape, BF),
+        VMEM(w_expand.shape, BF),
+        VMEM(w_query.shape, BF),
+        VMEM((lat_w, width), BF),
+        VMEM((rows, nope_w), BF),
+        VMEM((2 * rows, kv_w + LANES), F32),
+        VMEM((rows, kv_w + LANES), BF),
+        VMEM((rows, kv_w + LANES), BF),
+        VMEM((rows, q_w + kv_w), BF),
+        VMEM((rows, back_w), BF),
+        VMEM((piece, width), F32),
+        VMEM((piece, back_w), F32),
+        VMEM((piece, width), BF),
+        VMEM((piece, width), BF),
+        VMEM((piece, lat_w), BF),
+        VMEM((16, 512), F32),
+    ]
+    at, sub_at = len(own_scratch), {}
+    for key, job in subs.items():
+        sub_at[key] = (at, at + len(job.scratch))
+        at += len(job.scratch)
+
+    def run(net, me, ins, outs, scratch):
+        (mid_ref, attn_ref, prob_ref, kv_ref, ka_ref, kb_ref, qn_ref, qa_ref, qb_ref, cos_ref, sin_ref) = ins[:11]
+        (comp_ref, gk_ref, g1_ref, x_ref, mg_ref, m_ref, y_ref, gt_ref) = ins[11:19]
+        (ds_ref, wo_ref, we_ref, wq_ref, wl_ref) = ins[19:]
+        (block_out, input_out, gain_out, mid_out, logit_out, shared_out, head_out, lat_out) = outs
+        (wo, we, wq, wl, ogb, terms, swap_src, swap_got, head, part) = scratch[:10]
+        (y32, back32, ob, ib, lat, gains) = scratch[10:16]
+
+        def sub(key, src, dst):
+            a, b = sub_at[key]
+            return subs[key].run(net, me, (src,), (dst,), scratch[a:b])
+
+        loads = [
+            net.move(wo_ref, wo),
+            net.move(we_ref, we),
+            net.move(wq_ref, wq),
+            net.move(wl_ref, wl.at[pl.ds(0, KVR + DR)]),
+        ]
+        bg = Background()
+        y_run = sub("y", y_ref, y32)
+        next(y_run)
+        bg.add(sub("mid", mid_ref.at[:, pl.ds(0, width)], mid_out))
+        bg.add(sub("logit", mid_ref.at[:, pl.ds(width, part_w - width)], logit_out))
+        wl[KVR + DR :, :] = jnp.zeros((lat_w - KVR - DR, width), BF)
+        lane = lax.broadcasted_iota(jnp.int32, (rows, LANES), 1)
+        lane2 = lax.broadcasted_iota(jnp.int32, (2 * rows, LANES), 1)
+
+        loads[0].wait()
+        out_grad = dot_nt(mid_ref[:, 0:width], wo[...])
+        ogb[...] = out_grad.astype(BF)
+        weighted = out_grad * attn_ref[...].astype(F32)
+        dqa = jnp.zeros((rows, LANES), F32)
+        dqb, dka, dkb = dqa, jnp.zeros((2 * rows, LANES), F32), jnp.zeros((2 * rows, LANES), F32)
+        for h in range(n_head):
+            mine = (lane >= h * (DR // 2)) & (lane < (h + 1) * (DR // 2))
+            k_at, v_at = pl.ds(h * (DN + DV), DN), pl.ds(h * (DN + DV) + DN, DV)
+            og_h = ogb[:, h * DV : (h + 1) * DV]
+            p = prob_ref[h]
+            delta = jnp.sum(weighted[:, h * DV : (h + 1) * DV], axis=1, keepdims=True)
+            ds = (p * (dot_nt(og_h, kv_ref[:, v_at]) - delta)).astype(BF)
+            head[:, h * DN : (h + 1) * DN] = (mdot(ds, kv_ref[:, k_at]) * scale).astype(BF)
+            dqa = dqa + jnp.where(mine, mdot(ds, ka_ref[...]), 0.0)
+            dqb = dqb + jnp.where(mine, mdot(ds, kb_ref[...]), 0.0)
+            terms[:, k_at] = dot_tn(ds, qn_ref[:, h * DN : (h + 1) * DN]) * scale
+            terms[:, v_at] = dot_tn(p.astype(BF), og_h)
+            zero = jnp.zeros((), BF)
+            dka = dka + dot_tn(ds, jnp.where(mine, qa_ref[...], zero))
+            dkb = dkb + dot_tn(ds, jnp.where(mine, qb_ref[...], zero))
+        terms[:, kv_w:] = fold_heads(dka * scale, dkb * scale, lane2)
+        theirs = pl.ds(pl.multiple_of((1 - me.c) * rows, rows), rows)
+        swap_src[...] = terms[theirs, :].astype(BF)
+        swap = net.put(swap_src, swap_got, me.over_x)
+        dqa, dqb = dqa * scale, dqb * scale
+        cos, sin = cos_ref[...], sin_ref[...]
+        head[:, nope_w : nope_w + LANES] = (dqa * cos + dqb * sin).astype(BF)
+        head[:, nope_w + LANES : q_w] = (dqb * cos - dqa * sin).astype(BF)
+        next(y_run, None)
+        ob[...] = (m_ref[...] + y32[...]).astype(BF)
+        out_run = sub("out", ob, block_out)
+        next(out_run)
+        yield 1
+        for load in loads[1:]:
+            load.wait()
+        n_col = 4
+        col_w = width // n_col
+
+        def columns(n, carry):
+            cols = pl.ds(pl.multiple_of(n * col_w, col_w), col_w)
+            part[:, cols] = dot_nt(head[:, 0:q_w], wq[cols, :]).astype(BF)
+            return carry
+
+        lax.fori_loop(0, n_col, columns, 0)
+        swap.wait_recv()
+        ours = pl.ds(pl.multiple_of(me.c * rows, rows), rows)
+        head[:, q_w:] = (terms[ours, 0:kv_w] + swap_got[:, 0:kv_w].astype(F32)).astype(BF)
+        rope = terms[ours, kv_w:] + swap_got[:, kv_w:].astype(F32)
+        part[:, width : width + KVR] = dot_nt(head[:, q_w:], we[...]).astype(BF)
+        turned = jnp.where(
+            lane < DR // 2,
+            rope * cos + pltpu.roll(rope, LANES - DR // 2, 1) * sin,
+            jnp.where(lane < DR, rope * cos - pltpu.roll(rope, DR // 2, 1) * sin, 0.0),
+        )
+        part[:, width + KVR :] = turned.astype(BF)
+        back_run = sub("back", part, back32)
+        next(back_run)
+        bg.add(sub("head", head, head_out))
+        bg.add(out_run)
+        next(back_run, None)
+        comp_grad, gk = norm_back(comp_ref[...], gk_ref[...], back32[:, width : width + KVR])
+        lat[:, 0:KVR] = comp_grad.astype(BF)
+        lat[:, KVR:] = back32[:, width + KVR :].astype(BF)
+        one_grad = back32[:, 0:width] + mdot(lat[...], wl[...])
+        lat_run = sub("lat", lat, lat_out)
+        next(lat_run)
+        norm_grad, g1 = norm_back(x_ref[...], g1_ref[...], one_grad)
+        ib[...] = (mg_ref[...] + norm_grad).astype(BF)
+        bg.add(sub("inp", ib, input_out))
+        gains[...] = jnp.zeros_like(gains)
+        g1 = jnp.sum(g1, axis=0, keepdims=True)
+        for i in range(4):
+            gains[i : i + 1, :] = g1[:, i * 512 : (i + 1) * 512]
+            gains[4 + i : 5 + i, :] = gt_ref[:, i * 512 : (i + 1) * 512]
+        gains[8:9, :] = jnp.sum(gk, axis=0, keepdims=True)
+        bg.add(sub("gain", gains, gain_out))
+        bg.add(sub("shared", ds_ref, shared_out))
+        bg.add(lat_run)
+        bg.drain()
+
+    spaces = [VMEM] * 19 + [ANY] * 5
+    ins = (
+        mid_pack, attn, prob, kv, *keys_rope, q_nope, *q_rope, *tables,
+        compressed, *gains_in, *rows_in, y_part, gain_two_sum,
+        shared_grads, w_output, w_expand, w_query, w_latent_t,
+    )
+    outs = [
+        ((rows, width), BF, VMEM),
+        ((rows, width), BF, VMEM),
+        ((16, 512), F32, VMEM),
+        *subs["mid"].outs,
+        *subs["logit"].outs,
+        *subs["shared"].outs,
+        *subs["head"].outs,
+        *subs["lat"].outs,
+    ]
+    return Job(
+        run,
+        list(zip(ins, spaces)),
+        outs,
+        own_scratch + [s for job in subs.values() for s in job.scratch],
+        1 + sum(job.n_put for job in subs.values()),
+        4 + sum(job.n_local for job in subs.values()),
+        "xykzp",
+    )
+
+
+def attention_forward(
+    block, tables, w_query, w_latent_t, w_expand, w_output, router_t, small, cot_pack, shared, n_tp
+):
+    rows, width = block.shape
+    piece = rows // n_tp
+    q_w = w_query.shape[1]
+    nope_w = q_w - 2 * LANES
+    n_head = nope_w // DN
+    kv_w = w_expand.shape[1]
+    lat_rows = w_latent_t.shape[0]
+    lat_pad = padded(lat_rows)
+    scale = (DN + DR) ** (-0.5)
+    k_w, e_w = w_query.shape[0], w_expand.shape[0]
+    shard_w = w_output.shape[1]
+    f32 = lambda *shape: jax.ShapeDtypeStruct(shape, F32)
+    bf = lambda *shape: jax.ShapeDtypeStruct(shape, BF)
+    subs = dict(
+        cot=plane_gather(cot_pack),
+        sg=shard_rows(shared[0]),
+        su=shard_rows(shared[1]),
+        sd=shard_rows(shared[2]),
+        rs=tp_reduce_scatter(bf(rows, width), n_tp),
+    )
+    own_scratch = [
+        VMEM((4 * k_w, q_w), BF),
+        VMEM((lat_pad, width), BF),
+        VMEM((4 * e_w, kv_w), BF),
+        VMEM((w_output.shape[0], width), BF),
+        VMEM((router_t.shape[0], width), BF),
+        VMEM((4, *small.shape), F32),
+        VMEM((rows, width), BF),
+        VMEM((2 * rows, width), BF),
+        VMEM((2 * rows, KVR), F32),
+        VMEM((2 * rows, KVR), BF),
+        VMEM((rows, width), BF),
+        VMEM((piece, width), F32),
+    ]
+    at, sub_at = len(own_scratch), {}
+    for key, job in subs.items():
+        sub_at[key] = (at, at + len(job.scratch))
+        at += len(job.scratch)
+
+    def run(net, me, ins, outs, scratch):
+        x_ref, cos_ref, sin_ref = ins[:3]
+        wq_in, wl_in, we_in, wo_in, rt_in, small_in, cot_in = ins[3:10]
+        shared_in = ins[10:13]
+        (mid_out, two_out, attn_out, prob_out, kv_out, ka_out, kb_out, qn_out, qa_out, qb_out) = outs[:10]
+        (comp_out, one_out, latn_out, gain_out) = outs[10:14]
+        weights_out, cot_out, shared_out = outs[14:19], outs[19], outs[20:23]
+        (wq, wl, we, wo, rt, small_all, xo, n1, lat32, ln, part, res) = scratch[:12]
+
+        def sub(key, src, dst):
+            a, b = sub_at[key]
+            return subs[key].run(net, me, (src,), (dst,), scratch[a:b])
+
+        other = lax.rem(me.s + 2, 4)
+
+        def stacked(ref, size):
+            def place(s, which=None):
+                if which is None:
+                    return ref.at[pl.ds(pl.multiple_of(s * size, size), size)]
+                half = size // 2
+                return ref.at[pl.ds(pl.multiple_of(s * size + which * half, half), half)]
+
+            return place
+
+        def beside(ref, count):
+            def place(s, which=None):
+                cols = pl.ds(pl.multiple_of(s * shard_w, shard_w), shard_w)
+                if which is None:
+                    return ref.at[pl.ds(0, count), cols]
+                half = count // 2
+                return ref.at[pl.ds(pl.multiple_of(which * half, half), half), cols]
+
+            return place
+
+        halved = [
+            (wq_in, k_w, stacked(wq, k_w)),
+            (wl_in, lat_rows, beside(wl, lat_rows)),
+            (we_in, e_w, stacked(we, e_w)),
+        ]
+        whole = [
+            (small_in, lambda s: small_all.at[s]),
+            (wo_in, beside(wo, w_output.shape[0])),
+            (rt_in, beside(rt, router_t.shape[0])),
+        ]
+        local = [net.move(ref, place(me.s)) for ref, _, place in halved]
+        local += [net.move(ref, place(me.s)) for ref, place in whole]
+        whole_y = [net.put(small_in, small_all.at[me.s], me.over_y)]
+        whole_c = [net.put(small_in, small_all.at[me.s], me.over_core)]
+        half_y, half_c = [], []
+        for i, (ref, count, place) in enumerate(halved):
+            rows_c = pl.ds(pl.multiple_of(me.c * (count // 2), count // 2), count // 2)
+            half_y.append(net.put(ref.at[rows_c], place(me.s, me.c), me.over_y))
+            if i == 0:
+                x_wire = net.put(x_ref, xo, me.over_x)
+            half_c.append(net.put(ref, place(me.s), me.over_core))
+        for ref, place in whole[1:]:
+            whole_y.append(net.put(ref, place(me.s), me.over_y))
+            whole_c.append(net.put(ref, place(me.s), me.over_core))
+        wl[lat_rows:, :] = jnp.zeros((lat_pad - lat_rows, width), BF)
+
+        whole_y[0].wait_recv()
+        fwd = [net.put(small_all.at[other], small_all.at[other], me.over_core)]
+        whole_c[0].wait_recv()
+        fwd[0].wait_recv()
+        local[3].wait()
+        gain_out[...] = jnp.zeros_like(gain_out)
+        for s in range(4):
+            for i in range(4):
+                cols = pl.ds((4 * s + i) * LANES, LANES)
+                gain_out[0:1, cols] = small_all[s, i : i + 1, :]
+                gain_out[1:2, cols] = small_all[s, 4 + i : 5 + i, :]
+            gain_out[2:3, s * LANES : (s + 1) * LANES] = small_all[s, 8:9, :]
+
+        def norm_rows_into(src, base):
+            def one(r, carry):
+                v = src[row_at(0, r), :].astype(F32)
+                n1[row_at(base, r), :] = norm_rows(v, gain_out[0:1, :]).astype(BF)
+                return carry
+
+            lax.fori_loop(0, rows // STEP, one, 0)
+
+        ours, theirs = me.c * rows, (1 - me.c) * rows
+        norm_rows_into(x_ref, ours)
+        at_us = pl.ds(pl.multiple_of(ours, rows), rows)
+        one_out[...] = n1[at_us, :]
+        half_x, relays = [], []
+        for got, (_, _, place) in zip(half_y, halved):
+            got.wait_recv()
+            piece_ref = place(other, me.c)
+            half_x.append(net.put(piece_ref, piece_ref, me.over_x))
+            relays.append(net.put(piece_ref, piece_ref, me.over_core))
+        x_wire.wait_recv()
+        norm_rows_into(xo, theirs)
+        for got, (_, place) in zip(whole_y[1:], whole[1:]):
+            got.wait_recv()
+            relays.append(net.put(place(other), place(other), me.over_core))
+        for got, (_, _, place) in zip(half_x, halved):
+            got.wait_recv()
+            piece_ref = place(other, 1 - me.c)
+            relays.append(net.put(piece_ref, piece_ref, me.over_core))
+        bg = Background()
+        bg.add(sub("cot", cot_in, cot_out))
+        for key, src, dst in zip(("sg", "su", "sd"), shared_in, shared_out):
+            bg.add(sub(key, src, dst))
+        for got in half_c + whole_c[1:] + relays:
+            got.wait_recv()
+        for copy in local[:3] + local[4:]:
+            copy.wait()
+        stores = [
+            net.move(src, dst)
+            for src, dst in zip((wq, wl.at[pl.ds(0, lat_rows)], we, wo, rt), weights_out)
+        ]
+
+        lane = lax.broadcasted_iota(jnp.int32, (rows, LANES), 1)
+        lane2 = lax.broadcasted_iota(jnp.int32, (2 * rows, LANES), 1)
+        query = mdot(n1[at_us, :], wq[...])
+        cos, sin = cos_ref[at_us, :], sin_ref[at_us, :]
+        a, b = query[:, nope_w : nope_w + LANES], query[:, nope_w + LANES :]
+        qn_out[...] = query[:, :nope_w].astype(BF)
+        qa_out[...] = (a * cos - b * sin).astype(BF)
+        qb_out[...] = (a * sin + b * cos).astype(BF)
+        latent = dot_nt(n1[...], wl[...])
+        lat32[...] = latent[:, :KVR]
+        ln[...] = norm_rows(latent[:, :KVR], gain_out[2:3, 0:KVR]).astype(BF)
+        latn_out[...] = ln[at_us, :]
+        comp_out[...] = lat32[pl.ds(pl.multiple_of(ours + me.t * piece, piece), piece), :]
+
+        def spread_heads(v):
+            v = jnp.where(lane2 < DR // 2, v, 0.0)
+            v = v + pltpu.roll(v, DR // 2, 1)
+            return v + pltpu.roll(v, DR, 1)
+
+        tile = latent[:, KVR:]
+        a, b = spread_heads(tile), spread_heads(pltpu.roll(tile, LANES - DR // 2, 1))
+        ka_out[...] = (a * cos_ref[...] - b * sin_ref[...]).astype(BF)
+        kb_out[...] = (a * sin_ref[...] + b * cos_ref[...]).astype(BF)
+        kv_out[...] = mdot(ln[...], we[...]).astype(BF)
+        q_pos = ours + lax.broadcasted_iota(jnp.int32, (rows, 2 * rows), 0)
+        k_pos = lax.broadcasted_iota(jnp.int32, (rows, 2 * rows), 1)
+        zero = jnp.zeros((), BF)
+        for h in range(n_head):
+            mine = (lane >= h * (DR // 2)) & (lane < (h + 1) * (DR // 2))
+            k_at, v_at = pl.ds(h * (DN + DV), DN), pl.ds(h * (DN + DV) + DN, DV)
+            score = dot_nt(qn_out[:, h * DN : (h + 1) * DN], kv_out[:, k_at])
+            score = score + dot_nt(jnp.where(mine, qa_out[...], zero), ka_out[...])
+            score = score + dot_nt(jnp.where(mine, qb_out[...], zero), kb_out[...])
+            score = jnp.where(k_pos <= q_pos, score * scale, NEG)
+            top = jnp.max(score, axis=1, keepdims=True)
+            expo = jnp.exp(score - top)
+            total = jnp.sum(expo, axis=1, keepdims=True)
+            value = mdot(expo.astype(BF), kv_out[:, v_at])
+            attn_out[:, h * DV : (h + 1) * DV] = (value / total).astype(BF)
+            prob_out[h] = jnp.exp(score - (top + jnp.log(total)))
+        n_col = 4
+        col_w = width // n_col
+
+        def columns(n, carry):
+            cols = pl.ds(pl.multiple_of(n * col_w, col_w), col_w)
+            part[:, cols] = mdot(attn_out[...], wo[:, cols]).astype(BF)
+            return carry
+
+        lax.fori_loop(0, n_col, columns, 0)
+        rs = sub("rs", part, res)
+        next(rs)
+        yield 1
+        for _ in range(3):
+            bg.step()
+        next(rs, None)
+        quarter = pl.ds(pl.multiple_of(me.t * piece, piece), piece)
+        mid = x_ref[quarter, :].astype(F32) + res[...]
+        mid_out[...] = mid
+        two_out[...] = norm_rows(mid, gain_out[1:2, :]).astype(BF)
+        bg.drain()
+        for store in stores:
+            store.wait()
+
+    ins = (
+        block, *tables,
+        w_query, w_latent_t, w_expand, w_output, router_t, small, cot_pack, *shared,
+    )
+    outs = [
+        ((piece, width), F32, VMEM),
+        ((piece, width), BF, VMEM),
+        ((rows, n_head * DV), BF, VMEM),
+        ((n_head, rows, 2 * rows), F32, VMEM),
+        ((2 * rows, kv_w), BF, VMEM),
+        ((2 * rows, LANES), BF, VMEM),
+        ((2 * rows, LANES), BF, VMEM),
+        ((rows, nope_w), BF, VMEM),
+        ((rows, LANES), BF, VMEM),
+        ((rows, LANES), BF, VMEM),
+        ((piece, KVR), F32, VMEM),
+        ((rows, width), BF, VMEM),
+        ((rows, KVR), BF, VMEM),
+        ((8, width), F32, VMEM),
+        ((4 * k_w, q_w), BF, ANY),
+        ((lat_rows, width), BF, ANY),
+        ((4 * e_w, kv_w), BF, ANY),
+        ((w_output.shape[0], width), BF, ANY),
+        ((router_t.shape[0], width), BF, ANY),
+        *subs["cot"].outs,
+        *subs["sg"].outs,
+        *subs["su"].outs,
+        *subs["sd"].outs,
+    ]
+    return Job(
+        run,
+        list(zip(ins, [VMEM] * 3 + [ANY] * 10)),
+        outs,
+        own_scratch + [s for job in subs.values() for s in job.scratch],
+        25 + sum(job.n_put for job in subs.values()),
+        11 + sum(job.n_local for job in subs.values()),
+        "xykzp",
+    )
 
 
 def per_device(
@@ -1295,12 +1788,23 @@
     topk = routes.shape[1]
     experts = router_weight.shape[1]
     heads = q_weight.shape[1] // (DN + DR)
-    scale = (DN + DR) ** (-0.5)
     piece = rows // n_tp
     s_id, c_id, t_id = lax.axis_index(SHARD), lax.axis_index(CTX), lax.axis_index(TP)
     shard_w = width // 4
     kv_w = KVR // 4
-    pad = LANES - experts
+
+    by_head = q_weight.reshape(-1, heads, DN + DR)
+    q_weight = jnp.concatenate(
+        [
+            by_head[:, :, :DN].reshape(-1, heads * DN),
+            by_head[:, :, DN : DN + DR // 2].reshape(-1, LANES),
+            by_head[:, :, DN + DR // 2 :].reshape(-1, LANES),
+        ],
+        axis=1,
+    )
+
+    def own(a):
+        return lax.dynamic_slice_in_dim(a, t_id * piece, piece, 0)
 
     small = jnp.concatenate(
         [
@@ -1309,88 +1813,47 @@
             kv_norm_gain.reshape(-1, LANES),
             jnp.zeros((7, LANES), BF),
         ]
-    )
-    (gathered,) = comm_kernel(
+    ).astype(F32)
+    cot_pack = jnp.concatenate(
+        [cotangent.astype(BF), jnp.pad(routes.astype(BF), ((0, 0), (0, LANES - topk)))], axis=1
+    )
+    tables = [jnp.tile(v, (1, heads)) for v in rope_tables(2 * rows, jnp.float32(0))]
+    (
+        (
+            mid, two_own, attn_flat, prob, kv_flat, keys_first, keys_second, q_nope, q_first, q_second,
+            compressed, normed_one, latent_own, gains_all, w_query, w_latent_t, w_expand, w_output, router_t,
+            cot_all, sg_t, su_t, sd,
+        ),
+    ) = comm_kernel(
         [
-            shard_gather(
-                [
-                    (q_weight, False),
-                    (kva_weight.T, True),
-                    (kvb_weight, False),
-                    (small, False),
-                    (out_weight, True),
-                    (router_weight.T, True),
-                ],
+            attention_forward(
                 block_input,
+                tables,
+                q_weight,
+                kva_weight.T,
+                kvb_weight,
+                out_weight,
+                router_weight.T,
+                small,
+                cot_pack,
+                (shared_gate.T, shared_up.T, shared_down),
+                n_tp,
             )
         ],
         n_tp,
         0,
-        "start",
-    )
-    w_query, w_latent_t, w_expand, small_all, w_output, router_t, x_pair = gathered
-    w_query = w_query.reshape(width, -1)
-    w_expand = w_expand.reshape(KVR, -1)
-    gain_one = small_all[:, 0:4].reshape(-1)
-    gain_two = small_all[:, 4:8].reshape(-1)
-    gain_kv = small_all[:, 8:9].reshape(-1)
-
-    x_float = block_input.astype(F32)
-    cosine, sine = rope_tables(rows, (c_id * rows).astype(F32))
-    cos_all, sin_all = rope_tables(2 * rows, jnp.float32(0))
-    normed_pair = norm_rows(x_pair.reshape(2 * rows, width).astype(F32), gain_one).astype(BF)
-    normed_one = norm_rows(x_float, gain_one).astype(BF)
-    query = mdot(normed_one, w_query).reshape(rows, heads, DN + DR)
-    query_nope = query[..., :DN].astype(BF)
-    query_rope = rotate(query[..., DN:], cosine[:, None, :], sine[:, None, :]).astype(BF)
-    latent = dot_nt(normed_pair, w_latent_t)
-    latent_pair = norm_rows(latent[:, :KVR], gain_kv).astype(BF)
-    rope_pair = rotate(latent[:, KVR:], cos_all, sin_all).astype(BF)
-    kv_pair = mdot(latent_pair, w_expand).astype(BF).reshape(2 * rows, heads, DN + DV)
-    key_pair, value_pair = kv_pair[..., :DN], kv_pair[..., DN:]
-    score = jnp.einsum("qhd,khd->hqk", query_nope, key_pair, preferred_element_type=F32)
-    score = score + jnp.einsum("qhd,kd->hqk", query_rope, rope_pair, preferred_element_type=F32)
-    q_pos = c_id * rows + jnp.arange(rows, dtype=jnp.int32)
-    k_pos = jnp.arange(2 * rows, dtype=jnp.int32)
-    score = jnp.where(k_pos[None, None, :] <= q_pos[None, :, None], score * scale, NEG)
-    top = jnp.max(score, axis=-1, keepdims=True)
-    expo = jnp.exp(score - top)
-    total = jnp.sum(expo, axis=-1, keepdims=True)
-    attn = jnp.einsum("hqk,khd->hqd", expo.astype(BF), value_pair, preferred_element_type=F32)
-    attn_rows = (attn / total).astype(BF).transpose(1, 0, 2)
-    lse = top + jnp.log(total)
-    attn_flat = attn_rows.reshape(rows, heads * DV)
-
-    def own(a):
-        return lax.dynamic_slice_in_dim(a, t_id * piece, piece, 0)
-
-    cot_pack = jnp.concatenate(
-        [cotangent.astype(BF), jnp.pad(routes.astype(BF), ((0, 0), (0, LANES - topk)))], axis=1
-    )
-    (attn_full,), (cot_all,), (sg_t,), (su_t,), (sd,) = comm_kernel(
-        [
-            tp_reduce_scatter(mdot(attn_flat, w_output).astype(BF), n_tp),
-            plane_gather(cot_pack),
-            shard_rows(shared_gate.T),
-            shard_rows(shared_up.T),
-            shard_rows(shared_down),
-        ],
-        n_tp,
-        1,
-        "middle",
-    )
-    mid = own(x_float) + attn_full
-    two_own = norm_rows(mid, gain_two).astype(BF)
-    latent_own = lax.dynamic_slice_in_dim(latent_pair, c_id * rows, rows, 0)
+        "attention",
+    )
+    x_own = own(block_input).astype(F32)
 
     (
-        mid_grad, gain_two_sum, mid_pack, y_left, y_right, grad_gate, grad_up, grad_expert_down, shared_grads,
+        mid_grad, gain_two_sum, mid_pack, y_part, grad_gate, grad_up, grad_expert_down, shared_grads,
         two_cols, attn_all, one_cols, lat_cols,
     ) = feed_forward(
         two_own,
         mid,
         own(cotangent),
-        gain_two.astype(F32)[None, :],
+        gains_all[1:2],
         cot_all,
         expert_gate.transpose(0, 2, 1),
         expert_up.transpose(0, 2, 1),
@@ -1405,98 +1868,47 @@
         topk,
         n_tp,
     )
-    mid_b = mid_pack[:, :width]
-
-    out_grad = dot_nt(mid_b, w_output).reshape(rows, heads, DV)
-    out_grad_b = out_grad.astype(BF)
-    delta = jnp.sum(out_grad * attn_rows.astype(F32), axis=-1).T[..., None]
-    prob = jnp.exp(score - lse)
-    dprob = jnp.einsum("qhd,khd->hqk", out_grad_b, value_pair, preferred_element_type=F32)
-    dscore = (prob * (dprob - delta)).astype(BF)
-    nope_grad = jnp.einsum("hqk,khd->qhd", dscore, key_pair, preferred_element_type=F32) * scale
-    rope_qgrad = jnp.einsum("hqk,kd->qhd", dscore, rope_pair, preferred_element_type=F32) * scale
-    key_grad = jnp.einsum("hqk,qhd->khd", dscore, query_nope, preferred_element_type=F32) * scale
-    value_grad = jnp.einsum(
-        "hqk,qhd->khd", prob.astype(BF), out_grad_b, preferred_element_type=F32
-    )
-    rope_kgrad = jnp.einsum("hqk,qhd->kd", dscore, query_rope, preferred_element_type=F32) * scale
-    kv_terms = jnp.concatenate(
+    ((block_output, input_grad, gains, mid_cols, logit_all, shared_cols, head_all, lat_all),) = comm_kernel(
         [
-            jnp.concatenate([key_grad, value_grad], axis=-1).reshape(2 * rows, -1),
-            jnp.pad(rope_kgrad, ((0, 0), (0, LANES - DR))),
-        ],
-        axis=1,
-    )
-    mine = lax.dynamic_slice_in_dim(kv_terms, c_id * rows, rows, 0)
-    other = lax.dynamic_slice_in_dim(kv_terms, (1 - c_id) * rows, rows, 0).astype(BF)
-    (swapped,), (y_left,), (mid_cols,), (logit_all,) = comm_kernel(
-        [
-            ctx_swap(other),
-            reduce_everywhere(y_left, n_tp),
-            plane_columns(mid_b),
-            plane_gather(mid_pack[:, width:], 1),
+            attention_back(
+                mid_pack,
+                attn_flat,
+                prob,
+                kv_flat,
+                [keys_first, keys_second],
+                q_nope,
+                [q_first, q_second],
+                [lax.dynamic_slice_in_dim(v, c_id * rows, rows, 0) for v in tables],
+                compressed,
+                [gains_all[2:3, :KVR], gains_all[0:1]],
+                [x_own, mid_grad, mid],
+                y_part,
+                shared_grads.reshape(-1, width),
+                w_output,
+                w_expand,
+                w_query,
+                w_latent_t,
+                gain_two_sum,
+                n_tp,
+            )
         ],
         n_tp,
         2,
-        "swap",
-    )
-    kv_sum = mine + swapped.astype(F32)
-    kv_grad = kv_sum[:, : heads * (DN + DV)].astype(BF)
-    rope_part = rotate_back(kv_sum[:, heads * (DN + DV) :][:, :DR], cosine, sine)
-    rope_qback = rotate_back(rope_qgrad, cosine[:, None, :], sine[:, None, :])
-    query_grad = jnp.concatenate([nope_grad, rope_qback], axis=-1).astype(BF).reshape(rows, -1)
-    latent_part = dot_nt(kv_grad, w_expand)
-    one_part = dot_nt(query_grad, w_query)
-    back_part = jnp.concatenate(
-        [one_part, latent_part, jnp.pad(rope_part, ((0, 0), (0, LANES - DR)))], axis=1
-    ).astype(BF)
-    (back,), (y_right,), (shared_cols,) = comm_kernel(
-        [
-            tp_reduce_scatter(back_part, n_tp),
-            reduce_everywhere(y_right, n_tp),
-            plane_columns(shared_grads.reshape(-1, width)),
-        ],
-        n_tp,
-        3,
         "back",
-    )
-    out_own = mid + jnp.concatenate([y_left, y_right], axis=1)
-
-    compressed = own(lax.dynamic_slice_in_dim(latent, c_id * rows, rows, 0))[:, :KVR]
-    compressed_grad, gain_kv_terms = norm_back(compressed, gain_kv, back[:, width : width + KVR])
-    latent_grad = jnp.concatenate(
-        [compressed_grad, back[:, width + KVR : width + KVR + DR]], axis=1
-    ).astype(BF)
-    one_grad = back[:, :width] + mdot(latent_grad, w_latent_t)
-    input_norm_grad, gain_one_terms = norm_back(own(x_float), gain_one, one_grad)
-    input_own = mid_grad + input_norm_grad
-
-    lat_pack = jnp.pad(latent_grad, ((0, 0), (0, 5 * LANES - KVR - DR)))
-    gains = jnp.concatenate(
-        [
-            jnp.sum(gain_one_terms, axis=0),
-            gain_two_sum[0],
-            jnp.sum(gain_kv_terms, axis=0),
-            jnp.zeros((512,), F32),
-        ]
-    ).reshape(8, -1)
-    (lat_all,), (head_all,), (block_output,), (input_grad,), (gains,) = comm_kernel(
-        [
-            gather_rows(lat_pack, n_tp),
-            plane_gather(jnp.concatenate([query_grad, kv_grad], axis=1)),
-            tp_all_gather(out_own.astype(BF), n_tp),
-            tp_all_gather(input_own.astype(BF), n_tp),
-            sum_everywhere(gains, n_tp),
-        ],
-        n_tp,
-        5,
-        "finish",
     )
     head_all = head_all.reshape(8 * rows, -1)
     split = heads * (DN + DR)
     lat_all = lat_all.reshape(8 * rows, -1)[:, : KVR + DR]
     one_cols = one_cols.reshape(8 * rows, -1)
     grad_query = dot_tn(one_cols, head_all[:, :split])
+    grad_query = jnp.concatenate(
+        [
+            grad_query[:, : heads * DN].reshape(shard_w, heads, DN),
+            grad_query[:, heads * DN : heads * DN + LANES].reshape(shard_w, heads, DR // 2),
+            grad_query[:, heads * DN + LANES :].reshape(shard_w, heads, DR // 2),
+        ],
+        axis=2,
+    ).reshape(shard_w, -1)
     grad_latent = dot_tn(lat_all, one_cols).T
     grad_expand = dot_tn(lat_cols.reshape(8 * rows, -1), head_all[:, split:])
     grad_out_w = dot_tn(attn_all.reshape(8 * rows, -1), mid_cols.reshape(8 * rows, -1))

time: 390 us -> 308 us (0.79); the launches traced: 389 us -> 303 us
  Pallas kernels: 297 us -> 251 us
  other arithmetic: 32.3 us -> 10.7 us
  matrix products: 28.1 us -> 9.22 us
    pallas_call x5 -> x2, Pallas kernels: 202 us -> 152 us  [comm_kernel(): pl.pallas_call(body, out_shape=tuple((jax.ShapeDtypeStruct(shape, dtype)...]
    dot_general x17 -> x0, matrix products: 14.2 us -> none  [the longest x4 6.7 us: mdot(): return jnp.dot(left, right, preferred_element_type=F32)]
    convert_element_type x11 -> x2, other arithmetic: 10.3 us -> 2.3 us  [the longest x1 1.62 us: per_device(): x_own = own(block_input).astype(F32)]
    unnamed x132 -> x40, local copies, waits for them, and re-layouts: 13.1 us -> 19.3 us
    reduce_sum x7 -> x0, other arithmetic: 5.51 us -> none  [the longest x4 5.02 us: norm_rows(): factor = lax.rsqrt(jnp.mean(value * value, axis=-1, keepdims=True) + EPS)]
    dot_general x5, matrix products: 13.9 us -> 9.22 us  [dot_tn(): lax.dot_general(left, right, (((0,), (0,)), ((), ())), preferred_element_...]
    reshape x5 -> x4, local copies, waits for them, and re-layouts: 4.82 us -> 0.79 us  [the longest x1 0.34 us: per_device(): grad_query[:, :heads * DN].reshape(shard_w, heads, DN)]
where the time goes in v4:
time: 308 us; the launch traced here: 303 us
  Pallas kernels  251 us (81%)
  local copies, waits for them, and re-layouts  31.4 us (10%)
  other arithmetic  10.7 us (3%)
  matrix products  9.22 us (3%)
    pallas_call x2, Pallas kernels, comm_kernel(): pl.pallas_call(body, out_shape=tuple((jax.ShapeDtypeStruct(shape, dtype)...  152 us
    pallas_call x1, Pallas kernels, feed_forward(): pl.pallas_call(body, out_shape=tuple((jax.ShapeDtypeStruct(*o) for o in o...  98.6 us
    unnamed x40, local copies, waits for them, and re-layouts  19.3 us
    dot_general x5, matrix products, dot_tn(): lax.dot_general(left, right, (((0,), (0,)), ((), ())), preferred_element_...  9.22 us

profile of v4, /device:TPU:0, one launch (start us, length us, event | category | flops | bytes accessed | tf_op | source)
XLA Modules:
  0.0 302.7 jit_solution(3748851733543345288)
XLA Ops:
  0.6 1.4 copy.49
  2.1 0.1 copy.51
  2.2 0.1 copy.52
  2.4 0.0 copy-start
  2.4 0.2 copy.64
  2.6 0.9 pad_maximum_fusion.1.refs_3_
  3.6 0.2 fusion.10
  3.8 0.8 copy.54.refs_1_
  4.6 0.8 copy.55.refs_2_
  5.3 0.1 convert_element_type.35
  5.4 0.1 copy.53
  5.6 0.9 fusion.7.refs_9_
  6.4 0.1 pad.13.clone
  6.5 0.7 maximum_convert_fusion.refs_8_
  7.2 72.3 %attention.1 = (f32[32,2048]{1,0:T(8,128)}, bf16[32,2048]{1,0:T(8,128)(2,1)}, bf16[128,512]{1,0:T(8,128)(2,1)}, f32[4,128,256]{2,1,0:T(8,128)}, bf16[256,1024]{1...) custom-call(bf16[128,2048]{1,0:T(8,128)(2,1)} %refs_0_.1, ...), custom_call_target="tpu_custom_call" | custom-call | tf_op jit(solution)/shard_map/attention/pallas_call | solution.py:193
  79.5 1.5 fusion.15
  81.0 0.7 constant_dynamic-slice_fusion.2.refs_2_
  81.8 98.6 %feed_forward.1 = (f32[32,2048]{1,0:T(8,128)}, f32[1,2048]{1,0:T(1,128)}, bf16[128,2176]{1,0:T(8,128)(2,1)}, bf16[128,2048]{1,0:T(8,128)(2,1)}, f32[2,352,2048]{...) custom-call(bf16[32,2048]{1,0:T(8,128)(2,1)} %get-tuple-element.59.r, ...), custom_call_target="tpu_custom_call" | custom-call | tf_op jit(solution)/shard_map/feed_forward/pallas_call | solution.py:1280
  180.3 1.3 slice.52.refs_12_
  181.6 1.5 constant_dynamic-slice_fusion
  183.1 1.6 dynamic-slice_convert_fusion.refs_14_
  184.8 79.7 %back.1 = (bf16[128,2048]{1,0:T(8,128)(2,1)}, bf16[128,2048]{1,0:T(8,128)(2,1)}, f32[16,512]{1,0:T(8,128)}, bf16[8,128,512]{2,1,0:T(8,128)(2,1)}, bf16[8,128,128...) custom-call(bf16[128,2176]{1,0:T(8,128)(2,1)} %get-tuple-element.70., ...), custom_call_target="tpu_custom_call" | custom-call | tf_op jit(solution)/shard_map/back/pallas_call | solution.py:193
  264.4 2.0 fusion.8
  266.4 3.1 %convolution_bitcast_fusion = f32[512,512]{1,0:T(8,128)} fusion(bf16[8,128,512]{2,1,0:T(8,128)(2,1)S(1)} %copy-done.14, bf16[8,128,512]{2,1,0:T(8,128)(2,1)} %get-tuple-element.95), kind=kOutput, calls=%fused_computation.7 | convolution fusion | flops 536870912 | bytes 3145728 | tf_op jit(solution)/shard_map/dot_general | solution.py:79
  269.5 1.3 fusion
  270.8 0.0 copy-done.12
  270.8 0.5 copy-done.13
  271.3 1.8 fusion.4
  273.2 1.0 fusion.2
  274.2 1.1 copy-done.1
  275.4 0.1 slice.68
  275.5 0.3 copy.65
  275.8 1.1 fusion.13
  276.9 0.1 copy.58
  277.1 0.1 copy.59
  277.2 0.1 pad_maximum_fusion
  277.3 1.6 copy.62
  278.9 1.7 fusion.12
  280.6 1.3 bitcast_convert_fusion
  282.0 1.3 convert_bitcast_fusion
  283.3 1.3 convert_bitcast_fusion.1
  284.7 1.1 convert_element_type.38
  285.7 1.1 convert_element_type.39
  286.8 0.7 fusion.16
  287.5 0.6 dynamic_slice.26
  288.1 6.0 %copy.70 = f32[2,2048,352]{1,2,0:T(8,128)} copy(f32[2,2048,352]{1,2,0:T(8,128)} %bitcast.56) | data formatting | bytes 11534336
  294.1 6.0 %copy.71 = f32[2,2048,352]{1,2,0:T(8,128)} copy(f32[2,2048,352]{1,2,0:T(8,128)} %bitcast.55) | data formatting | bytes 11534336
  300.1 2.5 copy.72
  (39 shorter events, 0.2 us)
Async XLA Ops:
  2.4 2.9 copy-start
  3.6 1.8 copy-start.8
  4.5 1.9 copy-start.9
  4.6 1.9 copy-start.10
  4.6 1.9 copy-start.11
  184.8 79.7 %copy-start.3 = (bf16[8,128,512]{2,1,0:T(8,128)(2,1)S(1)}, bf16[8,128,512]{2,1,0:T(8,128)(2,1)}, u32[]{:S(2)}) copy-start(bf16[8,128,512]{2,1,0:T(8,128)(2,1)} %get-tuple-element.96) | copy-start | bytes 3145732
  184.8 81.7 %copy-start.14 = (bf16[8,128,512]{2,1,0:T(8,128)(2,1)S(1)}, bf16[8,128,512]{2,1,0:T(8,128)(2,1)}, u32[]{:S(2)}) copy-start(bf16[8,128,512]{2,1,0:T(8,128)(2,1)} %get-tuple-element.94) | copy-start | bytes 3145732
  266.4 3.1 %copy-start.2 = (bf16[8,128,1792]{2,1,0:T(8,128)(2,1)S(1)}, bf16[8,128,1792]{2,1,0:T(8,128)(2,1)}, u32[]{:S(2)}) copy-start(bf16[8,128,1792]{2,1,0:T(8,128)(2,1)} %get-tuple-element.91) | copy-start | bytes 11010052
  266.4 3.1 %copy-start.6 = (bf16[8,128,128]{2,1,0:T(8,128)(2,1)S(1)}, bf16[8,128,128]{2,1,0:T(8,128)(2,1)}, u32[]{:S(2)}) copy-start(bf16[8,128,128]{2,1,0:T(8,128)(2,1)} %get-tuple-element.93) | copy-start | bytes 786436
  269.5 1.3 copy-start.12
  269.5 1.8 copy-start.13
  274.2 1.1 copy-start.1
  283.3 1.3 copy-start.5
  283.3 2.4 copy-start.4
  284.7 2.2 copy-start.7
  288.1 12.0 %slice-start = ((s8[5767168]{0:T(1024)(128)(4,1)}), s8[4194304]{0:T(1024)(128)(4,1)S(1)}, s32[]{:S(2)}) async-start(s8[5767168]{0:T(1024)(128)(4,1)} %bitcast.53), calls=%async_computation | async-start | bytes 8388608
  294.1 6.0 %slice-start.1 = ((s8[5767168]{0:T(1024)(128)(4,1)}), s8[1572864]{0:T(1024)(128)(4,1)S(1)}, s32[]{:S(2)}) async-start(s8[5767168]{0:T(1024)(128)(4,1)} %bitcast.53), calls=%async_computation.1 | async-start | bytes 3145728
